TPU v7x, 128 devices: a whole 4x4x4 slice. The times are simulated.
128 devices in a mesh: data: 1, ctx: 128 (over z, y, x, core).
Axes of the slice: x: 4, y: 4, z: 4, core: 2. Of those that a mesh axis runs over, the one named last changes fastest.
Arguments:
- queries: bfloat16 [1, 32768, 5, 128], P('data', 'ctx')
- keys_in: bfloat16 [1, 32768, 1, 128], P('data', 'ctx')
- values_in: bfloat16 [1, 32768, 1, 128], P('data', 'ctx')
- grad_out: bfloat16 [1, 32768, 5, 128], P('data', 'ctx')
Outputs:
- output 1: bfloat16 [1, 32768, 5, 128], P('data', 'ctx')
- output 2: bfloat16 [1, 32768, 5, 128], P('data', 'ctx')
- output 3: bfloat16 [1, 32768, 1, 128], P('data', 'ctx')
- output 4: bfloat16 [1, 32768, 1, 128], P('data', 'ctx')
All inputs are finite; a program needn't handle non-finite values.
Results may differ from a plain program's by a relative error of at most 0.00975.
Values are sent between devices in bfloat16 or wider.
A program may use at most 1 GiB of HBM per device.

v0:
```python
import jax
import jax.numpy as jnp
from jax import lax
from jax.sharding import PartitionSpec as P

MASK_VALUE = -1e30


def solution(mesh):
    ctx_size = mesh.shape["ctx"]
    block_spec = P("data", "ctx", None, None)
    perm_next = [(dev_id, (dev_id + 1) % ctx_size) for dev_id in range(ctx_size)]

    def local_attention(queries, keys_in, values_in, grad_out):
        batch_size, shard_len, q_heads, head_dim = queries.shape
        kv_heads = keys_in.shape[2]
        group_size = q_heads // kv_heads
        half_len = shard_len // 2
        score_scale = head_dim ** -0.5
        my_index = lax.axis_index("ctx")
        q_five = queries.reshape(batch_size, shard_len, kv_heads, group_size, head_dim)
        g_five = grad_out.reshape(batch_size, shard_len, kv_heads, group_size, head_dim)
        own_mask = jnp.arange(shard_len)[:, None] >= jnp.arange(shard_len)[None, :]

        def scores_of(q_blk, k_blk, mask_tile):
            raw_scores = jnp.einsum("bqhgd,bkhd->bhgqk", q_blk, k_blk, preferred_element_type=jnp.float32) * score_scale
            if mask_tile is None:
                return raw_scores
            return jnp.where(mask_tile, raw_scores, MASK_VALUE)

        def fwd_update(run_state, q_blk, k_blk, v_blk, mask_tile):
            run_max, run_sum, acc_out = run_state
            scores = scores_of(q_blk, k_blk, mask_tile)
            new_max = jnp.maximum(run_max, jnp.max(scores, axis=-1))
            prob_tile = jnp.exp(scores - new_max[..., None])
            decay_factor = jnp.exp(run_max - new_max)
            new_sum = run_sum * decay_factor + jnp.sum(prob_tile, axis=-1)
            pv_part = jnp.einsum("bhgqk,bkhd->bhgqd", prob_tile.astype(jnp.bfloat16), v_blk, preferred_element_type=jnp.float32)
            return new_max, new_sum, acc_out * decay_factor[..., None] + pv_part

        def fwd_past(op_args):
            run_state, k_cur, v_cur = op_args
            return fwd_update(run_state, q_five, k_cur[:, :half_len], v_cur[:, :half_len], None)

        def fwd_future(op_args):
            run_state, k_cur, v_cur = op_args
            low_half = tuple(tensor[:, :, :, :half_len] for tensor in run_state)
            high_half = tuple(tensor[:, :, :, half_len:] for tensor in run_state)
            high_half = fwd_update(high_half, q_five[:, half_len:], k_cur, v_cur, None)
            return tuple(jnp.concatenate([low_part, high_part], axis=3) for low_part, high_part in zip(low_half, high_half))

        def fwd_step(step_idx, loop_carry):
            k_cur, v_cur, run_state = loop_carry
            k_cur = lax.ppermute(k_cur, "ctx", perm_next)
            v_cur = lax.ppermute(v_cur, "ctx", perm_next)
            source_id = (my_index - step_idx) % ctx_size
            run_state = lax.cond(source_id < my_index, fwd_past, fwd_future, (run_state, k_cur, v_cur))
            return k_cur, v_cur, run_state

        stat_shape = (batch_size, kv_heads, group_size, shard_len)
        run_state = (jnp.full(stat_shape, MASK_VALUE, jnp.float32), jnp.zeros(stat_shape, jnp.float32), jnp.zeros(stat_shape + (head_dim,), jnp.float32))
        run_state = fwd_update(run_state, q_five, keys_in, values_in, own_mask)
        loop_out = lax.fori_loop(1, ctx_size, fwd_step, (keys_in, values_in, run_state))
        run_max, run_sum, acc_out = loop_out[2]
        out_heads = (acc_out / run_sum[..., None]).astype(jnp.bfloat16)
        log_sum = run_max + jnp.log(run_sum)
        attn_out = jnp.transpose(out_heads, (0, 3, 1, 2, 4)).reshape(batch_size, shard_len, q_heads, head_dim)
        d_rows = jnp.einsum("bqhgd,bhgqd->bhgq", g_five, out_heads, preferred_element_type=jnp.float32)

        def bwd_block(q_blk, g_blk, lse_blk, drow_blk, k_blk, v_blk, mask_tile):
            prob_tile = jnp.exp(scores_of(q_blk, k_blk, mask_tile) - lse_blk[..., None])
            grad_v = jnp.einsum("bhgqk,bqhgd->bkhd", prob_tile.astype(jnp.bfloat16), g_blk, preferred_element_type=jnp.float32)
            dprob_tile = jnp.einsum("bqhgd,bkhd->bhgqk", g_blk, v_blk, preferred_element_type=jnp.float32)
            dscore_tile = (prob_tile * (dprob_tile - drow_blk[..., None])).astype(jnp.bfloat16)
            grad_q = jnp.einsum("bhgqk,bkhd->bqhgd", dscore_tile, k_blk, preferred_element_type=jnp.float32) * score_scale
            grad_k = jnp.einsum("bhgqk,bqhgd->bkhd", dscore_tile, q_blk, preferred_element_type=jnp.float32) * score_scale
            return grad_q, grad_k, grad_v

        def bwd_past(op_args):
            dq_acc, dk_acc, dv_acc, k_cur, v_cur = op_args
            grad_q, grad_k, grad_v = bwd_block(q_five, g_five, log_sum, d_rows, k_cur[:, :half_len], v_cur[:, :half_len], None)
            dk_acc = jnp.concatenate([dk_acc[:, :half_len] + grad_k, dk_acc[:, half_len:]], axis=1)
            dv_acc = jnp.concatenate([dv_acc[:, :half_len] + grad_v, dv_acc[:, half_len:]], axis=1)
            return dq_acc + grad_q, dk_acc, dv_acc

        def bwd_future(op_args):
            dq_acc, dk_acc, dv_acc, k_cur, v_cur = op_args
            grad_q, grad_k, grad_v = bwd_block(q_five[:, half_len:], g_five[:, half_len:], log_sum[..., half_len:], d_rows[..., half_len:], k_cur, v_cur, None)
            dq_acc = jnp.concatenate([dq_acc[:, :half_len], dq_acc[:, half_len:] + grad_q], axis=1)
            return dq_acc, dk_acc + grad_k, dv_acc + grad_v

        def bwd_step(step_idx, loop_carry):
            dq_acc, dk_acc, dv_acc, k_cur, v_cur = loop_carry
            k_cur = lax.ppermute(k_cur, "ctx", perm_next)
            v_cur = lax.ppermute(v_cur, "ctx", perm_next)
            dk_acc = lax.ppermute(dk_acc, "ctx", perm_next)
            dv_acc = lax.ppermute(dv_acc, "ctx", perm_next)
            source_id = (my_index - step_idx) % ctx_size
            dq_acc, dk_acc, dv_acc = lax.cond(source_id < my_index, bwd_past, bwd_future, (dq_acc, dk_acc, dv_acc, k_cur, v_cur))
            return dq_acc, dk_acc, dv_acc, k_cur, v_cur

        first_grads = bwd_block(q_five, g_five, log_sum, d_rows, keys_in, values_in, own_mask)
        loop_out = lax.fori_loop(1, ctx_size, bwd_step, first_grads + (keys_in, values_in))
        grad_k = lax.ppermute(loop_out[1], "ctx", perm_next)
        grad_v = lax.ppermute(loop_out[2], "ctx", perm_next)
        grad_q = loop_out[0].reshape(batch_size, shard_len, q_heads, head_dim).astype(jnp.bfloat16)
        return attn_out, grad_q, grad_k.astype(jnp.bfloat16), grad_v.astype(jnp.bfloat16)

    return jax.shard_map(local_attention, mesh=mesh, in_specs=(block_spec,) * 4, out_specs=(block_spec,) * 4, check_vma=False)
```

profile of v0, /device:TPU:0, one launch (start us, length us, event | category | flops | bytes accessed | tf_op | source)
XLA Modules:
  0.0 3427.1 jit_solution(3349777382977087245)
XLA Ops:
  4.9 1530.4 %while.46 = (s32[]{:T(128)}, bf16[1,256,1,128]{3,1,2,0:T(8,128)(2,1)S(1)}, bf16[1,256,1,128]{3,1,2,0:T(8,128)(2,1)S(1)}, f32[1,1,5,256]{3,2,1,0:T(8,128)S(1)}, f...) while((s32[]{:T(128)}, ...), condition=%wide.region_9.10_spmd, body=%wide.region_2.9_spmd.sunk | while | flops 85201296 | bytes 5746116 | solution.py:63
  1539.0 1875.9 %while.47 = (s32[]{:T(128)}, f32[1,256,1,5,128]{4,1,3,2,0:T(8,128)S(1)}, f32[1,256,1,128]{3,1,2,0:T(8,128)}, f32[1,256,1,128]{3,1,2,0:T(8,128)}, bf16[1,256,1,12...) while((s32[]{:T(128)}, ...), condition=%wide.region_13.14_spmd, body=%wide.region_10.13_spmd.sunk | while | flops 211140624 | bytes 9849492 | solution.py:103
  1539.1 11.8 collective-permute-done.2
  1583.5 11.8 collective-permute-done.2
  1598.2 11.8 collective-permute-done.2
  1627.8 11.8 collective-permute-done.2
  1642.6 11.8 collective-permute-done.2
  1686.9 11.8 collective-permute-done.2
  1731.2 11.8 collective-permute-done.2
  1775.5 11.8 collective-permute-done.2
  1819.8 11.8 collective-permute-done.2
  1864.1 11.8 collective-permute-done.2
  1878.9 11.8 collective-permute-done.2
  1908.4 11.8 collective-permute-done.2
  1923.2 11.8 collective-permute-done.2
  1967.5 11.8 collective-permute-done.2
  2011.8 11.8 collective-permute-done.2
  2056.1 11.8 collective-permute-done.2
  2100.4 11.8 collective-permute-done.2
  2144.8 11.8 collective-permute-done.2
  2159.5 11.8 collective-permute-done.2
  2189.1 11.8 collective-permute-done.2
  2203.8 11.8 collective-permute-done.2
  2248.1 11.8 collective-permute-done.2
  2292.5 11.8 collective-permute-done.2
  2336.8 11.8 collective-permute-done.2
  2381.1 11.8 collective-permute-done.2
  2425.4 11.8 collective-permute-done.2
  2440.2 11.8 collective-permute-done.2
  2469.7 11.8 collective-permute-done.2
  2484.5 11.8 collective-permute-done.2
  2528.8 11.8 collective-permute-done.2
  2573.1 11.8 collective-permute-done.2
  2617.4 11.8 collective-permute-done.2
  2661.7 11.8 collective-permute-done.2
  2706.0 11.8 collective-permute-done.2
  2720.8 11.8 collective-permute-done.2
  2750.3 11.8 collective-permute-done.2
  2765.1 11.8 collective-permute-done.2
  2809.4 11.8 collective-permute-done.2
  2853.7 11.8 collective-permute-done.2
  2898.0 11.8 collective-permute-done.2
  2942.4 11.8 collective-permute-done.2
  2986.7 11.8 collective-permute-done.2
  3001.4 11.8 collective-permute-done.2
  3031.0 11.8 collective-permute-done.2
  3045.8 11.8 collective-permute-done.2
  3090.1 11.8 collective-permute-done.2
  (4942 shorter events, 3211.9 us)
Async XLA Ops:
  1539.0 12.6 collective-permute-start.5
  1553.8 12.6 collective-permute-start.5
  1568.5 12.6 collective-permute-start.5
  1583.3 12.6 collective-permute-start.5
  1598.1 12.6 collective-permute-start.5
  1612.9 12.6 collective-permute-start.5
  1627.6 12.6 collective-permute-start.5
  1642.4 12.6 collective-permute-start.5
  1657.2 12.6 collective-permute-start.5
  1671.9 12.6 collective-permute-start.5
  1686.7 12.6 collective-permute-start.5
  1701.5 12.6 collective-permute-start.5
  1716.2 12.6 collective-permute-start.5
  1745.8 12.6 collective-permute-start.5
  1760.6 12.6 collective-permute-start.5
  1790.1 12.6 collective-permute-start.5
  1804.9 12.6 collective-permute-start.5
  1834.4 12.6 collective-permute-start.5
  1849.2 12.6 collective-permute-start.5
  1864.0 12.6 collective-permute-start.5
  1878.7 12.6 collective-permute-start.5
  1893.5 12.6 collective-permute-start.5
  1908.3 12.6 collective-permute-start.5
  1923.0 12.6 collective-permute-start.5
  1937.8 12.6 collective-permute-start.5
  1952.6 12.6 collective-permute-start.5
  1967.3 12.6 collective-permute-start.5
  1982.1 12.6 collective-permute-start.5
  1996.9 12.6 collective-permute-start.5
  2026.4 12.6 collective-permute-start.5
  2041.2 12.6 collective-permute-start.5
  2070.7 12.6 collective-permute-start.5
  2085.5 12.6 collective-permute-start.5
  2115.0 12.6 collective-permute-start.5
  2129.8 12.6 collective-permute-start.5
  2144.6 12.6 collective-permute-start.5
  2159.4 12.6 collective-permute-start.5
  2174.1 12.6 collective-permute-start.5
  2188.9 12.6 collective-permute-start.5
  2203.7 12.6 collective-permute-start.5
  2218.4 12.6 collective-permute-start.5
  2233.2 12.6 collective-permute-start.5
  2248.0 12.6 collective-permute-start.5
  2262.8 12.6 collective-permute-start.5
  2277.5 12.6 collective-permute-start.5
  2307.1 12.6 collective-permute-start.5
  2321.8 12.6 collective-permute-start.5
  2351.4 12.6 collective-permute-start.5
  (975 other events, 9855.5 us)
where the time goes:
time: 3460 us; the launch traced here: 3430 us
  waiting for transfers between devices  2820 us (82%)
  matrix products  239 us (7%)
  local copies, waits for them, and re-layouts  189 us (5%)
  other arithmetic  108 us (3%)
  starting transfers between devices  36.3 us (1%)
    ppermute x127, waiting for transfers between devices, bwd_step(): k_cur = lax.ppermute(k_cur, 'ctx', perm_next)  1490 us
    ppermute x127, waiting for transfers between devices, fwd_step(): k_cur = lax.ppermute(k_cur, 'ctx', perm_next)  1140 us
    while x1143, local copies, waits for them, and re-layouts  178 us
    ppermute x127, waiting for transfers between devices, fwd_step(): v_cur = lax.ppermute(v_cur, 'ctx', perm_next)  89.2 us
    ppermute x127, waiting for transfers between devices, bwd_step(): v_cur = lax.ppermute(v_cur, 'ctx', perm_next)  88.4 us
    concatenate x254, other arithmetic, fwd_future(): jnp.concatenate([low_part, high_part], axis=3)  82.3 us

commit v1 on v0

v1 whole, which is shorter than its diff:
```python
import functools
import math

import jax
import jax.numpy as jnp
from jax import lax
from jax.experimental import pallas as pl
from jax.experimental.pallas import tpu as pltpu
from jax.sharding import PartitionSpec as P

MESH = pl.DeviceIdType.MESH
NEG = -1e30
HD = 128
HEADS = 5
PIECE = 128
SCALE = HD ** -0.5
LOG2E = 1.4426950408889634

TREE6 = [None, 0, 1, 1, 2, 0, 2, 0, 3, 3, 1, 3, 2, 3, 2, 2, 4, 4, 4, 1, 4, 4, 2, 4, 3, 0, 1, 0, 3, 4, 3, 2, 5, 0, 5, 5, 2, 5, 1, 1, 5,
         3, 1, 0, 3, 5, 5, 1, 4, 0, 4, 5, 2, 0, 4, 2, 3, 0, 5, 5, 5, 4, 2, 3]


def popcount(value):
    return bin(value).count("1")


class Plan:
    def __init__(self, dims):
        self.dims = dims
        self.blocks = 1 << dims
        self.pairs = self.blocks // 2
        if dims == 6:
            self.link = list(TREE6)
        else:
            self.link = [None] * self.blocks
            count = [0] * dims
            for r in sorted(range(1, self.blocks), key=popcount):
                self.link[r] = min((d for d in range(dims) if (r >> d) & 1), key=lambda d: count[d])
                count[self.link[r]] += 1
        self.kids = {r: [r | (1 << d) for d in range(dims) if not (r >> d) & 1 and self.link[r | (1 << d)] == d]
                     for r in range(self.blocks)}
        self.height = {}
        for r in sorted(range(self.blocks), key=popcount, reverse=True):
            self.height[r] = max([1 + self.height[k] for k in self.kids[r]], default=0)
        for r in self.kids:
            self.kids[r].sort(key=lambda k: -self.height[k])
        self.forward()
        self.backward()

    def forward(self, block_us=2.8, hop_us=1.9, group_us=0.36):
        free = [0.0] * self.dims
        due = {}
        done = {0}

        def send(r, now):
            for k in self.kids[r]:
                d = self.link[k]
                free[d] = max(free[d], now) + block_us
                due[k] = free[d] + hop_us

        send(0, 0.0)
        now = 1.5
        steps, waits, ready = [], [], []
        while len(done) < self.blocks or ready:
            for r in sorted((r for r in due if r not in done and due[r] <= now), key=lambda r: due[r]):
                done.add(r)
                now += 0.03
                send(r, now)
                waits.append(r)
                if r ^ 1 in done:
                    ready += [r >> 1] * (3 if r == 1 else 2)
            if ready and (0 in ready or steps):
                pair = 0 if 0 in ready else ready[0]
                ready.remove(pair)
                steps.append((waits, pair))
                waits = []
                now += group_us
            else:
                now = max(now, min(due[r] for r in due if r not in done))
        self.fwd_steps = steps

    def backward(self, block_us=5.6, hop_us=2.0, group_us=0.95):
        order = [pair for _, pair in reversed(self.fwd_steps)]
        free = [0.0] * self.dims
        due = {}
        computed, sent = set(), set()
        now = 0.0
        steps, left = [], {pair: order.count(pair) for pair in order}
        sends = []
        position = 0
        while True:
            again = True
            while again:
                again = False
                able = [r for r in computed - sent if r and all(due.get(k, 1e9) <= now for k in self.kids[r])]
                for r in sorted(able, key=lambda r: (-popcount(r), r)):
                    sent.add(r)
                    now += 0.12 * len(self.kids[r]) + 0.03
                    d = self.link[r]
                    free[d] = max(free[d], now) + block_us
                    due[r] = free[d] + hop_us
                    sends.append(r)
                    again = True
            if position < len(order):
                pair = order[position]
                position += 1
                now += group_us
                left[pair] -= 1
                if not left[pair]:
                    computed |= {2 * pair, 2 * pair + 1}
                steps.append((sends, pair))
                sends = []
            elif len(sent) < self.blocks - 1:
                now = max(now, min(max(due.get(k, 1e9) for k in self.kids[r]) for r in range(1, self.blocks) if r not in sent))
            else:
                break
        self.bwd_steps = steps
        self.bwd_tail = sends


def xor(a, b):
    return a + b - 2 * a * b


def lookup(index, table):
    level = [jnp.int32(v) for v in table]
    bit = 1
    while len(level) > 1:
        odd = (index // bit) % 2 == 1
        nxt = []
        for i in range(0, len(level) - 1, 2):
            nxt.append(jnp.where(odd, level[i + 1], level[i]))
        if len(level) % 2:
            nxt.append(level[-1])
        level = nxt
        bit *= 2
    return level[0]


def branch(index, low, high, leaf):
    if high - low == 1:
        leaf(low)
        return
    mid = (low + high) // 2

    @pl.when(index < mid)
    def _():
        branch(index, low, mid, leaf)

    @pl.when(index >= mid)
    def _():
        branch(index, mid, high, leaf)


def kernel(plan, q_ref, k_ref, v_ref, g_ref, o_ref, dq_out, dk_out, dv_out,
           kv, stg, land, q_s, g_s, q_t, g_t, acc, mst, lst, xacc, xm, xl, lrow, drow, lcol, dcol, dq_s, xdq,
           ag_send, ag_recv, rs_send, rs_recv, x_send, x_recv):
    dims = plan.dims
    pieces = 4 * plan.blocks
    me = lax.axis_index("ctx")
    core = me % 2
    chip = me // 2
    bits = [(chip // (1 << d)) % 2 for d in range(dims)]
    gray = [xor(bits[d], bits[d + 1]) if d % 2 == 0 and d + 1 < dims else bits[d] for d in range(dims)]
    nbr = []
    for d in range(dims):
        other = chip + (1 - 2 * bits[d]) * (1 << d)
        if d % 2:
            other = other + (1 - 2 * bits[d - 1]) * (1 << (d - 1))
        nbr.append(2 * other + core)
    mate = me + 1 - 2 * core
    my_pair = chip // 2

    barrier = pltpu.get_barrier_semaphore()
    for dev in nbr + [mate]:
        pl.semaphore_signal(barrier, inc=1, device_id={"ctx": dev}, device_id_type=MESH)

    for h in range(2):
        rows = pl.ds(h * PIECE, PIECE)
        kv[0, 0, 0, h] = k_ref[rows, :]
        kv[0, 0, 1, h] = v_ref[rows, :].T
        for head in range(HEADS):
            c = h * 10 + head
            q_s[c] = q_ref[head, rows, :]
            g_s[c] = g_ref[head, rows, :]
    mst[...] = jnp.full(mst.shape, NEG, jnp.float32)
    lst[...] = jnp.zeros(lst.shape, jnp.float32)
    acc[...] = jnp.zeros(acc.shape, jnp.float32)
    dq_s[...] = jnp.zeros(dq_s.shape, jnp.float32)

    pl.semaphore_wait(barrier, dims + 1)

    def ag_copy(k):
        d = plan.link[k]
        r = k ^ (1 << d)
        return pltpu.make_async_remote_copy(
            src_ref=kv.at[r >> 1, r & 1], dst_ref=kv.at[k >> 1, k & 1], send_sem=ag_send.at[k], recv_sem=ag_recv.at[k],
            device_id={"ctx": nbr[d]}, device_id_type=MESH)

    def rs_copy(r):
        return pltpu.make_async_remote_copy(
            src_ref=stg.at[r >> 1, r & 1], dst_ref=land.at[r], send_sem=rs_send.at[r], recv_sem=rs_recv.at[r],
            device_id={"ctx": nbr[plan.link[r]]}, device_id_type=MESH)

    def mate_copy(src, dst, sem):
        return pltpu.make_async_remote_copy(src_ref=src, dst_ref=dst, send_sem=x_send.at[sem], recv_sem=x_recv.at[sem],
                                            device_id={"ctx": mate}, device_id_type=MESH)

    def own(ref, h):
        return ref.at[pl.ds(h * 10, 5)]

    def theirs(ref, h):
        return ref.at[pl.ds(h * 10 + 5, 5)]

    x_q = [mate_copy(own(ref, h), theirs(ref, h), 2 * j + h) for j, ref in enumerate((q_s, g_s)) for h in range(2)]
    for copy in x_q:
        copy.start()
    for k in plan.kids[0]:
        ag_copy(k).start()

    def ag_events(waits):
        for r in waits:
            ag_copy(r).wait_recv()
            for k in plan.kids[r]:
                ag_copy(k).start()

    def transposes(c):
        q_t[c] = q_s[c].T
        g_t[c] = g_s[c].T

    for h in range(2):
        pl.loop(h * 10, h * 10 + 5)(transposes)
    for copy in x_q:
        copy.wait_recv()
    for h in range(2):
        pl.loop(h * 10 + 5, h * 10 + 10)(transposes)

    def is_future(pair):
        rel = [(pair // (1 << (d - 1))) % 2 for d in range(1, dims)]
        gp = [None] + [xor(gray[d], rel[d - 1]) for d in range(1, dims)]
        other = gp[1] if dims > 1 else 0
        for d in range(2, dims):
            bit = xor(gp[d], gp[d + 1]) if d % 2 == 0 and d + 1 < dims else gp[d]
            other = other + bit * (1 << (d - 1))
        return (other - my_pair + plan.blocks) // plan.blocks

    def key_base(par, h):
        low = me if par == 0 else 2 * (chip + 1 - 2 * (chip % 2)) + core
        return (pieces - 1 - low if h else low) * PIECE

    def query_base(c):
        h, par = c // 10, (c // 5) % 2
        low = me if par == 0 else mate
        return (pieces - 1 - low if h else low) * PIECE

    def two(base0, base1, shape, axis):
        i = lax.broadcasted_iota(jnp.int32, shape, axis)
        return i + jnp.where(i < PIECE, base0, base1 - PIECE)

    coef = SCALE * LOG2E

    def key_tile(pair, h):
        return jnp.concatenate([kv[pair, 0, 0, h], kv[pair, 1, 0, h]], axis=0)

    def value_tile_t(pair, h):
        return jnp.concatenate([kv[pair, 0, 1, h], kv[pair, 1, 1, h]], axis=1)

    def wide(ref, c):
        return jnp.concatenate([ref[c], ref[c + 1]], axis=1)

    def tall(ref, c):
        return jnp.concatenate([ref[c], ref[c + 1]], axis=0)

    def fwd_group(pair, h, qg, masked):
        kt = key_tile(pair, h)
        vt = value_tile_t(pair, h)
        for t in range(HEADS):
            c = qg * 10 + 2 * t
            s = jnp.dot(kt, wide(q_t, c), preferred_element_type=jnp.float32) * coef
            if masked:
                kpos = two(key_base(0, h), key_base(1, h), s.shape, 0)
                qpos = two(query_base(c), query_base(c + 1), s.shape, 1)
                s = jnp.where(qpos >= kpos, s, NEG)
            m_old = wide(mst, c)
            m_new = jnp.maximum(m_old, jnp.max(s, axis=0, keepdims=True))
            p = jnp.exp2(s - m_new[0:1])
            decay = jnp.exp2(m_old - m_new)
            l_new = wide(lst, c) * decay + jnp.sum(p.reshape(s.shape[0] // 8, 8, s.shape[1]), axis=0)
            a_new = wide(acc, c) * decay[0:1] + jnp.dot(vt, p.astype(jnp.bfloat16), preferred_element_type=jnp.float32)
            for j in range(2):
                cols = slice(j * 128, j * 128 + 128)
                mst[c + j] = m_new[:, cols]
                lst[c + j] = l_new[:, cols]
                acc[c + j] = a_new[:, cols]

    own_groups = ((0, 0, True), (0, 1, False), (1, 1, True))
    for step, (h, qg, masked) in enumerate(own_groups):
        ag_events(plan.fwd_steps[step][0])
        fwd_group(0, h, qg, masked)

    steps = plan.fwd_steps[3:]

    if steps:
        @pl.loop(0, len(steps))
        def _(step):
            branch(step, 0, len(steps), lambda i: ag_events(steps[i][0]))
            pair = lookup(step // 2, [pair for _, pair in steps[::2]])
            fut = is_future(pair)
            g = step % 2
            fwd_group(pair, fut * g, 1 - (1 - fut) * (1 - g), False)

    x_m = []
    for h in range(2):
        inbox = pl.ds(h * 5, 5)
        x_m += [mate_copy(theirs(acc, h), xacc.at[inbox], 4 + 3 * h), mate_copy(theirs(mst, h), xm.at[inbox], 5 + 3 * h),
                mate_copy(theirs(lst, h), xl.at[inbox], 6 + 3 * h)]
    for copy in x_m:
        copy.start()
    x_r = [mate_copy(own(ref, h), theirs(ref, h), 10 + 2 * j + h) for j, ref in enumerate((lrow, drow)) for h in range(2)]

    for h in range(2):
        for copy in x_m[3 * h:3 * h + 3]:
            copy.wait_recv()
        for head in range(HEADS):
            c, x = h * 10 + head, h * 5 + head
            m1, m2 = mst[c], xm[x]
            m = jnp.maximum(m1, m2)
            w1, w2 = jnp.exp2(m1 - m), jnp.exp2(m2 - m)
            total = jnp.sum(lst[c] * w1 + xl[x] * w2, axis=0, keepdims=True)
            out = (acc[c] * w1[0:1] + xacc[x] * w2[0:1]) / total
            low = out.astype(jnp.bfloat16)
            o_ref[head, pl.ds(h * PIECE, PIECE), :] = out.T.astype(jnp.bfloat16)
            lrow[c] = m + jnp.log2(total)
            d = jnp.sum(low.astype(jnp.float32) * g_t[c].astype(jnp.float32), axis=0, keepdims=True)
            drow[c] = jnp.broadcast_to(d, (8, 128))
    for copy in x_r:
        copy.start()

    def columns(c):
        lcol[c] = jnp.broadcast_to(lrow[c, 0:1], (128, 128)).T
        dcol[c] = jnp.broadcast_to(drow[c, 0:1], (128, 128)).T

    for h in range(2):
        pl.loop(h * 10, h * 10 + 5)(columns)
    for copy in x_r:
        copy.wait_recv()
    for h in range(2):
        pl.loop(h * 10 + 5, h * 10 + 10)(columns)

    def bwd_group(pair, h, qg, masked):
        kt = key_tile(pair, h)
        vt = value_tile_t(pair, h)
        dk_sum = dv_sum = None
        for t in range(HEADS):
            c = qg * 10 + 2 * t
            s = lax.dot_general(tall(q_s, c), kt, (((1,), (1,)), ((), ())), preferred_element_type=jnp.float32) * coef
            if masked:
                qpos = two(query_base(c), query_base(c + 1), s.shape, 0)
                kpos = two(key_base(0, h), key_base(1, h), s.shape, 1)
                s = jnp.where(qpos >= kpos, s, NEG)
            lse = tall(lcol, c)
            p = jnp.exp2(s - jnp.concatenate([lse, lse], axis=1))
            dp = jnp.dot(tall(g_s, c), vt, preferred_element_type=jnp.float32)
            dr = tall(dcol, c)
            ds = (p * (dp - jnp.concatenate([dr, dr], axis=1))).astype(jnp.bfloat16)
            dv = jnp.dot(wide(g_t, c), p.astype(jnp.bfloat16), preferred_element_type=jnp.float32)
            dk = jnp.dot(wide(q_t, c), ds, preferred_element_type=jnp.float32)
            dk_sum, dv_sum = (dk, dv) if dk_sum is None else (dk_sum + dk, dv_sum + dv)
            dq = jnp.dot(ds, kt, preferred_element_type=jnp.float32)
            for j in range(2):
                dq_s[c + j] += dq[j * 128:j * 128 + 128]
        for par in range(2):
            cols = slice(par * 128, par * 128 + 128)
            stg[pair, par, 0, h] += dk_sum[:, cols]
            stg[pair, par, 1, h] += dv_sum[:, cols]

    def rs_events(sends):
        for r in sends:
            for k in plan.kids[r]:
                rs_copy(k).wait_recv()

                @pl.loop(0, 4)
                def _(j):
                    stg[r >> 1, r & 1, j // 2, j % 2] += land[k, j // 2, j % 2]
            rs_copy(r).start()

    def clear(pair):
        for par in range(2):
            for j in range(4):
                stg[pair, par, j // 2, j % 2] = jnp.zeros((128, 128), jnp.float32)

    count = len(plan.bwd_steps) - 3
    if count:
        @pl.loop(0, count)
        def _(step):
            branch(step, 0, count, lambda i: rs_events(plan.bwd_steps[i][0]))
            pair = lookup(step // 2, [pair for _, pair in plan.bwd_steps[:count:2]])
            fut = is_future(pair)
            g = step % 2

            @pl.when(g == 0)
            def _():
                clear(pair)

            bwd_group(pair, fut * g, 1 - (1 - fut) * (1 - g), False)

    clear(0)
    for step, (h, qg, masked) in enumerate(own_groups):
        rs_events(plan.bwd_steps[count + step][0])
        bwd_group(0, h, qg, masked)

    x_d = [mate_copy(theirs(dq_s, h), xdq.at[pl.ds(h * 5, 5)], 14 + h) for h in range(2)]
    for copy in x_d:
        copy.start()
    rs_events(plan.bwd_tail)
    for h in range(2):
        x_d[h].wait_recv()
        for head in range(HEADS):
            total = (dq_s[h * 10 + head] + xdq[h * 5 + head]) * SCALE
            dq_out[head, pl.ds(h * PIECE, PIECE), :] = total.astype(jnp.bfloat16)
    for k in plan.kids[0]:
        rs_copy(k).wait_recv()
    for h in range(2):
        for j, ref in enumerate((dk_out, dv_out)):
            total = stg[0, 0, j, h]
            for k in plan.kids[0]:
                total = total + land[k, j, h]
            if j == 0:
                total = total * SCALE
            ref[pl.ds(h * PIECE, PIECE), :] = total.T.astype(jnp.bfloat16)

    for k in range(1, plan.blocks):
        ag_copy(k).wait_send()
        rs_copy(k).wait_send()
    for copy in x_q + x_m + x_r + x_d:
        copy.wait_send()


def solution(mesh):
    size = mesh.shape["ctx"]
    plan = Plan(int(math.log2(size)) - 1)
    spec = P("data", "ctx", None, None)
    n = plan.blocks
    f32, bf16 = jnp.float32, jnp.bfloat16
    vm = pltpu.VMEM

    def local(queries, keys, values, grad_out):
        tokens = queries.shape[1]
        q = queries[0].transpose(1, 0, 2)
        g = grad_out[0].transpose(1, 0, 2)
        tile = (128, 128)
        big = jax.ShapeDtypeStruct((HEADS, tokens, HD), bf16)
        small = jax.ShapeDtypeStruct((tokens, HD), bf16)
        flops = 14 * 640 * PIECE * n * 2 * HD
        o, dq, dk, dv = pl.pallas_call(
            functools.partial(kernel, plan),
            out_shape=(big, big, small, small),
            in_specs=[pl.BlockSpec(memory_space=vm)] * 4,
            out_specs=(pl.BlockSpec(memory_space=vm),) * 4,
            scratch_shapes=[
                vm((n // 2, 2, 2, 2) + tile, bf16),
                vm((n // 2, 2, 2, 2) + tile, f32),
                vm((n, 2, 2) + tile, f32),
                vm((20,) + tile, bf16), vm((20,) + tile, bf16), vm((20,) + tile, bf16), vm((20,) + tile, bf16),
                vm((20,) + tile, f32), vm((20, 8, 128), f32), vm((20, 8, 128), f32),
                vm((10,) + tile, f32), vm((10, 8, 128), f32), vm((10, 8, 128), f32),
                vm((20, 8, 128), f32), vm((20, 8, 128), f32),
                vm((20,) + tile, f32), vm((20,) + tile, f32),
                vm((20,) + tile, f32), vm((10,) + tile, f32),
                pltpu.SemaphoreType.DMA((n,)), pltpu.SemaphoreType.DMA((n,)),
                pltpu.SemaphoreType.DMA((n,)), pltpu.SemaphoreType.DMA((n,)),
                pltpu.SemaphoreType.DMA((16,)), pltpu.SemaphoreType.DMA((16,)),
            ],
            compiler_params=pltpu.CompilerParams(collective_id=0, has_side_effects=True, vmem_limit_bytes=67043328),
            cost_estimate=pl.CostEstimate(flops=flops, bytes_accessed=4 << 20, transcendentals=0),
        )(q, keys[0, :, 0], values[0, :, 0], g)
        return (o.transpose(1, 0, 2)[None], dq.transpose(1, 0, 2)[None], dk[None, :, None], dv[None, :, None])

    return jax.shard_map(local, mesh=mesh, in_specs=(spec,) * 4, out_specs=(spec,) * 4, check_vma=False)
```

time: 3460 us -> 243 us (0.07)
  waiting for transfers between devices: 2820 us -> 0 us
  matrix products: 239 us -> 0 us
  Pallas kernels: 0 us -> 238 us
  local copies, waits for them, and re-layouts: 189 us -> 4.12 us
  other arithmetic: 108 us -> 0 us
  starting transfers between devices: 36.3 us -> 0 us
    ppermute x764 -> x0, waiting for transfers between devices: 2820 us -> none  [the longest x127 1490 us: bwd_step(): k_cur = lax.ppermute(k_cur, 'ctx', perm_next)]
    dot_general x895 -> x0, matrix products: 239 us -> none  [the longest x255 68.3 us: scores_of(): jnp.einsum('bqhgd,bkhd->bhgqk', q_blk, k_blk, preferred_element_type=jnp....]
    pallas_call x0 -> x1, Pallas kernels: none -> 238 us  [local(): pl.pallas_call(functools.partial(kernel, plan), out_shape=(big, big, smal...]
    while x1143 -> x0, local copies, waits for them, and re-layouts: 178 us -> none
    concatenate x381 -> x0, other arithmetic: 88 us -> none  [the longest x254 82.3 us: fwd_future(): jnp.concatenate([low_part, high_part], axis=3)]
    ppermute x764 -> x0, starting transfers between devices: 36.3 us -> none  [the longest x127 11.2 us: fwd_step(): v_cur = lax.ppermute(v_cur, 'ctx', perm_next)]
where the time goes in v1:
time: 243 us
  Pallas kernels  238 us (98%)
  local copies, waits for them, and re-layouts  4.12 us (2%)
    pallas_call x1, Pallas kernels, local(): pl.pallas_call(functools.partial(kernel, plan), out_shape=(big, big, smal...  238 us

profile of v1, /device:TPU:0, one launch (start us, length us, event | category | flops | bytes accessed | tf_op | source)
XLA Modules:
  0.0 243.2 jit_solution(4245001303490452113)
XLA Ops:
  0.6 238.4 %shard_map.75 = (bf16[5,256,128]{2,1,0:T(8,128)(2,1)}, bf16[5,256,128]{2,1,0:T(8,128)(2,1)}, bf16[256,128]{1,0:T(8,128)(2,1)}, bf16[256,128]{1,0:T(8,128)(2,1)}) custom-call(bf16[5,256,128]{2,1,0:T(8,128)(2,1)} %bitcast.20, bf16[256,128]{1,0:T(8,128)(2,1)} %bitcast.22, bf16[256,128]{1,0:T(8,128)(2,1)} %bitcast.23, bf16[5,256,128]{2,1,0:T(8,128)(2,1)} %bitcast.21), custom_call_target="tpu_custom_call" | custom-call | flops 18790481920 | bytes 4194304 | tf_op jit(solution)/shard_map/pallas_call | solution.py:455
  239.0 0.0 copy-start
  239.1 1.8 copy.12
  240.8 0.0 copy-done
  240.8 0.0 copy-start.2
  240.8 0.7 copy.13
  241.5 0.1 copy-done.2
  241.7 0.0 copy-start.1
  241.7 0.6 copy.14
  242.3 0.2 copy-done.1
  242.5 0.6 copy.15
Async XLA Ops:
  239.0 1.8 copy-start
  240.8 0.9 copy-start.2
  241.7 0.9 copy-start.1

commit v2 on v1

--- a/solution.py
+++ b/solution.py
@@ -16,8 +16,7 @@
 SCALE = HD ** -0.5
 LOG2E = 1.4426950408889634
 
-TREE6 = [None, 0, 1, 1, 2, 0, 2, 0, 3, 3, 1, 3, 2, 3, 2, 2, 4, 4, 4, 1, 4, 4, 2, 4, 3, 0, 1, 0, 3, 4, 3, 2, 5, 0, 5, 5, 2, 5, 1, 1, 5,
-         3, 1, 0, 3, 5, 5, 1, 4, 0, 4, 5, 2, 0, 4, 2, 3, 0, 5, 5, 5, 4, 2, 3]
+TREE6 = "011202033132322444144243010343250552511531035514045204230555423"
 
 
 def popcount(value):
@@ -30,7 +29,7 @@
         self.blocks = 1 << dims
         self.pairs = self.blocks // 2
         if dims == 6:
-            self.link = list(TREE6)
+            self.link = [None] + [int(d) for d in TREE6]
         else:
             self.link = [None] * self.blocks
             count = [0] * dims
@@ -142,18 +141,11 @@
         leaf(low)
         return
     mid = (low + high) // 2
-
-    @pl.when(index < mid)
-    def _():
-        branch(index, low, mid, leaf)
-
-    @pl.when(index >= mid)
-    def _():
-        branch(index, mid, high, leaf)
+    lax.cond(index < mid, lambda: branch(index, low, mid, leaf), lambda: branch(index, mid, high, leaf))
 
 
 def kernel(plan, q_ref, k_ref, v_ref, g_ref, o_ref, dq_out, dk_out, dv_out,
-           kv, stg, land, q_s, g_s, q_t, g_t, acc, mst, lst, xacc, xm, xl, lrow, drow, lcol, dcol, dq_s, xdq,
+           kv, stg, land, s_buf, t_buf, p_buf, d_buf, q_s, g_s, q_t, g_t, acc, mst, lst, dec, xacc, xm, xl, lrow, drow, lcol, dcol, dq_s, xdq,
            ag_send, ag_recv, rs_send, rs_recv, x_send, x_recv):
     dims = plan.dims
     pieces = 4 * plan.blocks
@@ -186,6 +178,9 @@
     mst[...] = jnp.full(mst.shape, NEG, jnp.float32)
     lst[...] = jnp.zeros(lst.shape, jnp.float32)
     acc[...] = jnp.zeros(acc.shape, jnp.float32)
+    dec[...] = jnp.ones(dec.shape, jnp.float32)
+    p_buf[...] = jnp.zeros(p_buf.shape, jnp.bfloat16)
+    d_buf[...] = jnp.zeros(d_buf.shape, jnp.bfloat16)
     dq_s[...] = jnp.zeros(dq_s.shape, jnp.float32)
 
     pl.semaphore_wait(barrier, dims + 1)
@@ -246,12 +241,12 @@
 
     def key_base(par, h):
         low = me if par == 0 else 2 * (chip + 1 - 2 * (chip % 2)) + core
-        return (pieces - 1 - low if h else low) * PIECE
+        return (low + h * (pieces - 1 - 2 * low)) * PIECE
 
     def query_base(c):
         h, par = c // 10, (c // 5) % 2
-        low = me if par == 0 else mate
-        return (pieces - 1 - low if h else low) * PIECE
+        low = me + par * (mate - me)
+        return (low + h * (pieces - 1 - 2 * low)) * PIECE
 
     def two(base0, base1, shape, axis):
         i = lax.broadcasted_iota(jnp.int32, shape, axis)
@@ -271,43 +266,80 @@
     def tall(ref, c):
         return jnp.concatenate([ref[c], ref[c + 1]], axis=0)
 
-    def fwd_group(pair, h, qg, masked):
+    tiles = [slice(t * 256, t * 256 + 256) for t in range(HEADS)]
+
+    def mask_scores(h, qg, keys_axis):
+        @pl.loop(0, HEADS)
+        def _(t):
+            c = qg * 10 + 2 * t
+            shape = (256, 256)
+            kpos = two(key_base(0, h), key_base(1, h), shape, keys_axis)
+            qpos = two(query_base(c), query_base(c + 1), shape, 1 - keys_axis)
+            s_buf[t] = jnp.where(qpos >= kpos, s_buf[t], NEG)
+
+    def fwd_scores(pair, h, qg):
         kt = key_tile(pair, h)
-        vt = value_tile_t(pair, h)
+        for t in range(HEADS):
+            s_buf[t] = jnp.dot(kt, wide(q_t, qg * 10 + 2 * t), preferred_element_type=jnp.float32)
+
+    def fwd_softmax(qg):
         for t in range(HEADS):
             c = qg * 10 + 2 * t
-            s = jnp.dot(kt, wide(q_t, c), preferred_element_type=jnp.float32) * coef
-            if masked:
-                kpos = two(key_base(0, h), key_base(1, h), s.shape, 0)
-                qpos = two(query_base(c), query_base(c + 1), s.shape, 1)
-                s = jnp.where(qpos >= kpos, s, NEG)
             m_old = wide(mst, c)
-            m_new = jnp.maximum(m_old, jnp.max(s, axis=0, keepdims=True))
-            p = jnp.exp2(s - m_new[0:1])
+            m_new = jnp.maximum(m_old, jnp.max(s_buf[t], axis=0, keepdims=True) * coef)
+            p = jnp.exp2(s_buf[t] * coef - m_new[0:1])
             decay = jnp.exp2(m_old - m_new)
-            l_new = wide(lst, c) * decay + jnp.sum(p.reshape(s.shape[0] // 8, 8, s.shape[1]), axis=0)
-            a_new = wide(acc, c) * decay[0:1] + jnp.dot(vt, p.astype(jnp.bfloat16), preferred_element_type=jnp.float32)
+            l_new = wide(lst, c) * decay + jnp.sum(p.reshape(32, 8, 256), axis=0)
+            p_buf[tiles[t], :] = p.astype(jnp.bfloat16)
+            dec[t] = decay
             for j in range(2):
                 cols = slice(j * 128, j * 128 + 128)
                 mst[c + j] = m_new[:, cols]
                 lst[c + j] = l_new[:, cols]
-                acc[c + j] = a_new[:, cols]
-
-    own_groups = ((0, 0, True), (0, 1, False), (1, 1, True))
-    for step, (h, qg, masked) in enumerate(own_groups):
-        ag_events(plan.fwd_steps[step][0])
-        fwd_group(0, h, qg, masked)
-
-    steps = plan.fwd_steps[3:]
-
-    if steps:
-        @pl.loop(0, len(steps))
-        def _(step):
-            branch(step, 0, len(steps), lambda i: ag_events(steps[i][0]))
-            pair = lookup(step // 2, [pair for _, pair in steps[::2]])
-            fut = is_future(pair)
-            g = step % 2
-            fwd_group(pair, fut * g, 1 - (1 - fut) * (1 - g), False)
+
+    def fwd_out(pair, h, qg):
+        vt = value_tile_t(pair, h)
+        for t in range(HEADS):
+            c = qg * 10 + 2 * t
+            pv = jnp.dot(vt, p_buf[tiles[t], :], preferred_element_type=jnp.float32)
+            for j in range(2):
+                cols = slice(j * 128, j * 128 + 128)
+                acc[c + j] = acc[c + j] * dec[t, 0:1, cols] + pv[:, cols]
+
+    steps = plan.fwd_steps
+    nsteps = len(steps)
+    fwd_pairs = [pair for _, pair in steps]
+
+    def fwd_place(j):
+        j = jnp.minimum(j, nsteps - 1)
+        pair = lookup(j, fwd_pairs)
+        fut = is_future(pair)
+        mine = 1 - jnp.minimum(j // 3, 1)
+        g = (j - 3) % 2
+        h = mine * (j // 2) + (1 - mine) * fut * g
+        qg = mine * ((j + 1) // 2) + (1 - mine) * (1 - (1 - fut) * (1 - g))
+        return pair, h, qg
+
+    ag_events(steps[0][0])
+    fwd_scores(0, 0, 0)
+    first = (me * 0,) * 3
+
+    def fwd_turn(j, carry):
+        old, cur = carry
+        branch(j, 0, nsteps, lambda i: ag_events(steps[i + 1][0]) if i + 1 < nsteps else None)
+        new = fwd_place(j + 1)
+
+        @pl.when((j == 0) | (j == 2))
+        def _():
+            mask_scores(cur[1], cur[2], 0)
+
+        fwd_out(*old)
+        fwd_softmax(cur[2])
+        fwd_scores(*new)
+        return cur, new
+
+    last = lax.fori_loop(0, nsteps, fwd_turn, (first, first))[0]
+    fwd_out(*last)
 
     x_m = []
     for h in range(2):
@@ -347,34 +379,36 @@
     for h in range(2):
         pl.loop(h * 10 + 5, h * 10 + 10)(columns)
 
-    def bwd_group(pair, h, qg, masked):
+    def bwd_scores(pair, h, qg):
         kt = key_tile(pair, h)
         vt = value_tile_t(pair, h)
-        dk_sum = dv_sum = None
         for t in range(HEADS):
             c = qg * 10 + 2 * t
-            s = lax.dot_general(tall(q_s, c), kt, (((1,), (1,)), ((), ())), preferred_element_type=jnp.float32) * coef
-            if masked:
-                qpos = two(query_base(c), query_base(c + 1), s.shape, 0)
-                kpos = two(key_base(0, h), key_base(1, h), s.shape, 1)
-                s = jnp.where(qpos >= kpos, s, NEG)
-            lse = tall(lcol, c)
-            p = jnp.exp2(s - jnp.concatenate([lse, lse], axis=1))
-            dp = jnp.dot(tall(g_s, c), vt, preferred_element_type=jnp.float32)
-            dr = tall(dcol, c)
-            ds = (p * (dp - jnp.concatenate([dr, dr], axis=1))).astype(jnp.bfloat16)
-            dv = jnp.dot(wide(g_t, c), p.astype(jnp.bfloat16), preferred_element_type=jnp.float32)
-            dk = jnp.dot(wide(q_t, c), ds, preferred_element_type=jnp.float32)
-            dk_sum, dv_sum = (dk, dv) if dk_sum is None else (dk_sum + dk, dv_sum + dv)
-            dq = jnp.dot(ds, kt, preferred_element_type=jnp.float32)
+            s_buf[t] = lax.dot_general(tall(q_s, c), kt, (((1,), (1,)), ((), ())), preferred_element_type=jnp.float32)
+            t_buf[t] = jnp.dot(tall(g_s, c), vt, preferred_element_type=jnp.float32)
+
+    def bwd_softmax(qg):
+        for t in range(HEADS):
+            c = qg * 10 + 2 * t
+            lse, dr = tall(lcol, c), tall(dcol, c)
+            p = jnp.exp2(s_buf[t] * coef - jnp.concatenate([lse, lse], axis=1))
+            p_buf[tiles[t], :] = p.astype(jnp.bfloat16)
+            d_buf[tiles[t], :] = (p * (t_buf[t] - jnp.concatenate([dr, dr], axis=1))).astype(jnp.bfloat16)
+
+    def bwd_out(pair, h, qg):
+        kt = key_tile(pair, h)
+        for ref, buf, j in ((q_t, d_buf, 0), (g_t, p_buf, 1)):
+            rows = jnp.concatenate([ref[qg * 10 + i] for i in range(10)], axis=1)
+            grad = jnp.dot(rows, buf[...], preferred_element_type=jnp.float32)
+            for par in range(2):
+                stg[pair, par, j, h] += grad[:, par * 128:par * 128 + 128]
+        for t in range(HEADS):
+            c = qg * 10 + 2 * t
+            dq = jnp.dot(d_buf[tiles[t], :], kt, preferred_element_type=jnp.float32)
             for j in range(2):
                 dq_s[c + j] += dq[j * 128:j * 128 + 128]
-        for par in range(2):
-            cols = slice(par * 128, par * 128 + 128)
-            stg[pair, par, 0, h] += dk_sum[:, cols]
-            stg[pair, par, 1, h] += dv_sum[:, cols]
-
-    def rs_events(sends):
+
+    def rs_adds(sends):
         for r in sends:
             for k in plan.kids[r]:
                 rs_copy(k).wait_recv()
@@ -382,6 +416,9 @@
                 @pl.loop(0, 4)
                 def _(j):
                     stg[r >> 1, r & 1, j // 2, j % 2] += land[k, j // 2, j % 2]
+
+    def rs_starts(sends):
+        for r in sends:
             rs_copy(r).start()
 
     def clear(pair):
@@ -389,30 +426,53 @@
             for j in range(4):
                 stg[pair, par, j // 2, j % 2] = jnp.zeros((128, 128), jnp.float32)
 
-    count = len(plan.bwd_steps) - 3
-    if count:
-        @pl.loop(0, count)
-        def _(step):
-            branch(step, 0, count, lambda i: rs_events(plan.bwd_steps[i][0]))
-            pair = lookup(step // 2, [pair for _, pair in plan.bwd_steps[:count:2]])
-            fut = is_future(pair)
-            g = step % 2
-
-            @pl.when(g == 0)
-            def _():
-                clear(pair)
-
-            bwd_group(pair, fut * g, 1 - (1 - fut) * (1 - g), False)
-
-    clear(0)
-    for step, (h, qg, masked) in enumerate(own_groups):
-        rs_events(plan.bwd_steps[count + step][0])
-        bwd_group(0, h, qg, masked)
+    bwd_pairs = [pair for _, pair in plan.bwd_steps]
+    sends_at = [sends for sends, _ in plan.bwd_steps]
+
+    def bwd_place(j):
+        j = jnp.minimum(j, nsteps - 1)
+        pair = lookup(j, bwd_pairs)
+        fut = is_future(pair)
+        i = j - (nsteps - 3)
+        mine = (j + 3) // nsteps
+        g = j % 2
+        h = mine * (i // 2) + (1 - mine) * fut * g
+        qg = mine * ((i + 1) // 2) + (1 - mine) * (1 - (1 - fut) * (1 - g))
+        return pair, h, qg
+
+    first = bwd_place(me * 0)
+    bwd_scores(*first)
+
+    def bwd_turn(j, carry):
+        old, cur = carry
+        branch(j, 0, nsteps, lambda i: rs_adds(sends_at[i - 1] if i else ()))
+        new = bwd_place(j + 1)
+
+        @pl.when((j % 2 == 1) & (j < nsteps - 1))
+        def _():
+            clear(old[0])
+
+        @pl.when((j == nsteps - 3) | (j == nsteps - 1))
+        def _():
+            mask_scores(cur[1], cur[2], 1)
+
+        branch(j, 0, nsteps, lambda i: rs_starts(sends_at[i - 1] if i else ()))
+        bwd_out(*old)
+        bwd_softmax(cur[2])
+        bwd_scores(*new)
+        return cur, new
+
+    last = lax.fori_loop(0, nsteps, bwd_turn, (first, first))[0]
+    rs_adds(sends_at[nsteps - 1])
+    rs_starts(sends_at[nsteps - 1])
+    bwd_out(*last)
 
     x_d = [mate_copy(theirs(dq_s, h), xdq.at[pl.ds(h * 5, 5)], 14 + h) for h in range(2)]
     for copy in x_d:
         copy.start()
-    rs_events(plan.bwd_tail)
+    for r in plan.bwd_tail:
+        rs_adds([r])
+        rs_starts([r])
     for h in range(2):
         x_d[h].wait_recv()
         for head in range(HEADS):
@@ -461,8 +521,9 @@
                 vm((n // 2, 2, 2, 2) + tile, bf16),
                 vm((n // 2, 2, 2, 2) + tile, f32),
                 vm((n, 2, 2) + tile, f32),
+                vm((HEADS, 256, 256), f32), vm((HEADS, 256, 256), f32), vm((HEADS * 256, 256), bf16), vm((HEADS * 256, 256), bf16),
                 vm((20,) + tile, bf16), vm((20,) + tile, bf16), vm((20,) + tile, bf16), vm((20,) + tile, bf16),
-                vm((20,) + tile, f32), vm((20, 8, 128), f32), vm((20, 8, 128), f32),
+                vm((20,) + tile, f32), vm((20, 8, 128), f32), vm((20, 8, 128), f32), vm((HEADS, 8, 256), f32),
                 vm((10,) + tile, f32), vm((10, 8, 128), f32), vm((10, 8, 128), f32),
                 vm((20, 8, 128), f32), vm((20, 8, 128), f32),
                 vm((20,) + tile, f32), vm((20,) + tile, f32),

time: 243 us -> 172 us (0.71)
  Pallas kernels: 238 us -> 167 us
    pallas_call x1, Pallas kernels: 238 us -> 167 us  [local(): pl.pallas_call(functools.partial(kernel, plan), out_shape=(big, big, smal...]
where the time goes in v2:
time: 172 us; the launch traced here: 171 us
  Pallas kernels  167 us (97%)
  local copies, waits for them, and re-layouts  4.12 us (2%)
    pallas_call x1, Pallas kernels, local(): pl.pallas_call(functools.partial(kernel, plan), out_shape=(big, big, smal...  167 us
    unnamed x10, local copies, waits for them, and re-layouts  4.12 us

profile of v2, /device:TPU:0, one launch (start us, length us, event | category | flops | bytes accessed | tf_op | source)
XLA Modules:
  0.0 171.3 jit_solution(12979832880353100172)
XLA Ops:
  0.6 166.5 %shard_map.75 = (bf16[5,256,128]{2,1,0:T(8,128)(2,1)}, bf16[5,256,128]{2,1,0:T(8,128)(2,1)}, bf16[256,128]{1,0:T(8,128)(2,1)}, bf16[256,128]{1,0:T(8,128)(2,1)}) custom-call(bf16[5,256,128]{2,1,0:T(8,128)(2,1)} %bitcast.20, bf16[256,128]{1,0:T(8,128)(2,1)} %bitcast.22, bf16[256,128]{1,0:T(8,128)(2,1)} %bitcast.23, bf16[5,256,128]{2,1,0:T(8,128)(2,1)} %bitcast.21), custom_call_target="tpu_custom_call" | custom-call | flops 18790481920 | bytes 4194304 | tf_op jit(solution)/shard_map/pallas_call | solution.py:515
  167.2 0.0 copy-start
  167.2 1.8 %copy.12 = bf16[1,256,5,128]{3,1,2,0:T(8,128)(2,1)} copy(bf16[1,256,5,128]{3,1,2,0:T(8,128)(2,1)} %bitcast.17) | data formatting | bytes 655360
  169.0 0.0 copy-done
  169.0 0.0 copy-start.2
  169.0 0.7 copy.13
  169.7 0.1 copy-done.2
  169.8 0.0 copy-start.1
  169.8 0.6 copy.14
  170.5 0.2 copy-done.1
  170.7 0.6 copy.15
Async XLA Ops:
  167.2 1.8 %copy-start = (bf16[5,256,128]{2,1,0:T(8,128)(2,1)S(1)}, bf16[5,256,128]{2,1,0:T(8,128)(2,1)}, u32[]{:S(2)}) copy-start(bf16[5,256,128]{2,1,0:T(8,128)(2,1)} %get-tuple-element.9) | copy-start | bytes 983044
  169.0 0.9 copy-start.2
  169.8 0.9 copy-start.1

commit v3 on v1

v3 whole, which is shorter than its diff:
```python
import functools
import math

import jax
import jax.numpy as jnp
from jax import lax
from jax.experimental import pallas as pl
from jax.experimental.pallas import tpu as pltpu
from jax.sharding import PartitionSpec as P

MESH = pl.DeviceIdType.MESH
NEG = -1e30
HD = 128
HEADS = 5
PIECE = 128
SCALE = HD ** -0.5
LOG2E = 1.4426950408889634

FWD_TREE = "010202133103210444120443011432155552012335020504415455253342323"
BWD_TREE = "011222230313310441022204331404450555021505035314544242153135354"
BWD_ORDER = "tvlurfanb7spjm9dqehkcoi635g1428"


def popcount(value):
    return bin(value).count("1")


class Tree:
    def __init__(self, dims, links):
        blocks = 1 << dims
        if dims == 6:
            self.link = [None] + [int(d) for d in links]
        else:
            self.link = [None] * blocks
            count = [0] * dims
            for r in sorted(range(1, blocks), key=popcount):
                self.link[r] = min((d for d in range(dims) if (r >> d) & 1), key=lambda d: count[d])
                count[self.link[r]] += 1
        self.kids = {r: [k for k in range(1, blocks) if k & ~(1 << self.link[k]) == r] for r in range(blocks)}
        height = {}
        for r in sorted(range(blocks), key=popcount, reverse=True):
            height[r] = max([1 + height[k] for k in self.kids[r]], default=0)
        for r in self.kids:
            self.kids[r].sort(key=lambda k: -height[k])


class Plan:
    def __init__(self, dims):
        self.dims = dims
        self.blocks = 1 << dims
        self.fwd = Tree(dims, FWD_TREE)
        self.bwd = Tree(dims, BWD_TREE)
        self.forward()
        self.backward()

    def forward(self, block_us=2.82, hop_us=1.9, turn_us=1.0):
        free = [0.0] * self.dims
        due = {}
        done = {0}

        def send(r, now):
            for k in self.fwd.kids[r]:
                d = self.fwd.link[k]
                free[d] = max(free[d], now) + block_us
                due[k] = free[d] + hop_us

        send(0, 0.0)
        now = 1.5
        steps, waits, ready = [], [], []
        while len(done) < self.blocks or ready:
            for r in sorted((r for r in due if r not in done and due[r] <= now), key=lambda r: due[r]):
                done.add(r)
                now += 0.03
                send(r, now)
                waits.append(r)
                if r ^ 1 in done:
                    ready += [r >> 1] * (2 if r == 1 else 1)
            if ready and (0 in ready or steps):
                pair = 0 if 0 in ready else ready[0]
                ready.remove(pair)
                steps.append((waits, pair))
                waits = []
                now += turn_us
            else:
                now = max(now, min(due[r] for r in due if r not in done))
        self.fwd_steps = steps

    def backward(self, block_us=5.64, hop_us=2.0, turn_us=1.6, add_us=0.06):
        if self.dims == 6:
            order = [int(c, 32) for c in BWD_ORDER]
        else:
            order = sorted(range(1, self.blocks // 2), key=lambda pair: -popcount(pair))
        order += [0, 0]
        tree = self.bwd
        free = [0.0] * self.dims
        due = {}
        waiting = set()
        now = turn_us
        steps, sends = [], []
        position = 0
        while True:
            able = True
            while able:
                able = [r for r in waiting if all(due.get(k, 1e9) <= now for k in tree.kids[r])]
                for r in sorted(able, key=lambda r: (-popcount(r), r)):
                    waiting.discard(r)
                    now += add_us * len(tree.kids[r]) + 0.02
                    d = tree.link[r]
                    free[d] = max(free[d], now) + block_us
                    due[r] = free[d] + hop_us
                    sends.append(r)
            if position < len(order):
                pair = order[position]
                position += 1
                now += turn_us
                if pair or position == len(order):
                    waiting |= {2 * pair, 2 * pair + 1} - {0}
                steps.append((sends, pair))
                sends = []
            elif waiting:
                now = max(now, min(max(due.get(k, 1e9) for k in tree.kids[r]) for r in waiting))
            else:
                break
        self.bwd_steps = steps
        self.bwd_tail = sends


def xor(a, b):
    return a + b - 2 * a * b


def lookup(index, table):
    level = [jnp.int32(v) for v in table]
    bit = 1
    while len(level) > 1:
        odd = (index // bit) % 2 == 1
        nxt = []
        for i in range(0, len(level) - 1, 2):
            nxt.append(jnp.where(odd, level[i + 1], level[i]))
        if len(level) % 2:
            nxt.append(level[-1])
        level = nxt
        bit *= 2
    return level[0]


def branch(index, count, leaf):
    once = index // count + 1

    def pick(low, high):
        if high - low == 1:
            acts = leaf(low)
            if acts:
                pl.loop(0, once)(lambda _: [act() for act in acts] and None)
            return
        mid = (low + high) // 2
        lax.cond(index < mid, lambda: pick(low, mid), lambda: pick(mid, high))

    pick(0, count)


def kernel(plan, q_ref, k_ref, v_ref, g_ref, o_ref, dq_out, dk_out, dv_out,
           kv, stg, land, s_buf, t_buf, p_buf, d_buf, top, q_s, g_s, q_t, g_t, acc, mst, lst, dec, xacc, xm, xl, lrow, drow, lcol, dcol, dq_s, xdq,
           ag_send, ag_recv, rs_send, rs_recv, x_send, x_recv):
    dims = plan.dims
    pieces = 4 * plan.blocks
    me = lax.axis_index("ctx")
    core = me % 2
    chip = me // 2
    bits = [(chip // (1 << d)) % 2 for d in range(dims)]
    gray = [xor(bits[d], bits[d + 1]) if d % 2 == 0 and d + 1 < dims else bits[d] for d in range(dims)]
    nbr = []
    for d in range(dims):
        other = chip + (1 - 2 * bits[d]) * (1 << d)
        if d % 2:
            other = other + (1 - 2 * bits[d - 1]) * (1 << (d - 1))
        nbr.append(2 * other + core)
    mate = me + 1 - 2 * core
    my_pair = chip // 2

    barrier = pltpu.get_barrier_semaphore()
    for dev in nbr + [mate]:
        pl.semaphore_signal(barrier, inc=1, device_id={"ctx": dev}, device_id_type=MESH)

    for h in range(2):
        rows = pl.ds(h * PIECE, PIECE)
        kv[0, 0, 0, h] = k_ref[rows, :]
        kv[0, 0, 1, h] = v_ref[rows, :].T
        for head in range(HEADS):
            c = h * 10 + head
            q_s[c] = q_ref[head, rows, :]
            g_s[c] = g_ref[head, rows, :]
    mst[...] = jnp.full(mst.shape, NEG, jnp.float32)
    lst[...] = jnp.zeros(lst.shape, jnp.float32)
    acc[...] = jnp.zeros(acc.shape, jnp.float32)
    dec[...] = jnp.ones(dec.shape, jnp.float32)
    p_buf[...] = jnp.zeros(p_buf.shape, jnp.bfloat16)
    d_buf[...] = jnp.zeros(d_buf.shape, jnp.bfloat16)

    pl.semaphore_wait(barrier, dims + 1)

    def ag_copy(k):
        d = plan.fwd.link[k]
        r = k ^ (1 << d)
        return pltpu.make_async_remote_copy(
            src_ref=kv.at[r >> 1, r & 1], dst_ref=kv.at[k >> 1, k & 1], send_sem=ag_send.at[k], recv_sem=ag_recv.at[k],
            device_id={"ctx": nbr[d]}, device_id_type=MESH)

    def rs_copy(r):
        return pltpu.make_async_remote_copy(
            src_ref=stg.at[r >> 1, r & 1], dst_ref=land.at[r], send_sem=rs_send.at[r], recv_sem=rs_recv.at[r],
            device_id={"ctx": nbr[plan.bwd.link[r]]}, device_id_type=MESH)

    def mate_copy(src, dst, sem):
        return pltpu.make_async_remote_copy(src_ref=src, dst_ref=dst, send_sem=x_send.at[sem], recv_sem=x_recv.at[sem],
                                            device_id={"ctx": mate}, device_id_type=MESH)

    def own(ref, h):
        return ref.at[pl.ds(h * 10, 5)]

    def theirs(ref, h):
        return ref.at[pl.ds(h * 10 + 5, 5)]

    x_q = [mate_copy(own(ref, h), theirs(ref, h), 2 * j + h) for j, ref in enumerate((q_s, g_s)) for h in range(2)]
    for copy in x_q:
        copy.start()
    for k in plan.fwd.kids[0]:
        ag_copy(k).start()

    def ag_events(waits):
        return [act for r in waits for act in [ag_copy(r).wait_recv] + [ag_copy(k).start for k in plan.fwd.kids[r]]]

    def transposes(c):
        q_t[c] = q_s[c].T
        g_t[c] = g_s[c].T

    for h in range(2):
        pl.loop(h * 10, h * 10 + 5)(transposes)
    for copy in x_q:
        copy.wait_recv()
    for h in range(2):
        pl.loop(h * 10 + 5, h * 10 + 10)(transposes)

    def is_future(pair):
        rel = [(pair // (1 << (d - 1))) % 2 for d in range(1, dims)]
        gp = [None] + [xor(gray[d], rel[d - 1]) for d in range(1, dims)]
        other = gp[1] if dims > 1 else 0
        for d in range(2, dims):
            bit = xor(gp[d], gp[d + 1]) if d % 2 == 0 and d + 1 < dims else gp[d]
            other = other + bit * (1 << (d - 1))
        return (other - my_pair + plan.blocks) // plan.blocks

    def key_base(par, h):
        low = me if par == 0 else 2 * (chip + 1 - 2 * (chip % 2)) + core
        return (low + h * (pieces - 1 - 2 * low)) * PIECE

    def query_base(c):
        h, par = c // 10, (c // 5) % 2
        low = me + par * (mate - me)
        return (low + h * (pieces - 1 - 2 * low)) * PIECE

    def two(base0, base1, shape, axis):
        i = lax.broadcasted_iota(jnp.int32, shape, axis)
        return i + jnp.where(i < PIECE, base0, base1 - PIECE)

    coef = SCALE * LOG2E

    def key_tile(pair, h):
        return jnp.concatenate([kv[pair, 0, 0, h], kv[pair, 1, 0, h]], axis=0)

    def value_tile_t(pair, h):
        return jnp.concatenate([kv[pair, 0, 1, h], kv[pair, 1, 1, h]], axis=1)

    def wide(ref, c):
        return jnp.concatenate([ref[c], ref[c + 1]], axis=1)

    def tall(ref, c):
        return jnp.concatenate([ref[c], ref[c + 1]], axis=0)

    def rows(slot, t):
        return pl.ds((slot * HEADS + t) * 256, 256)

    def place(pair, own_turn):
        mine = (half_pairs - pair) // half_pairs
        fut = is_future(pair)
        return (pair,) + tuple(
            part for slot in range(2)
            for part in (mine * own_turn + (1 - mine) * fut * slot, mine * slot + (1 - mine) * (fut + (1 - fut) * slot)))

    half_pairs = plan.blocks // 2

    def groups(turn):
        return tuple((slot, turn[0], turn[1 + 2 * slot], turn[2 + 2 * slot]) for slot in range(2))

    def mask_scores(turn, keys_axis):
        h = turn[1]

        @pl.loop(0, HEADS * (1 + h))
        def _(t):
            c = 2 * t
            shape = (256, 256)
            kpos = two(key_base(0, h), key_base(1, h), shape, keys_axis)
            qpos = two(query_base(c), query_base(c + 1), shape, 1 - keys_axis)
            s = jnp.where(qpos >= kpos, s_buf[t], NEG)
            s_buf[t] = s
            if keys_axis == 0:
                top[t] = jnp.max(s.reshape(32, 8, 256), axis=0)

    def fwd_scores(turn, some=range(10)):
        for slot, pair, h, qg in groups(turn):
            kt = key_tile(pair, h)
            for t in range(HEADS):
                if slot * HEADS + t not in some:
                    continue
                s = jnp.dot(kt, wide(q_t, qg * 10 + 2 * t), preferred_element_type=jnp.float32)
                s_buf[slot * HEADS + t] = s
                top[slot * HEADS + t] = jnp.max(s.reshape(32, 8, 256), axis=0)

    def fwd_softmax(turn, some):
        for slot, _, _, qg in groups(turn):
            for t in range(HEADS):
                b = slot * HEADS + t
                if b not in some:
                    continue
                c = qg * 10 + 2 * t
                m_old = wide(mst, c)
                m_new = jnp.maximum(m_old, jnp.max(top[b], axis=0, keepdims=True) * coef)
                p = jnp.exp2(s_buf[b] * coef - m_new[0:1])
                decay = jnp.exp2(m_old - m_new)
                l_new = wide(lst, c) * decay + jnp.sum(p.reshape(32, 8, 256), axis=0)
                p_buf[rows(slot, t), :] = p.astype(jnp.bfloat16)
                dec[b] = decay
                for j in range(2):
                    cols = slice(j * 128, j * 128 + 128)
                    mst[c + j] = m_new[:, cols]
                    lst[c + j] = l_new[:, cols]

    def fwd_out(turn, some=range(10)):
        for slot, pair, h, qg in groups(turn):
            vt = value_tile_t(pair, h)
            for t in range(HEADS):
                if slot * HEADS + t not in some:
                    continue
                c = qg * 10 + 2 * t
                pv = jnp.dot(vt, p_buf[rows(slot, t), :], preferred_element_type=jnp.float32)
                for j in range(2):
                    cols = slice(j * 128, j * 128 + 128)
                    acc[c + j] = acc[c + j] * dec[slot * HEADS + t, 0:1, cols] + pv[:, cols]

    turns = len(plan.fwd_steps)
    fwd_waits = [waits for waits, _ in plan.fwd_steps]
    fwd_pairs = [pair for _, pair in plan.fwd_steps]

    def fwd_place(j):
        return place(lookup(jnp.minimum(j, turns - 1), fwd_pairs), jnp.minimum(j, 1))

    for act in ag_events(fwd_waits[0]):
        act()
    first = fwd_place(me * 0)
    fwd_scores(first)

    def fwd_turn(j, carry):
        old, cur = carry
        branch(j, turns, lambda i: ag_events(fwd_waits[i + 1]) if i + 1 < turns else [])
        new = fwd_place(j + 1)

        @pl.when(j < 2)
        def _():
            mask_scores(cur, 0)

        for b in range(12):
            fwd_out(old, (b,))
            fwd_softmax(cur, (b - 1,))
            fwd_scores(new, (b - 2,))
        return cur, new

    last = lax.fori_loop(0, turns, fwd_turn, (first, first))[0]
    fwd_out(last)

    def bwd_scores(turn, some=range(10)):
        for slot, pair, h, qg in groups(turn):
            kt = key_tile(pair, h)
            vt = value_tile_t(pair, h)
            for t in range(HEADS):
                if slot * HEADS + t not in some:
                    continue
                c = qg * 10 + 2 * t
                s_buf[slot * HEADS + t] = lax.dot_general(tall(q_s, c), kt, (((1,), (1,)), ((), ())),
                                                          preferred_element_type=jnp.float32)
                t_buf[slot * HEADS + t] = jnp.dot(tall(g_s, c), vt, preferred_element_type=jnp.float32)

    def bwd_softmax(turn, some):
        for slot, _, _, qg in groups(turn):
            for t in range(HEADS):
                b = slot * HEADS + t
                if b not in some:
                    continue
                c = qg * 10 + 2 * t
                lse, dr = tall(lcol, c), tall(dcol, c)
                p = jnp.exp2(s_buf[b] * coef - jnp.concatenate([lse, lse], axis=1))
                p_buf[rows(slot, t), :] = p.astype(jnp.bfloat16)
                d_buf[rows(slot, t), :] = (p * (t_buf[b] - jnp.concatenate([dr, dr], axis=1))).astype(jnp.bfloat16)

    def bwd_out(turn, some=range(10), sums=None):
        sums = {} if sums is None else sums
        for slot, pair, h, qg in groups(turn):
            kt = key_tile(pair, h)
            for t in range(HEADS):
                if slot * HEADS + t not in some:
                    continue
                c = qg * 10 + 2 * t
                ds = d_buf[rows(slot, t), :]
                for j, (ref, buf) in enumerate(((q_t, ds), (g_t, p_buf[rows(slot, t), :]))):
                    grad = jnp.dot(wide(ref, c), buf, preferred_element_type=jnp.float32)
                    sums[j] = sums[j] + grad if t else grad
                    for par in range(2 if t == HEADS - 1 else 0):
                        stg[pair, par, j, h] += sums[j][:, par * 128:par * 128 + 128]
                dq = lax.dot_general(kt, ds, (((0,), (1,)), ((), ())), preferred_element_type=jnp.float32)
                for j in range(2):
                    dq_s[c + j] += dq[:, j * 128:j * 128 + 128]
        return sums

    bwd_pairs = [pair for _, pair in plan.bwd_steps]
    sends_at = [sends for sends, _ in plan.bwd_steps]

    def bwd_place(j):
        return place(lookup(jnp.minimum(j, turns - 1), bwd_pairs), jnp.maximum(j - (turns - 2), 0) - jnp.maximum(j - (turns - 1), 0))

    x_m = []
    for h in range(2):
        inbox = pl.ds(h * 5, 5)
        x_m += [mate_copy(theirs(acc, h), xacc.at[inbox], 4 + 3 * h), mate_copy(theirs(mst, h), xm.at[inbox], 5 + 3 * h),
                mate_copy(theirs(lst, h), xl.at[inbox], 6 + 3 * h)]
    for copy in x_m:
        copy.start()
    p_buf[...] = jnp.zeros(p_buf.shape, jnp.bfloat16)
    dq_s[...] = jnp.zeros(dq_s.shape, jnp.float32)
    first = bwd_place(me * 0)
    bwd_scores(first)
    x_r = [mate_copy(own(ref, h), theirs(ref, h), 10 + 2 * j + h) for j, ref in enumerate((lrow, drow)) for h in range(2)]

    for h in range(2):
        for copy in x_m[3 * h:3 * h + 3]:
            copy.wait_recv()
        for head in range(HEADS):
            c, x = h * 10 + head, h * 5 + head
            m1, m2 = mst[c], xm[x]
            m = jnp.maximum(m1, m2)
            w1, w2 = jnp.exp2(m1 - m), jnp.exp2(m2 - m)
            total = jnp.sum(lst[c] * w1 + xl[x] * w2, axis=0, keepdims=True)
            out = (acc[c] * w1[0:1] + xacc[x] * w2[0:1]) / total
            low = out.astype(jnp.bfloat16)
            o_ref[head, pl.ds(h * PIECE, PIECE), :] = out.T.astype(jnp.bfloat16)
            lrow[c] = m + jnp.log2(total)
            d = jnp.sum(low.astype(jnp.float32) * g_t[c].astype(jnp.float32), axis=0, keepdims=True)
            drow[c] = jnp.broadcast_to(d, (8, 128))
    for copy in x_r:
        copy.start()

    def columns(c):
        lcol[c] = jnp.broadcast_to(lrow[c, 0:1], (128, 128)).T
        dcol[c] = jnp.broadcast_to(drow[c, 0:1], (128, 128)).T

    for h in range(2):
        pl.loop(h * 10, h * 10 + 5)(columns)
    for copy in x_r:
        copy.wait_recv()
    for h in range(2):
        pl.loop(h * 10 + 5, h * 10 + 10)(columns)

    def rs_add(r, k):
        rs_copy(k).wait_recv()
        for j in range(4):
            stg[r >> 1, r & 1, j // 2, j % 2] += land[k, j // 2, j % 2]

    def rs_events(sends):
        return [functools.partial(rs_add, r, k) for r in sends for k in plan.bwd.kids[r]] + [rs_copy(r).start for r in sends]

    def clear(pair):
        for par in range(2):
            for j in range(4):
                stg[pair, par, j // 2, j % 2] = jnp.zeros((128, 128), jnp.float32)

    def bwd_turn(j, carry):
        old, cur = carry
        branch(j, turns, lambda i: rs_events(sends_at[i - 1]) if i else [])
        new = bwd_place(j + 1)

        @pl.when((j > 0) & (j < turns))
        def _():
            clear(old[0])

        @pl.when(j >= turns - 2)
        def _():
            mask_scores(cur, 1)

        sums = {}
        for b in range(12):
            sums = bwd_out(old, (b,), sums)
            bwd_softmax(cur, (b - 1,))
            bwd_scores(new, (b - 2,))
        return cur, new

    last = lax.fori_loop(0, turns, bwd_turn, (first, first))[0]
    for act in rs_events(sends_at[turns - 1]):
        act()
    bwd_out(last)

    x_d = [mate_copy(theirs(dq_s, h), xdq.at[pl.ds(h * 5, 5)], 14 + h) for h in range(2)]
    for copy in x_d:
        copy.start()
    for r in plan.bwd_tail:
        for act in rs_events([r]):
            act()
    for h in range(2):
        x_d[h].wait_recv()
        for head in range(HEADS):
            total = (dq_s[h * 10 + head] + xdq[h * 5 + head]) * SCALE
            dq_out[head, pl.ds(h * PIECE, PIECE), :] = total.T.astype(jnp.bfloat16)
    for k in plan.bwd.kids[0]:
        rs_copy(k).wait_recv()
    for h in range(2):
        for j, ref in enumerate((dk_out, dv_out)):
            total = stg[0, 0, j, h]
            for k in plan.bwd.kids[0]:
                total = total + land[k, j, h]
            if j == 0:
                total = total * SCALE
            ref[pl.ds(h * PIECE, PIECE), :] = total.T.astype(jnp.bfloat16)

    for k in range(1, plan.blocks):
        ag_copy(k).wait_send()
        rs_copy(k).wait_send()
    for copy in x_q + x_m + x_r + x_d:
        copy.wait_send()


def solution(mesh):
    size = mesh.shape["ctx"]
    plan = Plan(int(math.log2(size)) - 1)
    spec = P("data", "ctx", None, None)
    n = plan.blocks
    f32, bf16 = jnp.float32, jnp.bfloat16
    vm = pltpu.VMEM

    def local(queries, keys, values, grad_out):
        tokens = queries.shape[1]
        q = queries[0].transpose(1, 0, 2)
        g = grad_out[0].transpose(1, 0, 2)
        tile = (128, 128)
        big = jax.ShapeDtypeStruct((HEADS, tokens, HD), bf16)
        small = jax.ShapeDtypeStruct((tokens, HD), bf16)
        flops = 14 * 640 * PIECE * n * 2 * HD
        o, dq, dk, dv = pl.pallas_call(
            functools.partial(kernel, plan),
            out_shape=(big, big, small, small),
            in_specs=[pl.BlockSpec(memory_space=vm)] * 4,
            out_specs=(pl.BlockSpec(memory_space=vm),) * 4,
            scratch_shapes=[
                vm((n // 2, 2, 2, 2) + tile, bf16),
                vm((n // 2, 2, 2, 2) + tile, f32),
                vm((n, 2, 2) + tile, f32),
                vm((10, 256, 256), f32), vm((10, 256, 256), f32), vm((2560, 256), bf16), vm((2560, 256), bf16), vm((10, 8, 256), f32),
                vm((20,) + tile, bf16), vm((20,) + tile, bf16), vm((20,) + tile, bf16), vm((20,) + tile, bf16),
                vm((20,) + tile, f32), vm((20, 8, 128), f32), vm((20, 8, 128), f32), vm((10, 8, 256), f32),
                vm((10,) + tile, f32), vm((10, 8, 128), f32), vm((10, 8, 128), f32),
                vm((20, 8, 128), f32), vm((20, 8, 128), f32),
                vm((20,) + tile, f32), vm((20,) + tile, f32),
                vm((20,) + tile, f32), vm((10,) + tile, f32),
                pltpu.SemaphoreType.DMA((n,)), pltpu.SemaphoreType.DMA((n,)),
                pltpu.SemaphoreType.DMA((n,)), pltpu.SemaphoreType.DMA((n,)),
                pltpu.SemaphoreType.DMA((16,)), pltpu.SemaphoreType.DMA((16,)),
            ],
            compiler_params=pltpu.CompilerParams(collective_id=0, has_side_effects=True, vmem_limit_bytes=67043328),
            cost_estimate=pl.CostEstimate(flops=flops, bytes_accessed=4 << 20, transcendentals=0),
        )(q, keys[0, :, 0], values[0, :, 0], g)
        return (o.transpose(1, 0, 2)[None], dq.transpose(1, 0, 2)[None], dk[None, :, None], dv[None, :, None])

    return jax.shard_map(local, mesh=mesh, in_specs=(spec,) * 4, out_specs=(spec,) * 4, check_vma=False)
```

time: 243 us -> 137 us (0.56)
  Pallas kernels: 238 us -> 132 us
    pallas_call x1, Pallas kernels: 238 us -> 132 us  [local(): pl.pallas_call(functools.partial(kernel, plan), out_shape=(big, big, smal...]
where the time goes in v3:
time: 137 us
  Pallas kernels  132 us (96%)
  local copies, waits for them, and re-layouts  4.12 us (3%)
    pallas_call x1, Pallas kernels, local(): pl.pallas_call(functools.partial(kernel, plan), out_shape=(big, big, smal...  132 us
    unnamed x10, local copies, waits for them, and re-layouts  4.12 us

profile of v3, /device:TPU:0, one launch (start us, length us, event | category | flops | bytes accessed | tf_op | source)
XLA Modules:
  0.0 136.5 jit_solution(7955017620450133492)
XLA Ops:
  0.6 131.8 %shard_map.75 = (bf16[5,256,128]{2,1,0:T(8,128)(2,1)}, bf16[5,256,128]{2,1,0:T(8,128)(2,1)}, bf16[256,128]{1,0:T(8,128)(2,1)}, bf16[256,128]{1,0:T(8,128)(2,1)}) custom-call(bf16[5,256,128]{2,1,0:T(8,128)(2,1)} %bitcast.20, bf16[256,128]{1,0:T(8,128)(2,1)} %bitcast.22, bf16[256,128]{1,0:T(8,128)(2,1)} %bitcast.23, bf16[5,256,128]{2,1,0:T(8,128)(2,1)} %bitcast.21), custom_call_target="tpu_custom_call" | custom-call | flops 18790481920 | bytes 4194304 | tf_op jit(solution)/shard_map/pallas_call | solution.py:554
  132.4 0.0 copy-start
  132.4 1.8 %copy.12 = bf16[1,256,5,128]{3,1,2,0:T(8,128)(2,1)} copy(bf16[1,256,5,128]{3,1,2,0:T(8,128)(2,1)} %bitcast.17) | data formatting | bytes 655360
  134.2 0.0 copy-done
  134.2 0.0 copy-start.2
  134.2 0.7 copy.13
  134.9 0.1 copy-done.2
  135.0 0.0 copy-start.1
  135.0 0.6 copy.14
  135.7 0.2 copy-done.1
  135.9 0.6 copy.15
Async XLA Ops:
  132.4 1.8 %copy-start = (bf16[5,256,128]{2,1,0:T(8,128)(2,1)S(1)}, bf16[5,256,128]{2,1,0:T(8,128)(2,1)}, u32[]{:S(2)}) copy-start(bf16[5,256,128]{2,1,0:T(8,128)(2,1)} %get-tuple-element.9) | copy-start | bytes 983044
  134.2 0.9 copy-start.2
  135.0 0.9 copy-start.1

commit v4 on v3

v4 whole, which is shorter than its diff:
```python
import functools
import math

import jax
import jax.numpy as jnp
from jax import lax
from jax.experimental import pallas as pl
from jax.experimental.pallas import tpu as pltpu
from jax.sharding import PartitionSpec as P

MESH = pl.DeviceIdType.MESH
NEG = -1e30
HD = 128
HEADS = 5
PIECE = 128
SCALE = HD ** -0.5
LOG2E = 1.4426950408889634
TILES = 2 * HEADS

KEY_TREE = "011221033303230444022204041233350552225555023554414241430104552"
VALUE_TREE = "010201133132030404124203411303055112015353553124445242153504414"
DK_TREE = "011201030113022404042143013424255155512503350504044245135103424"
DV_TREE = "011222133313022444124423431243055505220331030555415254133515214"
BWD_ORDER = "vlruetqkfpndmjbs7h9c56i34o8ag21"


def popcount(value):
    return bin(value).count("1")


class Tree:
    def __init__(self, dims, links):
        blocks = 1 << dims
        if dims == 6:
            self.link = [None] + [int(d) for d in links]
        else:
            self.link = [None] * blocks
            count = [0] * dims
            for r in sorted(range(1, blocks), key=popcount):
                self.link[r] = min((d for d in range(dims) if (r >> d) & 1), key=lambda d: count[d])
                count[self.link[r]] += 1
        self.kids = {r: [k for k in range(1, blocks) if k & ~(1 << self.link[k]) == r] for r in range(blocks)}
        height = {}
        for r in sorted(range(blocks), key=popcount, reverse=True):
            height[r] = max([1 + height[k] for k in self.kids[r]], default=0)
        for r in self.kids:
            self.kids[r].sort(key=lambda k: -height[k])


class Plan:
    def __init__(self, dims):
        self.dims = dims
        self.blocks = 1 << dims
        self.turns = self.blocks // 2 + 1
        self.fwd = [Tree(dims, KEY_TREE), Tree(dims, VALUE_TREE)]
        self.bwd = [Tree(dims, DK_TREE), Tree(dims, DV_TREE)]
        self.forward()
        self.backward()

    def forward(self, unit_us=1.41, hop_us=1.9, turn_us=0.85):
        free = [0.0] * self.dims
        due = {}
        done = {(0, 0), (0, 1)}
        now = 1.0
        steps, waits, ready, order = [], [], [0], []

        def send(r, x):
            for k in self.fwd[x].kids[r]:
                d = self.fwd[x].link[k]
                free[d] = max(free[d], now) + unit_us
                due[k, x] = free[d] + hop_us

        now = 0.0
        send(0, 0)
        send(0, 1)
        now = 1.0
        while True:
            for unit in sorted((u for u in due if u not in done and due[u] <= now), key=lambda u: (due[u], u)):
                done.add(unit)
                now += 0.02
                send(*unit)
                waits.append(unit)
                if unit[1] == 0 and (unit[0] ^ 1, 0) in done:
                    ready.append(unit[0] >> 1)
            turn = len(steps)
            late = order[max(turn - 2, 0):turn - 1] if turn < self.turns else order[turn - 2:]
            lacking = [r for pair in late for r in (2 * pair, 2 * pair + 1) if (r, 1) not in done]
            if turn == 2 < self.turns:
                lacking = []
            if lacking or not (ready or turn == self.turns):
                now = max(now, min(due[u] for u in due if u not in done))
                continue
            if turn == self.turns:
                break
            order.append(ready.pop(0))
            steps.append(waits)
            waits = []
            now += turn_us if turn else 0.0
        self.fwd_waits = steps + [waits]
        self.fwd_pairs = order
        self.fwd_mate = max(i for i, pair in enumerate(order) if pair == 0)

    def backward(self, unit_us=2.82, hop_us=2.0, turn_us=1.6, add_us=0.03):
        if self.dims == 6:
            order = [int(c, 32) for c in BWD_ORDER]
        else:
            order = sorted(range(1, self.blocks // 2), key=lambda pair: -popcount(pair))
        order += [0, 0]
        free = [0.0] * self.dims
        due = {}
        waiting = set()
        now = turn_us
        steps, sends = [], []
        position = 0

        def kids(unit):
            return [(k, unit[1]) for k in self.bwd[unit[1]].kids[unit[0]]]

        while True:
            able = True
            while able:
                able = [u for u in waiting if all(due.get(k, 1e9) <= now for k in kids(u))]
                for unit in sorted(able, key=lambda u: (-popcount(u[0]), u)):
                    waiting.discard(unit)
                    now += add_us * len(kids(unit)) + 0.01
                    d = self.bwd[unit[1]].link[unit[0]]
                    free[d] = max(free[d], now) + unit_us
                    due[unit] = free[d] + hop_us
                    sends.append(unit)
            if position < len(order):
                pair = order[position]
                position += 1
                now += turn_us
                if pair:
                    waiting |= {(2 * pair + i, x) for i in range(2) for x in range(2)}
                elif position < len(order):
                    waiting |= {(1, 0), (1, 1)}
                steps.append(sends)
                sends = []
            elif waiting:
                now = max(now, min(max(due.get(k, 1e9) for k in kids(u)) for u in waiting))
            else:
                break
        self.bwd_sends = steps + [sends]
        self.bwd_pairs = order
        self.bwd_last = sorted((u for x in range(2) for u in kids((0, x))), key=lambda u: due[u])


def xor(a, b):
    return a + b - 2 * a * b


def lookup(index, table):
    level = [jnp.int32(v) for v in table]
    bit = 1
    while len(level) > 1:
        odd = (index // bit) % 2 == 1
        nxt = [jnp.where(odd, level[i + 1], level[i]) for i in range(0, len(level) - 1, 2)]
        level = nxt + level[2 * len(nxt):]
        bit *= 2
    return level[0]


def branch(index, count, leaf):
    once = index // count + 1

    def pick(low, high):
        if high - low == 1:
            acts = leaf(low)
            if acts:
                pl.loop(0, once)(lambda _: [act() for act in acts] and None)
            return
        mid = (low + high) // 2
        lax.cond(index < mid, lambda: pick(low, mid), lambda: pick(mid, high))

    pick(0, count)


def kernel(plan, q_ref, k_ref, v_ref, g_ref, o_ref, dq_ref, dk_ref, dv_ref,
           kv, stg, land, s_buf, t_buf, p_buf, d_buf, top, q_s, g_s, v_s, q_t, g_t, c_t, acc, mst, lst, dec,
           xacc, xm, xl, lrow, drow, lcol, dcol, dq_s, xdq, o_s, dq_o, dk_o, dv_o,
           ag_send, ag_recv, rs_send, rs_recv, x_send, x_recv, io):
    dims, turns = plan.dims, plan.turns
    pieces = 4 * plan.blocks
    f32, bf16 = jnp.float32, jnp.bfloat16
    me = lax.axis_index("ctx")
    core = me % 2
    chip = me // 2
    bits = [(chip // (1 << d)) % 2 for d in range(dims)]
    gray = [xor(bits[d], bits[d + 1]) if d % 2 == 0 and d + 1 < dims else bits[d] for d in range(dims)]
    nbr = []
    for d in range(dims):
        other = chip + (1 - 2 * bits[d]) * (1 << d)
        if d % 2:
            other = other + (1 - 2 * bits[d - 1]) * (1 << (d - 1))
        nbr.append(2 * other + core)
    mate = me + 1 - 2 * core
    my_pair = chip // 2

    barrier = pltpu.get_barrier_semaphore()
    for dev in nbr + [mate]:
        pl.semaphore_signal(barrier, inc=1, device_id={"ctx": dev}, device_id_type=MESH)

    def half(h):
        return pl.ds(h * PIECE, PIECE)

    loads = []
    for h in range(2):
        loads += [pltpu.make_async_copy(v_ref.at[half(h)], v_s.at[h], io.at[h]),
                  pltpu.make_async_copy(k_ref.at[half(h)], kv.at[0, 0, 0, h], io.at[2 + h])]
    for h in range(2):
        for j, (src, dst) in enumerate(((q_ref, q_s), (g_ref, g_s))):
            loads.append(pltpu.make_async_copy(src.at[:, half(h)], dst.at[pl.ds(h * TILES, HEADS)], io.at[4 + 2 * j + h]))
    for copy in loads:
        copy.start()
    mst[...] = jnp.full(mst.shape, NEG, f32)
    lst[...] = jnp.zeros(lst.shape, f32)
    acc[...] = jnp.zeros(acc.shape, f32)
    dec[...] = jnp.ones(dec.shape, f32)
    p_buf[...] = jnp.zeros(p_buf.shape, bf16)
    for copy in loads[:4]:
        copy.wait()
    for h in range(2):
        kv[0, 0, 1, h] = v_s[h].T

    pl.semaphore_wait(barrier, dims + 1)

    def ag_copy(k, x):
        d = plan.fwd[x].link[k]
        r = k ^ (1 << d)
        return pltpu.make_async_remote_copy(
            src_ref=kv.at[r >> 1, r & 1, x], dst_ref=kv.at[k >> 1, k & 1, x], send_sem=ag_send.at[k, x],
            recv_sem=ag_recv.at[k, x], device_id={"ctx": nbr[d]}, device_id_type=MESH)

    def rs_copy(r, x):
        return pltpu.make_async_remote_copy(
            src_ref=stg.at[r >> 1, r & 1, x], dst_ref=land.at[r, x], send_sem=rs_send.at[r, x], recv_sem=rs_recv.at[r, x],
            device_id={"ctx": nbr[plan.bwd[x].link[r]]}, device_id_type=MESH)

    def mate_copy(src, dst, sem):
        return pltpu.make_async_remote_copy(src_ref=src, dst_ref=dst, send_sem=x_send.at[sem], recv_sem=x_recv.at[sem],
                                            device_id={"ctx": mate}, device_id_type=MESH)

    def own(ref, h):
        return ref.at[pl.ds(h * TILES, HEADS)]

    def theirs(ref, h):
        return ref.at[pl.ds(h * TILES + HEADS, HEADS)]

    for x in range(2):
        for k in plan.fwd[x].kids[0]:
            ag_copy(k, x).start()
    for copy in loads[4:]:
        copy.wait()
    x_q = [mate_copy(own(ref, h), theirs(ref, h), 2 * j + h) for j, ref in enumerate((q_s, g_s)) for h in range(2)]
    for copy in x_q:
        copy.start()

    def ag_events(waits):
        return [act for r, x in waits for act in [ag_copy(r, x).wait_recv] + [ag_copy(k, x).start for k in plan.fwd[x].kids[r]]]

    coef = SCALE * LOG2E

    def transposes(c):
        turned = q_s[c].T
        q_t[c] = turned
        g_t[c] = g_s[c].T
        scaled = turned.astype(f32) * coef
        high = scaled.astype(bf16)
        c_t[c, 0] = high
        c_t[c, 1] = (scaled - high.astype(f32)).astype(bf16)

    for h in range(2):
        pl.loop(h * TILES, h * TILES + HEADS)(transposes)
    for copy in x_q:
        copy.wait_recv()
    for h in range(2):
        pl.loop(h * TILES + HEADS, h * TILES + TILES)(transposes)

    def is_future(pair):
        rel = [(pair // (1 << (d - 1))) % 2 for d in range(1, dims)]
        gp = [None] + [xor(gray[d], rel[d - 1]) for d in range(1, dims)]
        other = gp[1] if dims > 1 else 0
        for d in range(2, dims):
            bit = xor(gp[d], gp[d + 1]) if d % 2 == 0 and d + 1 < dims else gp[d]
            other = other + bit * (1 << (d - 1))
        return (other - my_pair + plan.blocks) // plan.blocks

    def place(pair, a):
        mine = (plan.blocks // 2 - pair) // (plan.blocks // 2)
        fut = is_future(pair)
        turn = (pair,)
        for slot in range(2):
            h = (1 - mine) * fut * slot
            turn += (mine * a, h, mine * a + 1 - mine, mine + h, mine * slot + (1 - mine) * (fut + (1 - fut) * slot))
        return turn

    def groups(turn):
        for slot in range(2):
            p0, h0, p1, h1, qg = turn[1 + 5 * slot:6 + 5 * slot]
            yield slot, ((turn[0], p0, h0), (turn[0], p1, h1)), qg * TILES

    def key_tile(where):
        return jnp.concatenate([kv[pair, par, 0, h] for pair, par, h in where], axis=0)

    def value_tile_t(where):
        return jnp.concatenate([kv[pair, par, 1, h] for pair, par, h in where], axis=1)

    def wide(ref, c):
        return jnp.concatenate([ref[c], ref[c + 1]], axis=1)

    def tall(ref, c):
        return jnp.concatenate([ref[c], ref[c + 1]], axis=0)

    def rows(b):
        return pl.ds(b * 256, 256)

    def mask_scores(a, keys_axis):
        key_low = me + a * (2 * (1 - 2 * (chip % 2)))

        def two(base0, base1, axis):
            i = lax.broadcasted_iota(jnp.int32, (256, 256), axis)
            return i + jnp.where(i < PIECE, base0, base1 - PIECE)

        def query_base(c):
            h, par = c // TILES, (c // HEADS) % 2
            low = me + par * (mate - me)
            return (low + h * (pieces - 1 - 2 * low)) * PIECE

        @pl.loop(0, TILES)
        def _(b):
            kpos = two(key_low * PIECE, (pieces - 1 - key_low) * PIECE, keys_axis)
            qpos = two(query_base(2 * b), query_base(2 * b + 1), 1 - keys_axis)
            s = jnp.where(qpos >= kpos, s_buf[b], NEG)
            s_buf[b] = s
            if keys_axis == 0:
                top[b] = jnp.max(s.reshape(32, 8, 256), axis=0)

    def fwd_scores(turn, some=range(TILES)):
        for slot, where, base in groups(turn):
            kt = key_tile(where)
            twice = jnp.concatenate([kt, kt], axis=1)
            for t in range(HEADS):
                b, c = slot * HEADS + t, base + 2 * t
                if b in some:
                    scaled = jnp.concatenate([wide(c_t.at[:, i], c) for i in range(2)], axis=0)
                    s = jnp.dot(twice, scaled, preferred_element_type=f32)
                    s_buf[b] = s
                    top[b] = jnp.max(s.reshape(32, 8, 256), axis=0)

    def fwd_softmax(turn, some):
        for slot, _, base in groups(turn):
            for t in range(HEADS):
                b, c = slot * HEADS + t, base + 2 * t
                if b not in some:
                    continue
                m_old = wide(mst, c)
                m_new = jnp.maximum(m_old, jnp.max(top[b], axis=0, keepdims=True))
                p = jnp.exp2(s_buf[b] - m_new[0:1])
                decay = jnp.exp2(m_old - m_new)
                l_new = wide(lst, c) * decay + jnp.sum(p.reshape(32, 8, 256), axis=0)
                p_buf[rows(b), :] = p.astype(bf16)
                dec[b] = decay
                for j in range(2):
                    cols = slice(j * 128, j * 128 + 128)
                    mst[c + j] = m_new[:, cols]
                    lst[c + j] = l_new[:, cols]

    def fwd_out(turn, some=range(TILES)):
        for slot, where, base in groups(turn):
            vt = value_tile_t(where)
            for t in range(HEADS):
                b, c = slot * HEADS + t, base + 2 * t
                if b in some:
                    pv = jnp.dot(vt, p_buf[rows(b), :], preferred_element_type=f32)
                    for j in range(2):
                        cols = slice(j * 128, j * 128 + 128)
                        acc[c + j] = acc[c + j] * dec[b, 0:1, cols] + pv[:, cols]

    def fwd_place(j):
        return place(lookup(jnp.minimum(j, turns - 1), plan.fwd_pairs), jnp.minimum(j, 1))

    for act in ag_events(plan.fwd_waits[0]):
        act()
    first = fwd_place(me * 0)
    fwd_scores(first)

    def fwd_turn(j, carry):
        old, cur = carry
        branch(j, turns, lambda i: ag_events(plan.fwd_waits[i + 1]))
        new = fwd_place(j + 1)

        @pl.when((j == 0) | (j == plan.fwd_mate))
        def _():
            mask_scores(jnp.minimum(j, 1), 0)

        for b in range(TILES + 2):
            fwd_scores(new, (b - 2,))
            fwd_softmax(cur, (b - 1,))
            fwd_out(old, (b,))
        return cur, new

    last = lax.fori_loop(0, turns, fwd_turn, (first, first))[0]
    fwd_out(last)

    def bwd_scores(turn, some=range(TILES)):
        for slot, where, base in groups(turn):
            kt, vt = key_tile(where), value_tile_t(where)
            for t in range(HEADS):
                b, c = slot * HEADS + t, base + 2 * t
                if b in some:
                    s_buf[b] = lax.dot_general(tall(q_s, c), kt, (((1,), (1,)), ((), ())), preferred_element_type=f32)
                    t_buf[b] = jnp.dot(tall(g_s, c), vt, preferred_element_type=f32)

    def bwd_softmax(turn, some):
        for slot, _, base in groups(turn):
            for t in range(HEADS):
                b, c = slot * HEADS + t, base + 2 * t
                if b in some:
                    lse, dr = tall(lcol, c), tall(dcol, c)
                    p = jnp.exp2(s_buf[b] * coef - jnp.concatenate([lse, lse], axis=1))
                    p_buf[rows(b), :] = p.astype(bf16)
                    d_buf[rows(b), :] = (p * (t_buf[b] - jnp.concatenate([dr, dr], axis=1))).astype(bf16)

    def bwd_out(turn, sums, some=range(TILES)):
        for slot, where, base in groups(turn):
            kt = key_tile(where)
            for t in range(HEADS):
                b, c = slot * HEADS + t, base + 2 * t
                if b not in some:
                    continue
                ds = d_buf[rows(b), :]
                for x, (ref, buf) in enumerate(((q_t, ds), (g_t, p_buf[rows(b), :]))):
                    grad = jnp.dot(wide(ref, c), buf, preferred_element_type=f32)
                    sums[x] = sums[x] + grad if t else grad
                    for j, (pair, par, h) in enumerate(where if t == HEADS - 1 else ()):
                        stg[pair, par, x, h] += sums[x][:, j * 128:j * 128 + 128]
                dq = lax.dot_general(kt, ds, (((0,), (1,)), ((), ())), preferred_element_type=f32)
                for j in range(2):
                    dq_s[c + j] += dq[:, j * 128:j * 128 + 128]

    def bwd_place(j):
        at = jnp.minimum(j, turns - 1)
        return place(lookup(at, plan.bwd_pairs), 1 - (at + 1) // turns)

    x_m = []
    for h in range(2):
        inbox = pl.ds(h * HEADS, HEADS)
        x_m += [mate_copy(theirs(ref, h), box.at[inbox], 4 + 3 * h + i)
                for i, (ref, box) in enumerate(((acc, xacc), (mst, xm), (lst, xl)))]
    for copy in x_m:
        copy.start()
    first = bwd_place(me * 0)
    bwd_scores(first)
    p_buf[...] = jnp.zeros(p_buf.shape, bf16)
    d_buf[...] = jnp.zeros(d_buf.shape, bf16)
    dq_s[...] = jnp.zeros(dq_s.shape, f32)
    x_r = [mate_copy(own(ref, h), theirs(ref, h), 10 + 2 * j + h) for j, ref in enumerate((lrow, drow)) for h in range(2)]

    for h in range(2):
        for copy in x_m[3 * h:3 * h + 3]:
            copy.wait_recv()
        for head in range(HEADS):
            c, i = h * TILES + head, h * HEADS + head
            m1, m2 = mst[c], xm[i]
            m = jnp.maximum(m1, m2)
            w1, w2 = jnp.exp2(m1 - m), jnp.exp2(m2 - m)
            total = jnp.sum(lst[c] * w1 + xl[i] * w2, axis=0, keepdims=True)
            out = (acc[c] * w1[0:1] + xacc[i] * w2[0:1]) / total
            o_s[head, half(h), :] = out.T.astype(bf16)
            lrow[c] = m + jnp.log2(total)
            rounded = out.astype(bf16).astype(f32)
            drow[c] = jnp.broadcast_to(jnp.sum(rounded * g_t[c].astype(f32), axis=0, keepdims=True), (8, 128))
    for copy in x_r:
        copy.start()
    stores = [pltpu.make_async_copy(o_s, o_ref, io.at[8])]
    stores[0].start()

    def columns(c):
        lcol[c] = jnp.broadcast_to(lrow[c, 0:1], (128, 128)).T
        dcol[c] = jnp.broadcast_to(drow[c, 0:1], (128, 128)).T

    for h in range(2):
        pl.loop(h * TILES, h * TILES + HEADS)(columns)
    for copy in x_r:
        copy.wait_recv()
    for h in range(2):
        pl.loop(h * TILES + HEADS, h * TILES + TILES)(columns)

    def rs_add(r, k, x):
        rs_copy(k, x).wait_recv()
        for h in range(2):
            stg[r >> 1, r & 1, x, h] += land[k, x, h]

    def rs_events(sends):
        return ([functools.partial(rs_add, r, k, x) for r, x in sends for k in plan.bwd[x].kids[r]]
                + [rs_copy(r, x).start for r, x in sends])

    def clear(pair):
        for i in range(8):
            stg[pair, i // 4, i // 2 % 2, i % 2] = jnp.zeros((128, 128), f32)

    def bwd_turn(j, carry):
        old, cur = carry
        branch(j, turns, lambda i: rs_events(plan.bwd_sends[i - 1]) if i else [])
        new = bwd_place(j + 1)

        @pl.when((j > 0) & (j < turns))
        def _():
            clear(old[0])

        @pl.when(j >= turns - 2)
        def _():
            mask_scores(turns - 1 - j, 1)

        sums = {}
        for b in range(TILES + 2):
            bwd_out(old, sums, (b,))
            bwd_softmax(cur, (b - 1,))
            bwd_scores(new, (b - 2,))
        return cur, new

    last = lax.fori_loop(0, turns, bwd_turn, (first, first))[0]
    for act in rs_events(plan.bwd_sends[turns - 1]):
        act()
    bwd_out(last, {})

    x_d = [mate_copy(theirs(dq_s, h), xdq.at[pl.ds(h * HEADS, HEADS)], 14 + h) for h in range(2)]
    for copy in x_d:
        copy.start()
    for unit in plan.bwd_sends[turns]:
        for act in rs_events([unit]):
            act()
    for h in range(2):
        x_d[h].wait_recv()
        for head in range(HEADS):
            total = (dq_s[h * TILES + head] + xdq[h * HEADS + head]) * SCALE
            dq_o[head, half(h), :] = total.T.astype(bf16)
    stores.append(pltpu.make_async_copy(dq_o, dq_ref, io.at[9]))
    stores[1].start()
    for k, x in plan.bwd_last:
        rs_add(0, k, x)
    for x, (buf, ref, factor) in enumerate(((dk_o, dk_ref, SCALE), (dv_o, dv_ref, 1.0))):
        for h in range(2):
            buf[half(h), :] = (stg[0, 0, x, h] * factor).T.astype(bf16)
        stores.append(pltpu.make_async_copy(buf, ref, io.at[10 + x]))
        stores[-1].start()

    for k in range(1, plan.blocks):
        for x in range(2):
            ag_copy(k, x).wait_send()
            rs_copy(k, x).wait_send()
    for copy in x_q + x_m + x_r + x_d:
        copy.wait_send()
    for copy in stores:
        copy.wait()


def relay(*refs):
    count = (len(refs) - 1) // 3
    src, dst, buf, sem = refs[:count], refs[count:2 * count], refs[2 * count:3 * count], refs[3 * count]
    into = [pltpu.make_async_copy(a, b, sem.at[i]) for i, (a, b) in enumerate(zip(src, buf))]
    out = [pltpu.make_async_copy(b, c, sem.at[count + i]) for i, (b, c) in enumerate(zip(buf, dst))]
    for copy in into:
        copy.start()
    for i in range(count):
        into[i].wait()
        out[i].start()
    for copy in out:
        copy.wait()


def solution(mesh):
    size = mesh.shape["ctx"]
    plan = Plan(int(math.log2(size)) - 1)
    spec = P("data", "ctx", None, None)
    n = plan.blocks
    f32, bf16 = jnp.float32, jnp.bfloat16
    vm, sem = pltpu.VMEM, pltpu.SemaphoreType.DMA

    def local(queries, keys, values, grad_out):
        tokens = queries.shape[1]
        q = queries[0].transpose(1, 0, 2)
        g = grad_out[0].transpose(1, 0, 2)
        tile = (128, 128)
        big = jax.ShapeDtypeStruct((HEADS, tokens, HD), bf16)
        small = jax.ShapeDtypeStruct((tokens, HD), bf16)
        anywhere = pl.BlockSpec(memory_space=pl.ANY)
        twenty, ten, stat, few = (2 * TILES,) + tile, (TILES,) + tile, (2 * TILES, 8, 128), (TILES, 8, 128)
        results = pl.pallas_call(
            functools.partial(kernel, plan),
            out_shape=(big, big, small, small),
            in_specs=[anywhere] * 4,
            out_specs=(anywhere,) * 4,
            scratch_shapes=[
                vm((n // 2, 2, 2, 2) + tile, bf16), vm((n // 2, 2, 2, 2) + tile, f32), vm((n, 2, 2) + tile, f32),
                vm((TILES, 256, 256), f32), vm((TILES, 256, 256), f32), vm((TILES * 256, 256), bf16), vm((TILES * 256, 256), bf16),
                vm((TILES, 8, 256), f32),
                vm(twenty, bf16), vm(twenty, bf16), vm((2,) + tile, bf16), vm(twenty, bf16), vm(twenty, bf16),
                vm((2 * TILES, 2) + tile, bf16),
                vm(twenty, f32), vm(stat, f32), vm(stat, f32), vm((TILES, 8, 256), f32),
                vm(ten, f32), vm(few, f32), vm(few, f32), vm(stat, f32), vm(stat, f32), vm(twenty, f32), vm(twenty, f32),
                vm(twenty, f32), vm(ten, f32),
                vm(big.shape, bf16), vm(big.shape, bf16), vm(small.shape, bf16), vm(small.shape, bf16),
                sem((n, 2)), sem((n, 2)), sem((n, 2)), sem((n, 2)), sem((16,)), sem((16,)), sem((12,)),
            ],
            compiler_params=pltpu.CompilerParams(collective_id=0, has_side_effects=True, vmem_limit_bytes=67043328),
            cost_estimate=pl.CostEstimate(flops=14 * 640 * PIECE * n * 2 * HD, bytes_accessed=4 << 20, transcendentals=0),
        )(q, keys[0, :, 0], values[0, :, 0], g)
        o, dq, dk, dv = pl.pallas_call(
            relay,
            out_shape=(big, big, small, small),
            in_specs=[anywhere] * 4,
            out_specs=(anywhere,) * 4,
            scratch_shapes=[vm(x.shape, bf16) for x in (big, big, small, small)] + [sem((8,))],
            cost_estimate=pl.CostEstimate(flops=1 << 20, bytes_accessed=2 << 20, transcendentals=0),
        )(*results)
        return (o.transpose(1, 0, 2)[None], dq.transpose(1, 0, 2)[None], dk[None, :, None], dv[None, :, None])

    return jax.shard_map(local, mesh=mesh, in_specs=(spec,) * 4, out_specs=(spec,) * 4, check_vma=False)
```

time: 137 us -> 131 us (0.956)
  local copies, waits for them, and re-layouts: 4.12 us -> 0 us
  Pallas kernels: 132 us -> 130 us
    unnamed x10 -> x0, local copies, waits for them, and re-layouts: 4.12 us -> none
    pallas_call x1, Pallas kernels: 132 us -> 128 us  [local(): pl.pallas_call(functools.partial(kernel, plan), out_shape=(big, big, smal...]
    pallas_call x0 -> x1, Pallas kernels: none -> 1.91 us  [local(): pl.pallas_call(relay, out_shape=(big, big, small, small), in_specs=[anywh...]
where the time goes in v4:
time: 131 us; the launch traced here: 130 us
  Pallas kernels  130 us (99%)
    pallas_call x1, Pallas kernels, local(): pl.pallas_call(functools.partial(kernel, plan), out_shape=(big, big, smal...  128 us

profile of v4, /device:TPU:0, one launch (start us, length us, event | category | flops | bytes accessed | tf_op | source)
XLA Modules:
  0.0 130.4 jit_solution(2899339445893422867)
XLA Ops:
  0.6 127.9 %shard_map.75 = (bf16[5,256,128]{2,1,0:T(8,128)(2,1)}, bf16[5,256,128]{2,1,0:T(8,128)(2,1)}, bf16[256,128]{1,0:T(8,128)(2,1)}, bf16[256,128]{1,0:T(8,128)(2,1)}) custom-call(bf16[5,256,128]{2,1,0:T(8,128)(2,1)} %bitcast.16, bf16[256,128]{1,0:T(8,128)(2,1)} %bitcast.20, bf16[256,128]{1,0:T(8,128)(2,1)} %bitcast.21, bf16[5,256,128]{2,1,0:T(8,128)(2,1)} %bitcast.17), custom_call_target="tpu_custom_call" | custom-call | flops 18790481920 | bytes 4194304 | tf_op jit(solution)/shard_map/pallas_call | solution.py:590
  128.5 1.9 %shard_map.76 = (bf16[5,256,128]{2,1,0:T(8,128)(2,1)}, bf16[5,256,128]{2,1,0:T(8,128)(2,1)}, bf16[256,128]{1,0:T(8,128)(2,1)}, bf16[256,128]{1,0:T(8,128)(2,1)}) custom-call(bf16[5,256,128]{2,1,0:T(8,128)(2,1)} %get-tuple-element.12.refs_0_, bf16[5,256,128]{2,1,0:T(8,128)(2,1)} %get-tuple-element.13.refs_1_, bf16[256,128]{1,0:T(8,128)(2,1)} %get-tuple-element.14.refs_2_, ...), custom_call_target="tpu_custom_call" | custom-call | flops 1048576 | bytes 2097152 | tf_op jit(solution)/shard_map/pallas_call | solution.py:610

commit v5 on v4

--- a/solution.py
+++ b/solution.py
@@ -17,11 +17,11 @@
 LOG2E = 1.4426950408889634
 TILES = 2 * HEADS
 
-KEY_TREE = "011221033303230444022204041233350552225555023554414241430104552"
-VALUE_TREE = "010201133132030404124203411303055112015353553124445242153504414"
-DK_TREE = "011201030113022404042143013424255155512503350504044245135103424"
-DV_TREE = "011222133313022444124423431243055505220331030555415254133515214"
-BWD_ORDER = "vlruetqkfpndmjbs7h9c56i34o8ag21"
+KEY_TREE = "010222233102310441124214030442355112212553052304545225430514015"
+VALUE_TREE = "011201033303033401044244434301355115220533150515540242154453254"
+DK_TREE = "010222230332012401140144034343155105020503552515410521435133551"
+DV_TREE = "011221233112231444444123310433250555512333020125545204050434440"
+BWD_ORDER = "vtrnuqs7p3colifmejbad495h6k28g1"
 
 
 def popcount(value):
@@ -57,7 +57,7 @@
         self.forward()
         self.backward()
 
-    def forward(self, unit_us=1.41, hop_us=1.9, turn_us=0.85):
+    def forward(self, unit_us=1.41, hop_us=1.9, turn_us=0.84):
         free = [0.0] * self.dims
         due = {}
         done = {(0, 0), (0, 1)}
@@ -100,7 +100,7 @@
         self.fwd_pairs = order
         self.fwd_mate = max(i for i, pair in enumerate(order) if pair == 0)
 
-    def backward(self, unit_us=2.82, hop_us=2.0, turn_us=1.6, add_us=0.03):
+    def backward(self, unit_us=2.82, hop_us=2.0, turn_us=1.52, add_us=0.03):
         if self.dims == 6:
             order = [int(c, 32) for c in BWD_ORDER]
         else:
@@ -146,6 +146,14 @@
         self.bwd_last = sorted((u for x in range(2) for u in kids((0, x))), key=lambda u: due[u])
 
 
+def div(a, b):
+    return lax.div(a, jnp.int32(b))
+
+
+def mod(a, b):
+    return lax.rem(a, jnp.int32(b))
+
+
 def xor(a, b):
     return a + b - 2 * a * b
 
@@ -154,7 +162,7 @@
     level = [jnp.int32(v) for v in table]
     bit = 1
     while len(level) > 1:
-        odd = (index // bit) % 2 == 1
+        odd = mod(div(index, bit), 2) == 1
         nxt = [jnp.where(odd, level[i + 1], level[i]) for i in range(0, len(level) - 1, 2)]
         level = nxt + level[2 * len(nxt):]
         bit *= 2
@@ -162,7 +170,7 @@
 
 
 def branch(index, count, leaf):
-    once = index // count + 1
+    once = div(index, count) + 1
 
     def pick(low, high):
         if high - low == 1:
@@ -184,9 +192,9 @@
     pieces = 4 * plan.blocks
     f32, bf16 = jnp.float32, jnp.bfloat16
     me = lax.axis_index("ctx")
-    core = me % 2
-    chip = me // 2
-    bits = [(chip // (1 << d)) % 2 for d in range(dims)]
+    core = mod(me, 2)
+    chip = div(me, 2)
+    bits = [mod(div(chip, 1 << d), 2) for d in range(dims)]
     gray = [xor(bits[d], bits[d + 1]) if d % 2 == 0 and d + 1 < dims else bits[d] for d in range(dims)]
     nbr = []
     for d in range(dims):
@@ -195,7 +203,7 @@
             other = other + (1 - 2 * bits[d - 1]) * (1 << (d - 1))
         nbr.append(2 * other + core)
     mate = me + 1 - 2 * core
-    my_pair = chip // 2
+    my_pair = div(chip, 2)
 
     barrier = pltpu.get_barrier_semaphore()
     for dev in nbr + [mate]:
@@ -216,8 +224,6 @@
     mst[...] = jnp.full(mst.shape, NEG, f32)
     lst[...] = jnp.zeros(lst.shape, f32)
     acc[...] = jnp.zeros(acc.shape, f32)
-    dec[...] = jnp.ones(dec.shape, f32)
-    p_buf[...] = jnp.zeros(p_buf.shape, bf16)
     for copy in loads[:4]:
         copy.wait()
     for h in range(2):
@@ -278,16 +284,16 @@
         pl.loop(h * TILES + HEADS, h * TILES + TILES)(transposes)
 
     def is_future(pair):
-        rel = [(pair // (1 << (d - 1))) % 2 for d in range(1, dims)]
+        rel = [mod(div(pair, 1 << (d - 1)), 2) for d in range(1, dims)]
         gp = [None] + [xor(gray[d], rel[d - 1]) for d in range(1, dims)]
         other = gp[1] if dims > 1 else 0
         for d in range(2, dims):
             bit = xor(gp[d], gp[d + 1]) if d % 2 == 0 and d + 1 < dims else gp[d]
             other = other + bit * (1 << (d - 1))
-        return (other - my_pair + plan.blocks) // plan.blocks
+        return div(other - my_pair + plan.blocks, plan.blocks)
 
     def place(pair, a):
-        mine = (plan.blocks // 2 - pair) // (plan.blocks // 2)
+        mine = div(plan.blocks // 2 - pair, plan.blocks // 2)
         fut = is_future(pair)
         turn = (pair,)
         for slot in range(2):
@@ -295,8 +301,10 @@
             turn += (mine * a, h, mine * a + 1 - mine, mine + h, mine * slot + (1 - mine) * (fut + (1 - fut) * slot))
         return turn
 
-    def groups(turn):
+    def groups(turn, some):
         for slot in range(2):
+            if not any(slot * HEADS <= b < slot * HEADS + HEADS for b in some):
+                continue
             p0, h0, p1, h1, qg = turn[1 + 5 * slot:6 + 5 * slot]
             yield slot, ((turn[0], p0, h0), (turn[0], p1, h1)), qg * TILES
 
@@ -316,14 +324,14 @@
         return pl.ds(b * 256, 256)
 
     def mask_scores(a, keys_axis):
-        key_low = me + a * (2 * (1 - 2 * (chip % 2)))
+        key_low = me + a * (2 * (1 - 2 * mod(chip, 2)))
 
         def two(base0, base1, axis):
             i = lax.broadcasted_iota(jnp.int32, (256, 256), axis)
             return i + jnp.where(i < PIECE, base0, base1 - PIECE)
 
         def query_base(c):
-            h, par = c // TILES, (c // HEADS) % 2
+            h, par = div(c, TILES), mod(div(c, HEADS), 2)
             low = me + par * (mate - me)
             return (low + h * (pieces - 1 - 2 * low)) * PIECE
 
@@ -337,7 +345,7 @@
                 top[b] = jnp.max(s.reshape(32, 8, 256), axis=0)
 
     def fwd_scores(turn, some=range(TILES)):
-        for slot, where, base in groups(turn):
+        for slot, where, base in groups(turn, some):
             kt = key_tile(where)
             twice = jnp.concatenate([kt, kt], axis=1)
             for t in range(HEADS):
@@ -349,7 +357,7 @@
                     top[b] = jnp.max(s.reshape(32, 8, 256), axis=0)
 
     def fwd_softmax(turn, some):
-        for slot, _, base in groups(turn):
+        for slot, _, base in groups(turn, some):
             for t in range(HEADS):
                 b, c = slot * HEADS + t, base + 2 * t
                 if b not in some:
@@ -367,7 +375,7 @@
                     lst[c + j] = l_new[:, cols]
 
     def fwd_out(turn, some=range(TILES)):
-        for slot, where, base in groups(turn):
+        for slot, where, base in groups(turn, some):
             vt = value_tile_t(where)
             for t in range(HEADS):
                 b, c = slot * HEADS + t, base + 2 * t
@@ -382,38 +390,45 @@
 
     for act in ag_events(plan.fwd_waits[0]):
         act()
-    first = fwd_place(me * 0)
-    fwd_scores(first)
+    old = fwd_place(me * 0)
+    fwd_scores(old)
+    mask_scores(0, 0)
+    for act in ag_events(plan.fwd_waits[1]):
+        act()
+    cur = fwd_place(me * 0 + 1)
+    for b in range(TILES + 1):
+        fwd_scores(cur, (b - 1,))
+        fwd_softmax(old, (b,))
 
     def fwd_turn(j, carry):
-        old, cur = carry
-        branch(j, turns, lambda i: ag_events(plan.fwd_waits[i + 1]))
-        new = fwd_place(j + 1)
-
-        @pl.when((j == 0) | (j == plan.fwd_mate))
+        old, cur, new = carry
+        branch(j, turns, lambda i: ag_events(plan.fwd_waits[i + 1]) if i else [])
+
+        @pl.when(j == plan.fwd_mate)
         def _():
-            mask_scores(jnp.minimum(j, 1), 0)
-
+            mask_scores(1, 0)
+
+        after = fwd_place(j + 2)
         for b in range(TILES + 2):
             fwd_scores(new, (b - 2,))
             fwd_softmax(cur, (b - 1,))
             fwd_out(old, (b,))
-        return cur, new
-
-    last = lax.fori_loop(0, turns, fwd_turn, (first, first))[0]
+        return cur, new, after
+
+    last = lax.fori_loop(1, turns, fwd_turn, (old, cur, fwd_place(me * 0 + 2)))[0]
     fwd_out(last)
 
-    def bwd_scores(turn, some=range(TILES)):
-        for slot, where, base in groups(turn):
-            kt, vt = key_tile(where), value_tile_t(where)
+    def bwd_scores(turn, some=range(TILES), parts=(0, 1)):
+        for slot, where, base in groups(turn, some):
+            kt_t, vt = key_tile(where).T, value_tile_t(where)
             for t in range(HEADS):
                 b, c = slot * HEADS + t, base + 2 * t
-                if b in some:
-                    s_buf[b] = lax.dot_general(tall(q_s, c), kt, (((1,), (1,)), ((), ())), preferred_element_type=f32)
-                    t_buf[b] = jnp.dot(tall(g_s, c), vt, preferred_element_type=f32)
+                for part in parts if b in some else ():
+                    buf, lhs, rhs = ((s_buf, q_s, kt_t), (t_buf, g_s, vt))[part]
+                    buf[b] = jnp.dot(tall(lhs, c), rhs, preferred_element_type=f32)
 
     def bwd_softmax(turn, some):
-        for slot, _, base in groups(turn):
+        for slot, _, base in groups(turn, some):
             for t in range(HEADS):
                 b, c = slot * HEADS + t, base + 2 * t
                 if b in some:
@@ -422,26 +437,30 @@
                     p_buf[rows(b), :] = p.astype(bf16)
                     d_buf[rows(b), :] = (p * (t_buf[b] - jnp.concatenate([dr, dr], axis=1))).astype(bf16)
 
-    def bwd_out(turn, sums, some=range(TILES)):
-        for slot, where, base in groups(turn):
-            kt = key_tile(where)
+    def bwd_out(turn, sums, some=range(TILES), parts=(0, 1)):
+        for slot, where, base in groups(turn, some):
+            kt_t = key_tile(where).T
             for t in range(HEADS):
                 b, c = slot * HEADS + t, base + 2 * t
                 if b not in some:
                     continue
                 ds = d_buf[rows(b), :]
-                for x, (ref, buf) in enumerate(((q_t, ds), (g_t, p_buf[rows(b), :]))):
+                if 0 in parts:
+                    dq = lax.dot_general(kt_t, ds, (((1,), (1,)), ((), ())), preferred_element_type=f32)
+                    for j in range(2):
+                        dq_s[c + j] += dq[:, j * 128:j * 128 + 128]
+                for x, (ref, buf) in enumerate(((q_t, ds), (g_t, p_buf[rows(b), :])) if 1 in parts else ()):
                     grad = jnp.dot(wide(ref, c), buf, preferred_element_type=f32)
                     sums[x] = sums[x] + grad if t else grad
                     for j, (pair, par, h) in enumerate(where if t == HEADS - 1 else ()):
-                        stg[pair, par, x, h] += sums[x][:, j * 128:j * 128 + 128]
-                dq = lax.dot_general(kt, ds, (((0,), (1,)), ((), ())), preferred_element_type=f32)
-                for j in range(2):
-                    dq_s[c + j] += dq[:, j * 128:j * 128 + 128]
+                        value = sums[x][:, j * 128:j * 128 + 128]
+                        if slot:
+                            value = value + stg[pair, par, x, h]
+                        stg[pair, par, x, h] = value
 
     def bwd_place(j):
         at = jnp.minimum(j, turns - 1)
-        return place(lookup(at, plan.bwd_pairs), 1 - (at + 1) // turns)
+        return place(lookup(at, plan.bwd_pairs), 1 - div(at + 1, turns))
 
     x_m = []
     for h in range(2):
@@ -452,8 +471,6 @@
         copy.start()
     first = bwd_place(me * 0)
     bwd_scores(first)
-    p_buf[...] = jnp.zeros(p_buf.shape, bf16)
-    d_buf[...] = jnp.zeros(d_buf.shape, bf16)
     dq_s[...] = jnp.zeros(dq_s.shape, f32)
     x_r = [mate_copy(own(ref, h), theirs(ref, h), 10 + 2 * j + h) for j, ref in enumerate((lrow, drow)) for h in range(2)]
 
@@ -471,8 +488,8 @@
             lrow[c] = m + jnp.log2(total)
             rounded = out.astype(bf16).astype(f32)
             drow[c] = jnp.broadcast_to(jnp.sum(rounded * g_t[c].astype(f32), axis=0, keepdims=True), (8, 128))
-    for copy in x_r:
-        copy.start()
+        for copy in x_r[h::2]:
+            copy.start()
     stores = [pltpu.make_async_copy(o_s, o_ref, io.at[8])]
     stores[0].start()
 
@@ -496,31 +513,35 @@
         return ([functools.partial(rs_add, r, k, x) for r, x in sends for k in plan.bwd[x].kids[r]]
                 + [rs_copy(r, x).start for r, x in sends])
 
-    def clear(pair):
-        for i in range(8):
-            stg[pair, i // 4, i // 2 % 2, i % 2] = jnp.zeros((128, 128), f32)
+    if turns == 2:
+        mask_scores(1, 1)
+    cur = bwd_place(me * 0 + 1)
+    for b in range(TILES + 1):
+        bwd_softmax(first, (b,))
+        bwd_scores(cur, (b - 1,))
 
     def bwd_turn(j, carry):
-        old, cur = carry
+        old, cur, new = carry
         branch(j, turns, lambda i: rs_events(plan.bwd_sends[i - 1]) if i else [])
-        new = bwd_place(j + 1)
-
-        @pl.when((j > 0) & (j < turns))
+
+        @pl.when(j < turns - 1)
         def _():
-            clear(old[0])
+            for i in range(4):
+                stg[old[0], i // 2, i % 2, 1] = jnp.zeros((128, 128), f32)
 
         @pl.when(j >= turns - 2)
         def _():
             mask_scores(turns - 1 - j, 1)
 
+        after = bwd_place(j + 2)
         sums = {}
         for b in range(TILES + 2):
             bwd_out(old, sums, (b,))
             bwd_softmax(cur, (b - 1,))
             bwd_scores(new, (b - 2,))
-        return cur, new
-
-    last = lax.fori_loop(0, turns, bwd_turn, (first, first))[0]
+        return cur, new, after
+
+    last = lax.fori_loop(1, turns, bwd_turn, (first, cur, bwd_place(me * 0 + 2)))[0]
     for act in rs_events(plan.bwd_sends[turns - 1]):
         act()
     bwd_out(last, {})

time: 131 us -> 125 us (0.954)
  Pallas kernels: 130 us -> 124 us
    pallas_call x1, Pallas kernels: 128 us -> 122 us  [local(): pl.pallas_call(functools.partial(kernel, plan), out_shape=(big, big, smal...]
where the time goes in v5:
time: 125 us
  Pallas kernels  124 us (99%)
    pallas_call x1, Pallas kernels, local(): pl.pallas_call(functools.partial(kernel, plan), out_shape=(big, big, smal...  122 us

profile of v5, /device:TPU:0, one launch (start us, length us, event | category | flops | bytes accessed | tf_op | source)
XLA Modules:
  0.0 124.7 jit_solution(6852352617273451148)
XLA Ops:
  0.6 122.2 %shard_map.75 = (bf16[5,256,128]{2,1,0:T(8,128)(2,1)}, bf16[5,256,128]{2,1,0:T(8,128)(2,1)}, bf16[256,128]{1,0:T(8,128)(2,1)}, bf16[256,128]{1,0:T(8,128)(2,1)}) custom-call(bf16[5,256,128]{2,1,0:T(8,128)(2,1)} %bitcast.16, bf16[256,128]{1,0:T(8,128)(2,1)} %bitcast.20, bf16[256,128]{1,0:T(8,128)(2,1)} %bitcast.21, bf16[5,256,128]{2,1,0:T(8,128)(2,1)} %bitcast.17), custom_call_target="tpu_custom_call" | custom-call | flops 18790481920 | bytes 4194304 | tf_op jit(solution)/shard_map/pallas_call | solution.py:611
  122.8 1.9 %shard_map.76 = (bf16[5,256,128]{2,1,0:T(8,128)(2,1)}, bf16[5,256,128]{2,1,0:T(8,128)(2,1)}, bf16[256,128]{1,0:T(8,128)(2,1)}, bf16[256,128]{1,0:T(8,128)(2,1)}) custom-call(bf16[5,256,128]{2,1,0:T(8,128)(2,1)} %get-tuple-element.12.refs_0_, bf16[5,256,128]{2,1,0:T(8,128)(2,1)} %get-tuple-element.13.refs_1_, bf16[256,128]{1,0:T(8,128)(2,1)} %get-tuple-element.14.refs_2_, ...), custom_call_target="tpu_custom_call" | custom-call | flops 1048576 | bytes 2097152 | tf_op jit(solution)/shard_map/pallas_call | solution.py:631

commit v6 on v5

--- a/solution.py
+++ b/solution.py
@@ -17,11 +17,11 @@
 LOG2E = 1.4426950408889634
 TILES = 2 * HEADS
 
-KEY_TREE = "010222233102310441124214030442355112212553052304545225430514015"
-VALUE_TREE = "011201033303033401044244434301355115220533150515540242154453254"
-DK_TREE = "010222230332012401140144034343155105020503552515410521435133551"
-DV_TREE = "011221233112231444444123310433250555512333020125545204050434440"
-BWD_ORDER = "vtrnuqs7p3colifmejbad495h6k28g1"
+KEY_TREE = "011222233332220401120144343324455112221331530525044554535415311"
+VALUE_TREE = "010202030312010444044424310243155552011305020335411555543543021"
+DK_TREE = "011202030133312401444244343301355152021301322315050445445404320"
+DV_TREE = "011222133132330444122243010422050155555551523155450502240135413"
+BWD_ORDER = "vrndou7tmjqflpsh6ebk9ac35i4g128"
 
 
 def popcount(value):
@@ -57,7 +57,7 @@
         self.forward()
         self.backward()
 
-    def forward(self, unit_us=1.41, hop_us=1.9, turn_us=0.84):
+    def forward(self, unit_us=1.41, hop_us=1.9, turn_us=0.87):
         free = [0.0] * self.dims
         due = {}
         done = {(0, 0), (0, 1)}
@@ -100,7 +100,7 @@
         self.fwd_pairs = order
         self.fwd_mate = max(i for i, pair in enumerate(order) if pair == 0)
 
-    def backward(self, unit_us=2.82, hop_us=2.0, turn_us=1.52, add_us=0.03):
+    def backward(self, unit_us=2.86, hop_us=2.1, turn_us=1.55, add_us=0.035):
         if self.dims == 6:
             order = [int(c, 32) for c in BWD_ORDER]
         else:
@@ -108,15 +108,14 @@
         order += [0, 0]
         free = [0.0] * self.dims
         due = {}
-        waiting = set()
-        now = turn_us
-        steps, sends = [], []
-        position = 0
+        waiting, sends, steps = set(), [], []
+        now = 1.35
 
         def kids(unit):
             return [(k, unit[1]) for k in self.bwd[unit[1]].kids[unit[0]]]
 
-        while True:
+        def flush():
+            nonlocal now
             able = True
             while able:
                 able = [u for u in waiting if all(due.get(k, 1e9) <= now for k in kids(u))]
@@ -127,21 +126,22 @@
                     free[d] = max(free[d], now) + unit_us
                     due[unit] = free[d] + hop_us
                     sends.append(unit)
-            if position < len(order):
-                pair = order[position]
-                position += 1
-                now += turn_us
-                if pair:
-                    waiting |= {(2 * pair + i, x) for i in range(2) for x in range(2)}
-                elif position < len(order):
-                    waiting |= {(1, 0), (1, 1)}
+
+        for i, pair in enumerate(order):
+            waiting |= {(r, x) for r in (2 * pair, 2 * pair + 1) for x in range(2) if r} if i < len(order) - 1 else set()
+            flush()
+            steps.append(sends)
+            sends = []
+            if i == 0:
+                now += 0.85
+                flush()
                 steps.append(sends)
                 sends = []
-            elif waiting:
-                now = max(now, min(max(due.get(k, 1e9) for k in kids(u)) for u in waiting))
-            else:
-                break
-        self.bwd_sends = steps + [sends]
+            now += turn_us if i < len(order) - 1 else 0.0
+        while waiting:
+            now = max(now, min(max(due.get(k, 1e9) for k in kids(u)) for u in waiting))
+            flush()
+        self.bwd_sends = steps[:-1] + [steps[-1] + sends]
         self.bwd_pairs = order
         self.bwd_last = sorted((u for x in range(2) for u in kids((0, x))), key=lambda u: due[u])
 
@@ -314,6 +314,12 @@
     def value_tile_t(where):
         return jnp.concatenate([kv[pair, par, 1, h] for pair, par, h in where], axis=1)
 
+    def tile_of(memo, slot, kind, where):
+        key = (kind, slot)
+        if key not in memo:
+            memo[key] = value_tile_t(where) if kind == "v" else key_tile(where) if kind == "k" else key_tile(where).T
+        return memo[key]
+
     def wide(ref, c):
         return jnp.concatenate([ref[c], ref[c + 1]], axis=1)
 
@@ -344,9 +350,9 @@
             if keys_axis == 0:
                 top[b] = jnp.max(s.reshape(32, 8, 256), axis=0)
 
-    def fwd_scores(turn, some=range(TILES)):
+    def fwd_scores(turn, some, memo):
         for slot, where, base in groups(turn, some):
-            kt = key_tile(where)
+            kt = tile_of(memo, slot, "k", where)
             twice = jnp.concatenate([kt, kt], axis=1)
             for t in range(HEADS):
                 b, c = slot * HEADS + t, base + 2 * t
@@ -374,9 +380,9 @@
                     mst[c + j] = m_new[:, cols]
                     lst[c + j] = l_new[:, cols]
 
-    def fwd_out(turn, some=range(TILES)):
+    def fwd_out(turn, some, memo):
         for slot, where, base in groups(turn, some):
-            vt = value_tile_t(where)
+            vt = tile_of(memo, slot, "v", where)
             for t in range(HEADS):
                 b, c = slot * HEADS + t, base + 2 * t
                 if b in some:
@@ -388,16 +394,18 @@
     def fwd_place(j):
         return place(lookup(jnp.minimum(j, turns - 1), plan.fwd_pairs), jnp.minimum(j, 1))
 
+    every = range(TILES)
     for act in ag_events(plan.fwd_waits[0]):
         act()
     old = fwd_place(me * 0)
-    fwd_scores(old)
+    fwd_scores(old, every, {})
     mask_scores(0, 0)
     for act in ag_events(plan.fwd_waits[1]):
         act()
     cur = fwd_place(me * 0 + 1)
+    memo = {}
     for b in range(TILES + 1):
-        fwd_scores(cur, (b - 1,))
+        fwd_scores(cur, (b - 1,), memo)
         fwd_softmax(old, (b,))
 
     def fwd_turn(j, carry):
@@ -409,23 +417,23 @@
             mask_scores(1, 0)
 
         after = fwd_place(j + 2)
+        memo, memo_old = {}, {}
         for b in range(TILES + 2):
-            fwd_scores(new, (b - 2,))
+            fwd_scores(new, (b - 2,), memo)
             fwd_softmax(cur, (b - 1,))
-            fwd_out(old, (b,))
+            fwd_out(old, (b,), memo_old)
         return cur, new, after
 
     last = lax.fori_loop(1, turns, fwd_turn, (old, cur, fwd_place(me * 0 + 2)))[0]
-    fwd_out(last)
-
-    def bwd_scores(turn, some=range(TILES), parts=(0, 1)):
+    fwd_out(last, every, {})
+
+    def bwd_scores(turn, some, memo):
         for slot, where, base in groups(turn, some):
-            kt_t, vt = key_tile(where).T, value_tile_t(where)
             for t in range(HEADS):
                 b, c = slot * HEADS + t, base + 2 * t
-                for part in parts if b in some else ():
-                    buf, lhs, rhs = ((s_buf, q_s, kt_t), (t_buf, g_s, vt))[part]
-                    buf[b] = jnp.dot(tall(lhs, c), rhs, preferred_element_type=f32)
+                if b in some:
+                    for buf, lhs, kind in ((s_buf, q_s, "t"), (t_buf, g_s, "v")):
+                        buf[b] = jnp.dot(tall(lhs, c), tile_of(memo, slot, kind, where), preferred_element_type=f32)
 
     def bwd_softmax(turn, some):
         for slot, _, base in groups(turn, some):
@@ -437,26 +445,22 @@
                     p_buf[rows(b), :] = p.astype(bf16)
                     d_buf[rows(b), :] = (p * (t_buf[b] - jnp.concatenate([dr, dr], axis=1))).astype(bf16)
 
-    def bwd_out(turn, sums, some=range(TILES), parts=(0, 1)):
+    def bwd_out(turn, some, memo):
         for slot, where, base in groups(turn, some):
-            kt_t = key_tile(where).T
             for t in range(HEADS):
                 b, c = slot * HEADS + t, base + 2 * t
                 if b not in some:
                     continue
                 ds = d_buf[rows(b), :]
-                if 0 in parts:
-                    dq = lax.dot_general(kt_t, ds, (((1,), (1,)), ((), ())), preferred_element_type=f32)
-                    for j in range(2):
-                        dq_s[c + j] += dq[:, j * 128:j * 128 + 128]
-                for x, (ref, buf) in enumerate(((q_t, ds), (g_t, p_buf[rows(b), :])) if 1 in parts else ()):
+                dq = lax.dot_general(tile_of(memo, slot, "t", where), ds, (((1,), (1,)), ((), ())), preferred_element_type=f32)
+                for j in range(2):
+                    dq_s[c + j] += dq[:, j * 128:j * 128 + 128]
+                for x, (ref, buf) in enumerate(((q_t, ds), (g_t, p_buf[rows(b), :]))):
                     grad = jnp.dot(wide(ref, c), buf, preferred_element_type=f32)
-                    sums[x] = sums[x] + grad if t else grad
+                    memo[x] = memo[x] + grad if t else grad
                     for j, (pair, par, h) in enumerate(where if t == HEADS - 1 else ()):
-                        value = sums[x][:, j * 128:j * 128 + 128]
-                        if slot:
-                            value = value + stg[pair, par, x, h]
-                        stg[pair, par, x, h] = value
+                        value = memo[x][:, j * 128:j * 128 + 128]
+                        stg[pair, par, x, h] = value + stg[pair, par, x, h] if slot else value
 
     def bwd_place(j):
         at = jnp.minimum(j, turns - 1)
@@ -470,7 +474,7 @@
     for copy in x_m:
         copy.start()
     first = bwd_place(me * 0)
-    bwd_scores(first)
+    bwd_scores(first, every, {})
     dq_s[...] = jnp.zeros(dq_s.shape, f32)
     x_r = [mate_copy(own(ref, h), theirs(ref, h), 10 + 2 * j + h) for j, ref in enumerate((lrow, drow)) for h in range(2)]
 
@@ -513,38 +517,54 @@
         return ([functools.partial(rs_add, r, k, x) for r, x in sends for k in plan.bwd[x].kids[r]]
                 + [rs_copy(r, x).start for r, x in sends])
 
-    if turns == 2:
-        mask_scores(1, 1)
-    cur = bwd_place(me * 0 + 1)
-    for b in range(TILES + 1):
-        bwd_softmax(first, (b,))
-        bwd_scores(cur, (b - 1,))
+    def clear(pair):
+        for i in range(4):
+            stg[pair, i // 2, i % 2, 1] = jnp.zeros((128, 128), f32)
+
+    def bwd_start(j, carry):
+        _, cur, new = carry
+        if turns < 4:
+            mask_scores(turns - 1 - j, 1)
+        after = bwd_place(j + 2)
+        memo = {}
+        for b in range(TILES + 1):
+            bwd_softmax(cur, (b,))
+            bwd_scores(new, (b - 1,), memo)
+
+        @pl.when(j == 0)
+        def _():
+            clear(cur[0])
+            bwd_out(cur, every, {})
+            for act in rs_events(plan.bwd_sends[0]):
+                act()
+
+        return cur, new, after
 
     def bwd_turn(j, carry):
         old, cur, new = carry
-        branch(j, turns, lambda i: rs_events(plan.bwd_sends[i - 1]) if i else [])
+        branch(j, turns, lambda i: rs_events(plan.bwd_sends[i - 1]) if i > 1 else [])
 
         @pl.when(j < turns - 1)
         def _():
-            for i in range(4):
-                stg[old[0], i // 2, i % 2, 1] = jnp.zeros((128, 128), f32)
+            clear(old[0])
 
         @pl.when(j >= turns - 2)
         def _():
             mask_scores(turns - 1 - j, 1)
 
         after = bwd_place(j + 2)
-        sums = {}
+        memo, memo_old = {}, {}
         for b in range(TILES + 2):
-            bwd_out(old, sums, (b,))
+            bwd_out(old, (b,), memo_old)
             bwd_softmax(cur, (b - 1,))
-            bwd_scores(new, (b - 2,))
+            bwd_scores(new, (b - 2,), memo)
         return cur, new, after
 
-    last = lax.fori_loop(1, turns, bwd_turn, (first, cur, bwd_place(me * 0 + 2)))[0]
+    start = lax.fori_loop(0, 2, bwd_start, (first, first, bwd_place(me * 0 + 1)))
+    last = lax.fori_loop(2, turns, bwd_turn, start)[0]
     for act in rs_events(plan.bwd_sends[turns - 1]):
         act()
-    bwd_out(last, {})
+    bwd_out(last, every, {})
 
     x_d = [mate_copy(theirs(dq_s, h), xdq.at[pl.ds(h * HEADS, HEADS)], 14 + h) for h in range(2)]
     for copy in x_d:

time: 125 us -> 124 us (level)
  no operation moved by 1% of the time
where the time goes in v6:
time: 124 us
  Pallas kernels  123 us (99%)
    pallas_call x1, Pallas kernels, local(): pl.pallas_call(functools.partial(kernel, plan), out_shape=(big, big, smal...  121 us

profile of v6, /device:TPU:0, one launch (start us, length us, event | category | flops | bytes accessed | tf_op | source)
XLA Modules:
  0.0 123.9 jit_solution(15378386946923840598)
XLA Ops:
  0.6 121.1 %shard_map.75 = (bf16[5,256,128]{2,1,0:T(8,128)(2,1)}, bf16[5,256,128]{2,1,0:T(8,128)(2,1)}, bf16[256,128]{1,0:T(8,128)(2,1)}, bf16[256,128]{1,0:T(8,128)(2,1)}) custom-call(bf16[5,256,128]{2,1,0:T(8,128)(2,1)} %bitcast.16, bf16[256,128]{1,0:T(8,128)(2,1)} %bitcast.20, bf16[256,128]{1,0:T(8,128)(2,1)} %bitcast.21, bf16[5,256,128]{2,1,0:T(8,128)(2,1)} %bitcast.17), custom_call_target="tpu_custom_call" | custom-call | flops 18790481920 | bytes 4194304 | tf_op jit(solution)/shard_map/pallas_call | solution.py:631
  121.8 1.9 %shard_map.76 = (bf16[5,256,128]{2,1,0:T(8,128)(2,1)}, bf16[5,256,128]{2,1,0:T(8,128)(2,1)}, bf16[256,128]{1,0:T(8,128)(2,1)}, bf16[256,128]{1,0:T(8,128)(2,1)}) custom-call(bf16[5,256,128]{2,1,0:T(8,128)(2,1)} %get-tuple-element.12.refs_0_, bf16[5,256,128]{2,1,0:T(8,128)(2,1)} %get-tuple-element.13.refs_1_, bf16[256,128]{1,0:T(8,128)(2,1)} %get-tuple-element.14.refs_2_, ...), custom_call_target="tpu_custom_call" | custom-call | flops 1048576 | bytes 2097152 | tf_op jit(solution)/shard_map/pallas_call | solution.py:651

commit v7 on v6

--- a/solution.py
+++ b/solution.py
@@ -16,12 +16,13 @@
 SCALE = HD ** -0.5
 LOG2E = 1.4426950408889634
 TILES = 2 * HEADS
-
-KEY_TREE = "011222233332220401120144343324455112221331530525044554535415311"
-VALUE_TREE = "010202030312010444044424310243155552011305020335411555543543021"
-DK_TREE = "011202030133312401444244343301355152021301322315050445445404320"
-DV_TREE = "011222133132330444122243010422050155555551523155450502240135413"
-BWD_ORDER = "vrndou7tmjqflpsh6ebk9ac35i4g128"
+SPAN = HEADS * PIECE
+
+KEY_TREE = "011222133332330444044204331303450512252553132154554251534405024"
+VALUE_TREE = "011202133303032404124114441201150505210501022525540551434312353"
+DK_TREE = "010222133132320404040144013222455152212303525124550544534132251"
+DV_TREE = "011221233112332404420104340431355155511535030505014404035353440"
+BWD_ORDER = "vuntrfmplsj7beodk6cq35haig98241"
 
 
 def popcount(value):
@@ -57,7 +58,7 @@
         self.forward()
         self.backward()
 
-    def forward(self, unit_us=1.41, hop_us=1.9, turn_us=0.87):
+    def forward(self, unit_us=1.41, hop_us=1.9, turn_us=0.78):
         free = [0.0] * self.dims
         due = {}
         done = {(0, 0), (0, 1)}
@@ -100,7 +101,7 @@
         self.fwd_pairs = order
         self.fwd_mate = max(i for i, pair in enumerate(order) if pair == 0)
 
-    def backward(self, unit_us=2.86, hop_us=2.1, turn_us=1.55, add_us=0.035):
+    def backward(self, unit_us=2.9, hop_us=2.1, turn_us=1.55, add_us=0.035):
         if self.dims == 6:
             order = [int(c, 32) for c in BWD_ORDER]
         else:
@@ -109,7 +110,7 @@
         free = [0.0] * self.dims
         due = {}
         waiting, sends, steps = set(), [], []
-        now = 1.35
+        now = 1.57
 
         def kids(unit):
             return [(k, unit[1]) for k in self.bwd[unit[1]].kids[unit[0]]]
@@ -218,12 +219,14 @@
                   pltpu.make_async_copy(k_ref.at[half(h)], kv.at[0, 0, 0, h], io.at[2 + h])]
     for h in range(2):
         for j, (src, dst) in enumerate(((q_ref, q_s), (g_ref, g_s))):
-            loads.append(pltpu.make_async_copy(src.at[:, half(h)], dst.at[pl.ds(h * TILES, HEADS)], io.at[4 + 2 * j + h]))
+            loads.append(pltpu.make_async_copy(src.at[:, half(h)], dst.at[h, pl.ds(0, HEADS)], io.at[4 + 2 * j + h]))
     for copy in loads:
         copy.start()
     mst[...] = jnp.full(mst.shape, NEG, f32)
     lst[...] = jnp.zeros(lst.shape, f32)
     acc[...] = jnp.zeros(acc.shape, f32)
+    dec[...] = jnp.ones(dec.shape, f32)
+    p_buf[...] = jnp.zeros(p_buf.shape, bf16)
     for copy in loads[:4]:
         copy.wait()
     for h in range(2):
@@ -247,18 +250,15 @@
         return pltpu.make_async_remote_copy(src_ref=src, dst_ref=dst, send_sem=x_send.at[sem], recv_sem=x_recv.at[sem],
                                             device_id={"ctx": mate}, device_id_type=MESH)
 
-    def own(ref, h):
-        return ref.at[pl.ds(h * TILES, HEADS)]
-
-    def theirs(ref, h):
-        return ref.at[pl.ds(h * TILES + HEADS, HEADS)]
+    ours, theirs = pl.ds(0, SPAN), pl.ds(SPAN, SPAN)
 
     for x in range(2):
         for k in plan.fwd[x].kids[0]:
             ag_copy(k, x).start()
     for copy in loads[4:]:
         copy.wait()
-    x_q = [mate_copy(own(ref, h), theirs(ref, h), 2 * j + h) for j, ref in enumerate((q_s, g_s)) for h in range(2)]
+    x_q = [mate_copy(ref.at[h, pl.ds(0, HEADS)], ref.at[h, pl.ds(HEADS, HEADS)], 2 * j + h)
+           for j, ref in enumerate((q_s, g_s)) for h in range(2)]
     for copy in x_q:
         copy.start()
 
@@ -267,21 +267,25 @@
 
     coef = SCALE * LOG2E
 
-    def transposes(c):
-        turned = q_s[c].T
-        q_t[c] = turned
-        g_t[c] = g_s[c].T
-        scaled = turned.astype(f32) * coef
-        high = scaled.astype(bf16)
-        c_t[c, 0] = high
-        c_t[c, 1] = (scaled - high.astype(f32)).astype(bf16)
+    def transposes(h):
+        def turn(i):
+            cols = pl.ds(pl.multiple_of(i * 128, 128), 128)
+            turned = q_s[h, i].T
+            q_t[h, :, cols] = turned
+            g_t[h, :, cols] = g_s[h, i].T
+            scaled = turned.astype(f32) * coef
+            high = scaled.astype(bf16)
+            c_t[h, pl.ds(0, HD), cols] = high
+            c_t[h, pl.ds(HD, HD), cols] = (scaled - high.astype(f32)).astype(bf16)
+
+        return turn
 
     for h in range(2):
-        pl.loop(h * TILES, h * TILES + HEADS)(transposes)
+        pl.loop(0, HEADS)(transposes(h))
     for copy in x_q:
         copy.wait_recv()
     for h in range(2):
-        pl.loop(h * TILES + HEADS, h * TILES + TILES)(transposes)
+        pl.loop(HEADS, TILES)(transposes(h))
 
     def is_future(pair):
         rel = [mod(div(pair, 1 << (d - 1)), 2) for d in range(1, dims)]
@@ -306,7 +310,7 @@
             if not any(slot * HEADS <= b < slot * HEADS + HEADS for b in some):
                 continue
             p0, h0, p1, h1, qg = turn[1 + 5 * slot:6 + 5 * slot]
-            yield slot, ((turn[0], p0, h0), (turn[0], p1, h1)), qg * TILES
+            yield slot, ((turn[0], p0, h0), (turn[0], p1, h1)), qg
 
     def key_tile(where):
         return jnp.concatenate([kv[pair, par, 0, h] for pair, par, h in where], axis=0)
@@ -320,11 +324,11 @@
             memo[key] = value_tile_t(where) if kind == "v" else key_tile(where) if kind == "k" else key_tile(where).T
         return memo[key]
 
-    def wide(ref, c):
-        return jnp.concatenate([ref[c], ref[c + 1]], axis=1)
-
-    def tall(ref, c):
-        return jnp.concatenate([ref[c], ref[c + 1]], axis=0)
+    def tall(ref, qg, t):
+        return ref[qg, pl.ds(2 * t, 2)].reshape(256, 128)
+
+    def cols_of(t):
+        return pl.ds(t * 256, 256)
 
     def rows(b):
         return pl.ds(b * 256, 256)
@@ -351,45 +355,39 @@
                 top[b] = jnp.max(s.reshape(32, 8, 256), axis=0)
 
     def fwd_scores(turn, some, memo):
-        for slot, where, base in groups(turn, some):
+        for slot, where, qg in groups(turn, some):
             kt = tile_of(memo, slot, "k", where)
             twice = jnp.concatenate([kt, kt], axis=1)
             for t in range(HEADS):
-                b, c = slot * HEADS + t, base + 2 * t
+                b, cols = slot * HEADS + t, cols_of(t)
                 if b in some:
-                    scaled = jnp.concatenate([wide(c_t.at[:, i], c) for i in range(2)], axis=0)
-                    s = jnp.dot(twice, scaled, preferred_element_type=f32)
+                    s = jnp.dot(twice, c_t[qg, :, cols], preferred_element_type=f32)
                     s_buf[b] = s
                     top[b] = jnp.max(s.reshape(32, 8, 256), axis=0)
 
     def fwd_softmax(turn, some):
-        for slot, _, base in groups(turn, some):
+        for slot, _, qg in groups(turn, some):
             for t in range(HEADS):
-                b, c = slot * HEADS + t, base + 2 * t
+                b, cols = slot * HEADS + t, cols_of(t)
                 if b not in some:
                     continue
-                m_old = wide(mst, c)
+                m_old = mst[qg, :, cols]
                 m_new = jnp.maximum(m_old, jnp.max(top[b], axis=0, keepdims=True))
                 p = jnp.exp2(s_buf[b] - m_new[0:1])
                 decay = jnp.exp2(m_old - m_new)
-                l_new = wide(lst, c) * decay + jnp.sum(p.reshape(32, 8, 256), axis=0)
+                lst[qg, :, cols] = lst[qg, :, cols] * decay + jnp.sum(p.reshape(32, 8, 256), axis=0)
                 p_buf[rows(b), :] = p.astype(bf16)
                 dec[b] = decay
-                for j in range(2):
-                    cols = slice(j * 128, j * 128 + 128)
-                    mst[c + j] = m_new[:, cols]
-                    lst[c + j] = l_new[:, cols]
+                mst[qg, :, cols] = m_new
 
     def fwd_out(turn, some, memo):
-        for slot, where, base in groups(turn, some):
+        for slot, where, qg in groups(turn, some):
             vt = tile_of(memo, slot, "v", where)
             for t in range(HEADS):
-                b, c = slot * HEADS + t, base + 2 * t
+                b, cols = slot * HEADS + t, cols_of(t)
                 if b in some:
                     pv = jnp.dot(vt, p_buf[rows(b), :], preferred_element_type=f32)
-                    for j in range(2):
-                        cols = slice(j * 128, j * 128 + 128)
-                        acc[c + j] = acc[c + j] * dec[b, 0:1, cols] + pv[:, cols]
+                    acc[qg, :, cols] = acc[qg, :, cols] * dec[b, 0:1] + pv
 
     def fwd_place(j):
         return place(lookup(jnp.minimum(j, turns - 1), plan.fwd_pairs), jnp.minimum(j, 1))
@@ -397,24 +395,16 @@
     every = range(TILES)
     for act in ag_events(plan.fwd_waits[0]):
         act()
-    old = fwd_place(me * 0)
-    fwd_scores(old, every, {})
-    mask_scores(0, 0)
-    for act in ag_events(plan.fwd_waits[1]):
-        act()
-    cur = fwd_place(me * 0 + 1)
-    memo = {}
-    for b in range(TILES + 1):
-        fwd_scores(cur, (b - 1,), memo)
-        fwd_softmax(old, (b,))
+    first = fwd_place(me * 0)
+    fwd_scores(first, every, {})
 
     def fwd_turn(j, carry):
         old, cur, new = carry
-        branch(j, turns, lambda i: ag_events(plan.fwd_waits[i + 1]) if i else [])
-
-        @pl.when(j == plan.fwd_mate)
+        branch(j, turns, lambda i: ag_events(plan.fwd_waits[i + 1]))
+
+        @pl.when((j == 0) | (j == plan.fwd_mate))
         def _():
-            mask_scores(1, 0)
+            mask_scores(jnp.minimum(j, 1), 0)
 
         after = fwd_place(j + 2)
         memo, memo_old = {}, {}
@@ -424,39 +414,46 @@
             fwd_out(old, (b,), memo_old)
         return cur, new, after
 
-    last = lax.fori_loop(1, turns, fwd_turn, (old, cur, fwd_place(me * 0 + 2)))[0]
-    fwd_out(last, every, {})
+    old, cur, _ = lax.fori_loop(0, turns - 1, fwd_turn, (first, first, fwd_place(me * 0 + 1)))
+    for act in ag_events(plan.fwd_waits[turns]):
+        act()
+    if plan.fwd_mate == turns - 1:
+        mask_scores(1, 0)
+    memo = {}
+    for b in range(TILES + 1):
+        fwd_softmax(cur, (b - 1,))
+        fwd_out(old, (b,), memo)
+    fwd_out(cur, every, {})
 
     def bwd_scores(turn, some, memo):
-        for slot, where, base in groups(turn, some):
+        for slot, where, qg in groups(turn, some):
             for t in range(HEADS):
-                b, c = slot * HEADS + t, base + 2 * t
+                b, cols = slot * HEADS + t, cols_of(t)
                 if b in some:
                     for buf, lhs, kind in ((s_buf, q_s, "t"), (t_buf, g_s, "v")):
-                        buf[b] = jnp.dot(tall(lhs, c), tile_of(memo, slot, kind, where), preferred_element_type=f32)
+                        buf[b] = jnp.dot(tall(lhs, qg, t), tile_of(memo, slot, kind, where), preferred_element_type=f32)
 
     def bwd_softmax(turn, some):
-        for slot, _, base in groups(turn, some):
+        for slot, _, qg in groups(turn, some):
             for t in range(HEADS):
-                b, c = slot * HEADS + t, base + 2 * t
+                b, cols = slot * HEADS + t, cols_of(t)
                 if b in some:
-                    lse, dr = tall(lcol, c), tall(dcol, c)
+                    lse, dr = tall(lcol, qg, t), tall(dcol, qg, t)
                     p = jnp.exp2(s_buf[b] * coef - jnp.concatenate([lse, lse], axis=1))
                     p_buf[rows(b), :] = p.astype(bf16)
                     d_buf[rows(b), :] = (p * (t_buf[b] - jnp.concatenate([dr, dr], axis=1))).astype(bf16)
 
     def bwd_out(turn, some, memo):
-        for slot, where, base in groups(turn, some):
+        for slot, where, qg in groups(turn, some):
             for t in range(HEADS):
-                b, c = slot * HEADS + t, base + 2 * t
+                b, cols = slot * HEADS + t, cols_of(t)
                 if b not in some:
                     continue
                 ds = d_buf[rows(b), :]
                 dq = lax.dot_general(tile_of(memo, slot, "t", where), ds, (((1,), (1,)), ((), ())), preferred_element_type=f32)
-                for j in range(2):
-                    dq_s[c + j] += dq[:, j * 128:j * 128 + 128]
+                dq_s[qg, :, cols] += dq
                 for x, (ref, buf) in enumerate(((q_t, ds), (g_t, p_buf[rows(b), :]))):
-                    grad = jnp.dot(wide(ref, c), buf, preferred_element_type=f32)
+                    grad = jnp.dot(ref[qg, :, cols], buf, preferred_element_type=f32)
                     memo[x] = memo[x] + grad if t else grad
                     for j, (pair, par, h) in enumerate(where if t == HEADS - 1 else ()):
                         value = memo[x][:, j * 128:j * 128 + 128]
@@ -466,47 +463,39 @@
         at = jnp.minimum(j, turns - 1)
         return place(lookup(at, plan.bwd_pairs), 1 - div(at + 1, turns))
 
-    x_m = []
-    for h in range(2):
-        inbox = pl.ds(h * HEADS, HEADS)
-        x_m += [mate_copy(theirs(ref, h), box.at[inbox], 4 + 3 * h + i)
-                for i, (ref, box) in enumerate(((acc, xacc), (mst, xm), (lst, xl)))]
+    x_m = [mate_copy(ref.at[h, :, theirs], box.at[h], 4 + 3 * h + i)
+           for h in range(2) for i, (ref, box) in enumerate(((acc, xacc), (mst, xm), (lst, xl)))]
     for copy in x_m:
         copy.start()
     first = bwd_place(me * 0)
     bwd_scores(first, every, {})
     dq_s[...] = jnp.zeros(dq_s.shape, f32)
-    x_r = [mate_copy(own(ref, h), theirs(ref, h), 10 + 2 * j + h) for j, ref in enumerate((lrow, drow)) for h in range(2)]
+    x_r = [mate_copy(ref.at[h, :, ours], ref.at[h, :, theirs], 10 + 2 * j + h) for j, ref in enumerate((lrow, drow)) for h in range(2)]
 
     for h in range(2):
         for copy in x_m[3 * h:3 * h + 3]:
             copy.wait_recv()
         for head in range(HEADS):
-            c, i = h * TILES + head, h * HEADS + head
-            m1, m2 = mst[c], xm[i]
+            cols = pl.ds(head * PIECE, PIECE)
+            m1, m2 = mst[h, :, cols], xm[h, :, cols]
             m = jnp.maximum(m1, m2)
             w1, w2 = jnp.exp2(m1 - m), jnp.exp2(m2 - m)
-            total = jnp.sum(lst[c] * w1 + xl[i] * w2, axis=0, keepdims=True)
-            out = (acc[c] * w1[0:1] + xacc[i] * w2[0:1]) / total
+            total = jnp.sum(lst[h, :, cols] * w1 + xl[h, :, cols] * w2, axis=0, keepdims=True)
+            out = (acc[h, :, cols] * w1[0:1] + xacc[h, :, cols] * w2[0:1]) / total
             o_s[head, half(h), :] = out.T.astype(bf16)
-            lrow[c] = m + jnp.log2(total)
+            lrow[h, :, cols] = m + jnp.log2(total)
             rounded = out.astype(bf16).astype(f32)
-            drow[c] = jnp.broadcast_to(jnp.sum(rounded * g_t[c].astype(f32), axis=0, keepdims=True), (8, 128))
+            d = jnp.sum(rounded * g_t[h, :, cols].astype(f32), axis=0, keepdims=True)
+            drow[h, :, cols] = jnp.broadcast_to(d, (8, 128))
         for copy in x_r[h::2]:
             copy.start()
     stores = [pltpu.make_async_copy(o_s, o_ref, io.at[8])]
     stores[0].start()
 
-    def columns(c):
-        lcol[c] = jnp.broadcast_to(lrow[c, 0:1], (128, 128)).T
-        dcol[c] = jnp.broadcast_to(drow[c, 0:1], (128, 128)).T
-
-    for h in range(2):
-        pl.loop(h * TILES, h * TILES + HEADS)(columns)
-    for copy in x_r:
-        copy.wait_recv()
-    for h in range(2):
-        pl.loop(h * TILES + HEADS, h * TILES + TILES)(columns)
+    def columns(h, i):
+        cols = pl.ds(i * 128, 128)
+        for row, col in ((lrow, lcol), (drow, dcol)):
+            col[h, i] = jnp.broadcast_to(row[h, 0:1, cols], (128, 128)).T
 
     def rs_add(r, k, x):
         rs_copy(k, x).wait_recv()
@@ -521,24 +510,35 @@
         for i in range(4):
             stg[pair, i // 2, i % 2, 1] = jnp.zeros((128, 128), f32)
 
-    def bwd_start(j, carry):
-        _, cur, new = carry
-        if turns < 4:
-            mask_scores(turns - 1 - j, 1)
-        after = bwd_place(j + 2)
-        memo = {}
-        for b in range(TILES + 1):
-            bwd_softmax(cur, (b,))
-            bwd_scores(new, (b - 1,), memo)
-
-        @pl.when(j == 0)
-        def _():
-            clear(cur[0])
-            bwd_out(cur, every, {})
-            for act in rs_events(plan.bwd_sends[0]):
-                act()
-
-        return cur, new, after
+    for i in range(TILES):
+        columns(i // HEADS, i % HEADS)
+    if turns < 4:
+        mask_scores(turns - 1, 1)
+    second, third = bwd_place(me * 0 + 1), bwd_place(me * 0 + 2)
+    memo = {}
+    early = [b for b in every if b % HEADS < HEADS // 2]
+    for b in early:
+        bwd_softmax(first, (b,))
+        bwd_scores(second, (b,), memo)
+    for copy in x_r:
+        copy.wait_recv()
+    for i in range(TILES):
+        columns(i // HEADS, HEADS + i % HEADS)
+    memo = {}
+    for b in every:
+        if b not in early:
+            bwd_softmax(first, (b,))
+            bwd_scores(second, (b,), memo)
+    clear(first[0])
+    bwd_out(first, every, {})
+    for act in rs_events(plan.bwd_sends[0]):
+        act()
+    if turns < 4:
+        mask_scores(turns - 2, 1)
+    memo = {}
+    for b in range(TILES + 1):
+        bwd_softmax(second, (b,))
+        bwd_scores(third, (b - 1,), memo)
 
     def bwd_turn(j, carry):
         old, cur, new = carry
@@ -560,13 +560,12 @@
             bwd_scores(new, (b - 2,), memo)
         return cur, new, after
 
-    start = lax.fori_loop(0, 2, bwd_start, (first, first, bwd_place(me * 0 + 1)))
-    last = lax.fori_loop(2, turns, bwd_turn, start)[0]
+    last = lax.fori_loop(2, turns, bwd_turn, (second, third, bwd_place(me * 0 + 3)))[0]
     for act in rs_events(plan.bwd_sends[turns - 1]):
         act()
     bwd_out(last, every, {})
 
-    x_d = [mate_copy(theirs(dq_s, h), xdq.at[pl.ds(h * HEADS, HEADS)], 14 + h) for h in range(2)]
+    x_d = [mate_copy(dq_s.at[h, :, theirs], xdq.at[h], 14 + h) for h in range(2)]
     for copy in x_d:
         copy.start()
     for unit in plan.bwd_sends[turns]:
@@ -575,7 +574,8 @@
     for h in range(2):
         x_d[h].wait_recv()
         for head in range(HEADS):
-            total = (dq_s[h * TILES + head] + xdq[h * HEADS + head]) * SCALE
+            cols = pl.ds(head * PIECE, PIECE)
+            total = (dq_s[h, :, cols] + xdq[h, :, cols]) * SCALE
             dq_o[head, half(h), :] = total.T.astype(bf16)
     stores.append(pltpu.make_async_copy(dq_o, dq_ref, io.at[9]))
     stores[1].start()
@@ -627,7 +627,8 @@
         big = jax.ShapeDtypeStruct((HEADS, tokens, HD), bf16)
         small = jax.ShapeDtypeStruct((tokens, HD), bf16)
         anywhere = pl.BlockSpec(memory_space=pl.ANY)
-        twenty, ten, stat, few = (2 * TILES,) + tile, (TILES,) + tile, (2 * TILES, 8, 128), (TILES, 8, 128)
+        rows, wide, half_wide = (2, TILES) + tile, (2, HD, 2 * SPAN), (2, HD, SPAN)
+        stat, few = (2, 8, 2 * SPAN), (2, 8, SPAN)
         results = pl.pallas_call(
             functools.partial(kernel, plan),
             out_shape=(big, big, small, small),
@@ -637,11 +638,10 @@
                 vm((n // 2, 2, 2, 2) + tile, bf16), vm((n // 2, 2, 2, 2) + tile, f32), vm((n, 2, 2) + tile, f32),
                 vm((TILES, 256, 256), f32), vm((TILES, 256, 256), f32), vm((TILES * 256, 256), bf16), vm((TILES * 256, 256), bf16),
                 vm((TILES, 8, 256), f32),
-                vm(twenty, bf16), vm(twenty, bf16), vm((2,) + tile, bf16), vm(twenty, bf16), vm(twenty, bf16),
-                vm((2 * TILES, 2) + tile, bf16),
-                vm(twenty, f32), vm(stat, f32), vm(stat, f32), vm((TILES, 8, 256), f32),
-                vm(ten, f32), vm(few, f32), vm(few, f32), vm(stat, f32), vm(stat, f32), vm(twenty, f32), vm(twenty, f32),
-                vm(twenty, f32), vm(ten, f32),
+                vm(rows, bf16), vm(rows, bf16), vm((2,) + tile, bf16), vm(wide, bf16), vm(wide, bf16), vm((2, 2 * HD, 2 * SPAN), bf16),
+                vm(wide, f32), vm(stat, f32), vm(stat, f32), vm((TILES, 8, 256), f32),
+                vm(half_wide, f32), vm(few, f32), vm(few, f32), vm(stat, f32), vm(stat, f32), vm(rows, f32), vm(rows, f32),
+                vm(wide, f32), vm(half_wide, f32),
                 vm(big.shape, bf16), vm(big.shape, bf16), vm(small.shape, bf16), vm(small.shape, bf16),
                 sem((n, 2)), sem((n, 2)), sem((n, 2)), sem((n, 2)), sem((16,)), sem((16,)), sem((12,)),
             ],

time: 124 us -> 121 us (0.976)
  Pallas kernels: 123 us -> 120 us
    pallas_call x1, Pallas kernels: 121 us -> 118 us  [local(): pl.pallas_call(functools.partial(kernel, plan), out_shape=(big, big, smal...]
where the time goes in v7:
time: 121 us
  Pallas kernels  120 us (99%)
    pallas_call x1, Pallas kernels, local(): pl.pallas_call(functools.partial(kernel, plan), out_shape=(big, big, smal...  118 us

profile of v7, /device:TPU:0, one launch (start us, length us, event | category | flops | bytes accessed | tf_op | source)
XLA Modules:
  0.0 121.0 jit_solution(8113265643203490250)
XLA Ops:
  0.6 118.3 %shard_map.75 = (bf16[5,256,128]{2,1,0:T(8,128)(2,1)}, bf16[5,256,128]{2,1,0:T(8,128)(2,1)}, bf16[256,128]{1,0:T(8,128)(2,1)}, bf16[256,128]{1,0:T(8,128)(2,1)}) custom-call(bf16[5,256,128]{2,1,0:T(8,128)(2,1)} %bitcast.16, bf16[256,128]{1,0:T(8,128)(2,1)} %bitcast.20, bf16[256,128]{1,0:T(8,128)(2,1)} %bitcast.21, bf16[5,256,128]{2,1,0:T(8,128)(2,1)} %bitcast.17), custom_call_target="tpu_custom_call" | custom-call | flops 18790481920 | bytes 4194304 | tf_op jit(solution)/shard_map/pallas_call | solution.py:632
  118.9 1.9 %shard_map.76 = (bf16[5,256,128]{2,1,0:T(8,128)(2,1)}, bf16[5,256,128]{2,1,0:T(8,128)(2,1)}, bf16[256,128]{1,0:T(8,128)(2,1)}, bf16[256,128]{1,0:T(8,128)(2,1)}) custom-call(bf16[5,256,128]{2,1,0:T(8,128)(2,1)} %get-tuple-element.12.refs_0_, bf16[5,256,128]{2,1,0:T(8,128)(2,1)} %get-tuple-element.13.refs_1_, bf16[256,128]{1,0:T(8,128)(2,1)} %get-tuple-element.14.refs_2_, ...), custom_call_target="tpu_custom_call" | custom-call | flops 1048576 | bytes 2097152 | tf_op jit(solution)/shard_map/pallas_call | solution.py:651

commit v8 on v7

--- a/solution.py
+++ b/solution.py
@@ -215,8 +215,8 @@
 
     loads = []
     for h in range(2):
-        loads += [pltpu.make_async_copy(v_ref.at[half(h)], v_s.at[h], io.at[h]),
-                  pltpu.make_async_copy(k_ref.at[half(h)], kv.at[0, 0, 0, h], io.at[2 + h])]
+        loads += [pltpu.make_async_copy(k_ref.at[half(h)], kv.at[0, 0, 0, h], io.at[h]),
+                  pltpu.make_async_copy(v_ref.at[half(h)], v_s.at[h], io.at[2 + h])]
     for h in range(2):
         for j, (src, dst) in enumerate(((q_ref, q_s), (g_ref, g_s))):
             loads.append(pltpu.make_async_copy(src.at[:, half(h)], dst.at[h, pl.ds(0, HEADS)], io.at[4 + 2 * j + h]))
@@ -423,7 +423,8 @@
     for b in range(TILES + 1):
         fwd_softmax(cur, (b - 1,))
         fwd_out(old, (b,), memo)
-    fwd_out(cur, every, {})
+    late = [b for b in every if b % HEADS < HEADS // 2]
+    fwd_out(cur, [b for b in every if b not in late], {})
 
     def bwd_scores(turn, some, memo):
         for slot, where, qg in groups(turn, some):
@@ -443,16 +444,17 @@
                     p_buf[rows(b), :] = p.astype(bf16)
                     d_buf[rows(b), :] = (p * (t_buf[b] - jnp.concatenate([dr, dr], axis=1))).astype(bf16)
 
-    def bwd_out(turn, some, memo):
+    def bwd_out(turn, some, memo, parts=(True, True)):
         for slot, where, qg in groups(turn, some):
             for t in range(HEADS):
                 b, cols = slot * HEADS + t, cols_of(t)
                 if b not in some:
                     continue
                 ds = d_buf[rows(b), :]
-                dq = lax.dot_general(tile_of(memo, slot, "t", where), ds, (((1,), (1,)), ((), ())), preferred_element_type=f32)
-                dq_s[qg, :, cols] += dq
-                for x, (ref, buf) in enumerate(((q_t, ds), (g_t, p_buf[rows(b), :]))):
+                if parts[1]:
+                    dq_s[qg, :, cols] += lax.dot_general(tile_of(memo, slot, "t", where), ds, (((1,), (1,)), ((), ())),
+                                                         preferred_element_type=f32)
+                for x, (ref, buf) in enumerate(((q_t, ds), (g_t, p_buf[rows(b), :])) if parts[0] else ()):
                     grad = jnp.dot(ref[qg, :, cols], buf, preferred_element_type=f32)
                     memo[x] = memo[x] + grad if t else grad
                     for j, (pair, par, h) in enumerate(where if t == HEADS - 1 else ()):
@@ -467,8 +469,12 @@
            for h in range(2) for i, (ref, box) in enumerate(((acc, xacc), (mst, xm), (lst, xl)))]
     for copy in x_m:
         copy.start()
+    fwd_out(cur, late, {})
     first = bwd_place(me * 0)
     bwd_scores(first, every, {})
+    for k in range(1, plan.blocks):
+        for x in range(2):
+            ag_copy(k, x).wait_send()
     dq_s[...] = jnp.zeros(dq_s.shape, f32)
     x_r = [mate_copy(ref.at[h, :, ours], ref.at[h, :, theirs], 10 + 2 * j + h) for j, ref in enumerate((lrow, drow)) for h in range(2)]
 
@@ -516,8 +522,7 @@
         mask_scores(turns - 1, 1)
     second, third = bwd_place(me * 0 + 1), bwd_place(me * 0 + 2)
     memo = {}
-    early = [b for b in every if b % HEADS < HEADS // 2]
-    for b in early:
+    for b in late:
         bwd_softmax(first, (b,))
         bwd_scores(second, (b,), memo)
     for copy in x_r:
@@ -526,13 +531,14 @@
         columns(i // HEADS, HEADS + i % HEADS)
     memo = {}
     for b in every:
-        if b not in early:
+        if b not in late:
             bwd_softmax(first, (b,))
             bwd_scores(second, (b,), memo)
     clear(first[0])
-    bwd_out(first, every, {})
+    bwd_out(first, every, {}, (True, False))
     for act in rs_events(plan.bwd_sends[0]):
         act()
+    bwd_out(first, every, {}, (False, True))
     if turns < 4:
         mask_scores(turns - 2, 1)
     memo = {}
@@ -579,20 +585,22 @@
             dq_o[head, half(h), :] = total.T.astype(bf16)
     stores.append(pltpu.make_async_copy(dq_o, dq_ref, io.at[9]))
     stores[1].start()
-    for k, x in plan.bwd_last:
-        rs_add(0, k, x)
-    for x, (buf, ref, factor) in enumerate(((dk_o, dk_ref, SCALE), (dv_o, dv_ref, 1.0))):
-        for h in range(2):
-            buf[half(h), :] = (stg[0, 0, x, h] * factor).T.astype(bf16)
-        stores.append(pltpu.make_async_copy(buf, ref, io.at[10 + x]))
-        stores[-1].start()
-
     for k in range(1, plan.blocks):
         for x in range(2):
-            ag_copy(k, x).wait_send()
             rs_copy(k, x).wait_send()
     for copy in x_q + x_m + x_r + x_d:
         copy.wait_send()
+    left = [dims, dims]
+    for k, x in plan.bwd_last:
+        rs_add(0, k, x)
+        left[x] -= 1
+        if not left[x]:
+            buf, ref, factor = ((dk_o, dk_ref, SCALE), (dv_o, dv_ref, 1.0))[x]
+            for h in range(2):
+                buf[half(h), :] = (stg[0, 0, x, h] * factor).T.astype(bf16)
+            stores.append(pltpu.make_async_copy(buf, ref, io.at[10 + x]))
+            stores[-1].start()
+
     for copy in stores:
         copy.wait()
 

time: 121 us -> 121 us (level)
  no operation moved by 1% of the time
where the time goes in v8:
time: 121 us
  Pallas kernels  120 us (99%)
    pallas_call x1, Pallas kernels, local(): pl.pallas_call(functools.partial(kernel, plan), out_shape=(big, big, smal...  118 us

profile of v8, /device:TPU:0, one launch (start us, length us, event | category | flops | bytes accessed | tf_op | source)
XLA Modules:
  0.0 121.0 jit_solution(9768825842449433639)
XLA Ops:
  0.6 118.3 %shard_map.75 = (bf16[5,256,128]{2,1,0:T(8,128)(2,1)}, bf16[5,256,128]{2,1,0:T(8,128)(2,1)}, bf16[256,128]{1,0:T(8,128)(2,1)}, bf16[256,128]{1,0:T(8,128)(2,1)}) custom-call(bf16[5,256,128]{2,1,0:T(8,128)(2,1)} %bitcast.16, bf16[256,128]{1,0:T(8,128)(2,1)} %bitcast.20, bf16[256,128]{1,0:T(8,128)(2,1)} %bitcast.21, bf16[5,256,128]{2,1,0:T(8,128)(2,1)} %bitcast.17), custom_call_target="tpu_custom_call" | custom-call | flops 18790481920 | bytes 4194304 | tf_op jit(solution)/shard_map/pallas_call | solution.py:640
  118.9 1.9 %shard_map.76 = (bf16[5,256,128]{2,1,0:T(8,128)(2,1)}, bf16[5,256,128]{2,1,0:T(8,128)(2,1)}, bf16[256,128]{1,0:T(8,128)(2,1)}, bf16[256,128]{1,0:T(8,128)(2,1)}) custom-call(bf16[5,256,128]{2,1,0:T(8,128)(2,1)} %get-tuple-element.12.refs_0_, bf16[5,256,128]{2,1,0:T(8,128)(2,1)} %get-tuple-element.13.refs_1_, bf16[256,128]{1,0:T(8,128)(2,1)} %get-tuple-element.14.refs_2_, ...), custom_call_target="tpu_custom_call" | custom-call | flops 1048576 | bytes 2097152 | tf_op jit(solution)/shard_map/pallas_call | solution.py:659

commit v9 on v8

--- a/solution.py
+++ b/solution.py
@@ -20,9 +20,9 @@
 
 KEY_TREE = "011222133332330444044204331303450512252553132154554251534405024"
 VALUE_TREE = "011202133303032404124114441201150505210501022525540551434312353"
-DK_TREE = "010222133132320404040144013222455152212303525124550544534132251"
-DV_TREE = "011221233112332404420104340431355155511535030505014404035353440"
-BWD_ORDER = "vuntrfmplsj7beodk6cq35haig98241"
+DK_TREE = "011202230302020401042203040443255115012501525315014524043545435"
+DV_TREE = "011221233332313444144214343331155555212333535104510402554435224"
+BWD_ORDER = "vtfrsnmud7qjklp3cobe9ai6h45g128"
 
 
 def popcount(value):
@@ -101,7 +101,7 @@
         self.fwd_pairs = order
         self.fwd_mate = max(i for i, pair in enumerate(order) if pair == 0)
 
-    def backward(self, unit_us=2.9, hop_us=2.1, turn_us=1.55, add_us=0.035):
+    def backward(self, unit_us=2.9, hop_us=2.1, turn_us=1.6, add_us=0.025):
         if self.dims == 6:
             order = [int(c, 32) for c in BWD_ORDER]
         else:
@@ -110,7 +110,7 @@
         free = [0.0] * self.dims
         due = {}
         waiting, sends, steps = set(), [], []
-        now = 1.57
+        now = 1.65
 
         def kids(unit):
             return [(k, unit[1]) for k in self.bwd[unit[1]].kids[unit[0]]]
@@ -129,20 +129,23 @@
                     sends.append(unit)
 
         for i, pair in enumerate(order):
-            waiting |= {(r, x) for r in (2 * pair, 2 * pair + 1) for x in range(2) if r} if i < len(order) - 1 else set()
-            flush()
-            steps.append(sends)
-            sends = []
-            if i == 0:
-                now += 0.85
+            if i:
+                now += 0.12
                 flush()
                 steps.append(sends)
                 sends = []
-            now += turn_us if i < len(order) - 1 else 0.0
+                now += turn_us
+            waiting |= {(r, x) for r in (2 * pair, 2 * pair + 1) for x in range(2) if r} if i < len(order) - 1 else set()
+            if not i:
+                flush()
+                steps.append(sends)
+                sends = []
+                now += 0.9
+        flush()
         while waiting:
             now = max(now, min(max(due.get(k, 1e9) for k in kids(u)) for u in waiting))
             flush()
-        self.bwd_sends = steps[:-1] + [steps[-1] + sends]
+        self.bwd_sends = steps + [sends]
         self.bwd_pairs = order
         self.bwd_last = sorted((u for x in range(2) for u in kids((0, x))), key=lambda u: due[u])
 
@@ -186,8 +189,8 @@
 
 
 def kernel(plan, q_ref, k_ref, v_ref, g_ref, o_ref, dq_ref, dk_ref, dv_ref,
-           kv, stg, land, s_buf, t_buf, p_buf, d_buf, top, q_s, g_s, v_s, q_t, g_t, c_t, acc, mst, lst, dec,
-           xacc, xm, xl, lrow, drow, lcol, dcol, dq_s, xdq, o_s, dq_o, dk_o, dv_o,
+           kv, kt_s, stg, land, s_buf, t_buf, p_buf, d_buf, top, q_s, g_s, v_s, q_t, g_t, c_t, acc, mst, lst, dec,
+           xacc, xm, xl, lrow, drow, lcol, dcol, o_s, dq_o, dk_o, dv_o,
            ag_send, ag_recv, rs_send, rs_recv, x_send, x_recv, io):
     dims, turns = plan.dims, plan.turns
     pieces = 4 * plan.blocks
@@ -243,7 +246,7 @@
 
     def rs_copy(r, x):
         return pltpu.make_async_remote_copy(
-            src_ref=stg.at[r >> 1, r & 1, x], dst_ref=land.at[r, x], send_sem=rs_send.at[r, x], recv_sem=rs_recv.at[r, x],
+            src_ref=stg.at[r >> 1, r & 1, x], dst_ref=land.at[r - 1, x], send_sem=rs_send.at[r, x], recv_sem=rs_recv.at[r, x],
             device_id={"ctx": nbr[plan.bwd[x].link[r]]}, device_id_type=MESH)
 
     def mate_copy(src, dst, sem):
@@ -318,10 +321,13 @@
     def value_tile_t(where):
         return jnp.concatenate([kv[pair, par, 1, h] for pair, par, h in where], axis=1)
 
+    def key_tile_t(where):
+        return jnp.concatenate([kt_s[pair, par, h] for pair, par, h in where], axis=1)
+
     def tile_of(memo, slot, kind, where):
         key = (kind, slot)
         if key not in memo:
-            memo[key] = value_tile_t(where) if kind == "v" else key_tile(where) if kind == "k" else key_tile(where).T
+            memo[key] = value_tile_t(where) if kind == "v" else key_tile(where) if kind == "k" else key_tile_t(where)
         return memo[key]
 
     def tall(ref, qg, t):
@@ -361,6 +367,9 @@
             for t in range(HEADS):
                 b, cols = slot * HEADS + t, cols_of(t)
                 if b in some:
+                    if t == 0:
+                        for pair, par, h in where:
+                            kt_s[pair, par, h] = kv[pair, par, 0, h].T
                     s = jnp.dot(twice, c_t[qg, :, cols], preferred_element_type=f32)
                     s_buf[b] = s
                     top[b] = jnp.max(s.reshape(32, 8, 256), axis=0)
@@ -452,12 +461,16 @@
                     continue
                 ds = d_buf[rows(b), :]
                 if parts[1]:
-                    dq_s[qg, :, cols] += lax.dot_general(tile_of(memo, slot, "t", where), ds, (((1,), (1,)), ((), ())),
+                    acc[qg, :, cols] += lax.dot_general(tile_of(memo, slot, "t", where), ds, (((1,), (1,)), ((), ())),
                                                          preferred_element_type=f32)
                 for x, (ref, buf) in enumerate(((q_t, ds), (g_t, p_buf[rows(b), :])) if parts[0] else ()):
                     grad = jnp.dot(ref[qg, :, cols], buf, preferred_element_type=f32)
                     memo[x] = memo[x] + grad if t else grad
-                    for j, (pair, par, h) in enumerate(where if t == HEADS - 1 else ()):
+                    if t < HEADS - 1:
+                        continue
+                    for pair, par, _ in () if slot else where:
+                        stg[pair, par, x, 1] = jnp.zeros((128, 128), f32)
+                    for j, (pair, par, h) in enumerate(where):
                         value = memo[x][:, j * 128:j * 128 + 128]
                         stg[pair, par, x, h] = value + stg[pair, par, x, h] if slot else value
 
@@ -475,7 +488,6 @@
     for k in range(1, plan.blocks):
         for x in range(2):
             ag_copy(k, x).wait_send()
-    dq_s[...] = jnp.zeros(dq_s.shape, f32)
     x_r = [mate_copy(ref.at[h, :, ours], ref.at[h, :, theirs], 10 + 2 * j + h) for j, ref in enumerate((lrow, drow)) for h in range(2)]
 
     for h in range(2):
@@ -495,6 +507,9 @@
             drow[h, :, cols] = jnp.broadcast_to(d, (8, 128))
         for copy in x_r[h::2]:
             copy.start()
+    for copy in x_m:
+        copy.wait_send()
+    acc[...] = jnp.zeros(acc.shape, f32)
     stores = [pltpu.make_async_copy(o_s, o_ref, io.at[8])]
     stores[0].start()
 
@@ -503,18 +518,18 @@
         for row, col in ((lrow, lcol), (drow, dcol)):
             col[h, i] = jnp.broadcast_to(row[h, 0:1, cols], (128, 128)).T
 
-    def rs_add(r, k, x):
-        rs_copy(k, x).wait_recv()
+    def rs_sum(r, x, kids):
+        for k in kids:
+            rs_copy(k, x).wait_recv()
         for h in range(2):
-            stg[r >> 1, r & 1, x, h] += land[k, x, h]
+            total = stg[r >> 1, r & 1, x, h]
+            for k in kids:
+                total = total + land[k - 1, x, h]
+            stg[r >> 1, r & 1, x, h] = total
 
     def rs_events(sends):
-        return ([functools.partial(rs_add, r, k, x) for r, x in sends for k in plan.bwd[x].kids[r]]
+        return ([functools.partial(rs_sum, r, x, plan.bwd[x].kids[r]) for r, x in sends if plan.bwd[x].kids[r]]
                 + [rs_copy(r, x).start for r, x in sends])
-
-    def clear(pair):
-        for i in range(4):
-            stg[pair, i // 2, i % 2, 1] = jnp.zeros((128, 128), f32)
 
     for i in range(TILES):
         columns(i // HEADS, i % HEADS)
@@ -534,7 +549,6 @@
         if b not in late:
             bwd_softmax(first, (b,))
             bwd_scores(second, (b,), memo)
-    clear(first[0])
     bwd_out(first, every, {}, (True, False))
     for act in rs_events(plan.bwd_sends[0]):
         act()
@@ -550,10 +564,6 @@
         old, cur, new = carry
         branch(j, turns, lambda i: rs_events(plan.bwd_sends[i - 1]) if i > 1 else [])
 
-        @pl.when(j < turns - 1)
-        def _():
-            clear(old[0])
-
         @pl.when(j >= turns - 2)
         def _():
             mask_scores(turns - 1 - j, 1)
@@ -561,9 +571,10 @@
         after = bwd_place(j + 2)
         memo, memo_old = {}, {}
         for b in range(TILES + 2):
-            bwd_out(old, (b,), memo_old)
+            bwd_scores(new, (b - 2,), memo)
+            bwd_out(old, (b - 1,), memo_old, (False, True))
+            bwd_out(old, (b,), memo_old, (True, False))
             bwd_softmax(cur, (b - 1,))
-            bwd_scores(new, (b - 2,), memo)
         return cur, new, after
 
     last = lax.fori_loop(2, turns, bwd_turn, (second, third, bwd_place(me * 0 + 3)))[0]
@@ -571,7 +582,7 @@
         act()
     bwd_out(last, every, {})
 
-    x_d = [mate_copy(dq_s.at[h, :, theirs], xdq.at[h], 14 + h) for h in range(2)]
+    x_d = [mate_copy(acc.at[h, :, theirs], xacc.at[h], 14 + h) for h in range(2)]
     for copy in x_d:
         copy.start()
     for unit in plan.bwd_sends[turns]:
@@ -581,18 +592,18 @@
         x_d[h].wait_recv()
         for head in range(HEADS):
             cols = pl.ds(head * PIECE, PIECE)
-            total = (dq_s[h, :, cols] + xdq[h, :, cols]) * SCALE
+            total = (acc[h, :, cols] + xacc[h, :, cols]) * SCALE
             dq_o[head, half(h), :] = total.T.astype(bf16)
     stores.append(pltpu.make_async_copy(dq_o, dq_ref, io.at[9]))
     stores[1].start()
     for k in range(1, plan.blocks):
         for x in range(2):
             rs_copy(k, x).wait_send()
-    for copy in x_q + x_m + x_r + x_d:
+    for copy in x_q + x_r + x_d:
         copy.wait_send()
     left = [dims, dims]
     for k, x in plan.bwd_last:
-        rs_add(0, k, x)
+        rs_sum(0, x, [k])
         left[x] -= 1
         if not left[x]:
             buf, ref, factor = ((dk_o, dk_ref, SCALE), (dv_o, dv_ref, 1.0))[x]
@@ -643,13 +654,12 @@
             in_specs=[anywhere] * 4,
             out_specs=(anywhere,) * 4,
             scratch_shapes=[
-                vm((n // 2, 2, 2, 2) + tile, bf16), vm((n // 2, 2, 2, 2) + tile, f32), vm((n, 2, 2) + tile, f32),
+                vm((n // 2, 2, 2, 2) + tile, bf16), vm((n // 2, 2, 2) + tile, bf16), vm((n // 2, 2, 2, 2) + tile, f32), vm((n - 1, 2, 2) + tile, f32),
                 vm((TILES, 256, 256), f32), vm((TILES, 256, 256), f32), vm((TILES * 256, 256), bf16), vm((TILES * 256, 256), bf16),
                 vm((TILES, 8, 256), f32),
                 vm(rows, bf16), vm(rows, bf16), vm((2,) + tile, bf16), vm(wide, bf16), vm(wide, bf16), vm((2, 2 * HD, 2 * SPAN), bf16),
                 vm(wide, f32), vm(stat, f32), vm(stat, f32), vm((TILES, 8, 256), f32),
                 vm(half_wide, f32), vm(few, f32), vm(few, f32), vm(stat, f32), vm(stat, f32), vm(rows, f32), vm(rows, f32),
-                vm(wide, f32), vm(half_wide, f32),
                 vm(big.shape, bf16), vm(big.shape, bf16), vm(small.shape, bf16), vm(small.shape, bf16),
                 sem((n, 2)), sem((n, 2)), sem((n, 2)), sem((n, 2)), sem((16,)), sem((16,)), sem((12,)),
             ],

time: 121 us -> 121 us (level)
  no operation moved by 1% of the time
where the time goes in v9:
time: 121 us
  Pallas kernels  120 us (99%)
    pallas_call x1, Pallas kernels, local(): pl.pallas_call(functools.partial(kernel, plan), out_shape=(big, big, smal...  118 us

profile of v9, /device:TPU:0, one launch (start us, length us, event | category | flops | bytes accessed | tf_op | source)
XLA Modules:
  0.0 120.7 jit_solution(9342639502002518258)
XLA Ops:
  0.6 118.0 %shard_map.75 = (bf16[5,256,128]{2,1,0:T(8,128)(2,1)}, bf16[5,256,128]{2,1,0:T(8,128)(2,1)}, bf16[256,128]{1,0:T(8,128)(2,1)}, bf16[256,128]{1,0:T(8,128)(2,1)}) custom-call(bf16[5,256,128]{2,1,0:T(8,128)(2,1)} %bitcast.16, bf16[256,128]{1,0:T(8,128)(2,1)} %bitcast.20, bf16[256,128]{1,0:T(8,128)(2,1)} %bitcast.21, bf16[5,256,128]{2,1,0:T(8,128)(2,1)} %bitcast.17), custom_call_target="tpu_custom_call" | custom-call | flops 18790481920 | bytes 4194304 | tf_op jit(solution)/shard_map/pallas_call | solution.py:651
  118.6 1.9 %shard_map.76 = (bf16[5,256,128]{2,1,0:T(8,128)(2,1)}, bf16[5,256,128]{2,1,0:T(8,128)(2,1)}, bf16[256,128]{1,0:T(8,128)(2,1)}, bf16[256,128]{1,0:T(8,128)(2,1)}) custom-call(bf16[5,256,128]{2,1,0:T(8,128)(2,1)} %get-tuple-element.12.refs_0_, bf16[5,256,128]{2,1,0:T(8,128)(2,1)} %get-tuple-element.13.refs_1_, bf16[256,128]{1,0:T(8,128)(2,1)} %get-tuple-element.14.refs_2_, ...), custom_call_target="tpu_custom_call" | custom-call | flops 1048576 | bytes 2097152 | tf_op jit(solution)/shard_map/pallas_call | solution.py:669

commit v10 on v9

--- a/solution.py
+++ b/solution.py
@@ -58,12 +58,15 @@
         self.forward()
         self.backward()
 
-    def forward(self, unit_us=1.41, hop_us=1.9, turn_us=0.78):
+    def forward(self, unit_us=1.45, hop_us=2.0, single_us=0.92, double_us=0.83):
+        bodies = self.turns - 1
+        self.singles = bodies if bodies < 4 else 2 + bodies % 2
+        self.doubles = (bodies - self.singles) // 2
         free = [0.0] * self.dims
         due = {}
         done = {(0, 0), (0, 1)}
-        now = 1.0
         steps, waits, ready, order = [], [], [0], []
+        now = 0.0
 
         def send(r, x):
             for k in self.fwd[x].kids[r]:
@@ -71,33 +74,31 @@
                 free[d] = max(free[d], now) + unit_us
                 due[k, x] = free[d] + hop_us
 
-        now = 0.0
         send(0, 0)
         send(0, 1)
         now = 1.0
-        while True:
-            for unit in sorted((u for u in due if u not in done and due[u] <= now), key=lambda u: (due[u], u)):
-                done.add(unit)
-                now += 0.02
-                send(*unit)
-                waits.append(unit)
-                if unit[1] == 0 and (unit[0] ^ 1, 0) in done:
-                    ready.append(unit[0] >> 1)
-            turn = len(steps)
-            late = order[max(turn - 2, 0):turn - 1] if turn < self.turns else order[turn - 2:]
-            lacking = [r for pair in late for r in (2 * pair, 2 * pair + 1) if (r, 1) not in done]
-            if turn == 2 < self.turns:
-                lacking = []
-            if lacking or not (ready or turn == self.turns):
+        for group in [1] * (1 + self.singles) + [2] * self.doubles + [0]:
+            while True:
+                for unit in sorted((u for u in due if u not in done and due[u] <= now), key=lambda u: (due[u], u)):
+                    done.add(unit)
+                    now += 0.02
+                    send(*unit)
+                    waits.append(unit)
+                    if unit[1] == 0 and (unit[0] ^ 1, 0) in done:
+                        ready.append(unit[0] >> 1)
+                i = len(order)
+                outs = order[max(i - 2, 0):i - 2 + group] if group else order[i - 2:]
+                skip = i == 2 < self.turns
+                lacking = [r for pair in (() if skip else outs) for r in (2 * pair, 2 * pair + 1) if (r, 1) not in done]
+                if not lacking and len(ready) >= group:
+                    break
                 now = max(now, min(due[u] for u in due if u not in done))
-                continue
-            if turn == self.turns:
-                break
-            order.append(ready.pop(0))
             steps.append(waits)
             waits = []
-            now += turn_us if turn else 0.0
-        self.fwd_waits = steps + [waits]
+            for _ in range(group):
+                order.append(ready.pop(0))
+                now += 0.0 if len(order) == 1 else double_us if group > 1 else single_us
+        self.fwd_waits = steps
         self.fwd_pairs = order
         self.fwd_mate = max(i for i, pair in enumerate(order) if pair == 0)
 
@@ -406,25 +407,46 @@
         act()
     first = fwd_place(me * 0)
     fwd_scores(first, every, {})
+    singles, doubles = plan.singles, plan.doubles
+
+    def fwd_body(line):
+        count = len(line) - 2
+        memos = [{} for _ in line], [{} for _ in line]
+        for b in range(count * TILES + 2):
+            for lag, stage in ((2, 2), (1, 1), (0, 0)):
+                i, tile = (b - lag) // TILES, (b - lag) % TILES
+                if not 0 <= i < count:
+                    continue
+                if stage == 2:
+                    fwd_scores(line[i + 2], (tile,), memos[0][i])
+                elif stage == 1:
+                    fwd_softmax(line[i + 1], (tile,))
+                else:
+                    fwd_out(line[i], (tile,), memos[1][i])
 
     def fwd_turn(j, carry):
         old, cur, new = carry
-        branch(j, turns, lambda i: ag_events(plan.fwd_waits[i + 1]))
+        branch(j, singles, lambda i: ag_events(plan.fwd_waits[i + 1]))
 
         @pl.when((j == 0) | (j == plan.fwd_mate))
         def _():
             mask_scores(jnp.minimum(j, 1), 0)
 
         after = fwd_place(j + 2)
-        memo, memo_old = {}, {}
-        for b in range(TILES + 2):
-            fwd_scores(new, (b - 2,), memo)
-            fwd_softmax(cur, (b - 1,))
-            fwd_out(old, (b,), memo_old)
+        fwd_body((old, cur, new))
         return cur, new, after
 
-    old, cur, _ = lax.fori_loop(0, turns - 1, fwd_turn, (first, first, fwd_place(me * 0 + 1)))
-    for act in ag_events(plan.fwd_waits[turns]):
+    def fwd_double(i, carry):
+        old, cur, new, then = carry
+        branch(i, doubles, lambda i: ag_events(plan.fwd_waits[singles + 1 + i]))
+        after = fwd_place(singles + 2 * i + 3), fwd_place(singles + 2 * i + 4)
+        fwd_body((old, cur, new, then))
+        return (new, then) + after
+
+    old, cur, new = lax.fori_loop(0, singles, fwd_turn, (first, first, fwd_place(me * 0 + 1)))
+    if doubles:
+        old, cur, _, _ = lax.fori_loop(0, doubles, fwd_double, (old, cur, new, fwd_place(me * 0 + singles + 2)))
+    for act in ag_events(plan.fwd_waits[singles + doubles + 1]):
         act()
     if plan.fwd_mate == turns - 1:
         mask_scores(1, 0)

time: 121 us -> 122 us (level)
  no operation moved by 1% of the time
where the time goes in v10:
time: 122 us
  Pallas kernels  121 us (99%)
    pallas_call x1, Pallas kernels, local(): pl.pallas_call(functools.partial(kernel, plan), out_shape=(big, big, smal...  119 us

profile of v10, /device:TPU:0, one launch (start us, length us, event | category | flops | bytes accessed | tf_op | source)
XLA Modules:
  0.0 121.7 jit_solution(2491705863323384521)
XLA Ops:
  0.6 119.0 %shard_map.75 = (bf16[5,256,128]{2,1,0:T(8,128)(2,1)}, bf16[5,256,128]{2,1,0:T(8,128)(2,1)}, bf16[256,128]{1,0:T(8,128)(2,1)}, bf16[256,128]{1,0:T(8,128)(2,1)}) custom-call(bf16[5,256,128]{2,1,0:T(8,128)(2,1)} %bitcast.16, bf16[256,128]{1,0:T(8,128)(2,1)} %bitcast.20, bf16[256,128]{1,0:T(8,128)(2,1)} %bitcast.21, bf16[5,256,128]{2,1,0:T(8,128)(2,1)} %bitcast.17), custom_call_target="tpu_custom_call" | custom-call | flops 18790481920 | bytes 4194304 | tf_op jit(solution)/shard_map/pallas_call | solution.py:673
  119.6 1.9 %shard_map.76 = (bf16[5,256,128]{2,1,0:T(8,128)(2,1)}, bf16[5,256,128]{2,1,0:T(8,128)(2,1)}, bf16[256,128]{1,0:T(8,128)(2,1)}, bf16[256,128]{1,0:T(8,128)(2,1)}) custom-call(bf16[5,256,128]{2,1,0:T(8,128)(2,1)} %get-tuple-element.12.refs_0_, bf16[5,256,128]{2,1,0:T(8,128)(2,1)} %get-tuple-element.13.refs_1_, bf16[256,128]{1,0:T(8,128)(2,1)} %get-tuple-element.14.refs_2_, ...), custom_call_target="tpu_custom_call" | custom-call | flops 1048576 | bytes 2097152 | tf_op jit(solution)/shard_map/pallas_call | solution.py:691

commit v11 on v9

--- a/solution.py
+++ b/solution.py
@@ -20,9 +20,9 @@
 
 KEY_TREE = "011222133332330444044204331303450512252553132154554251534405024"
 VALUE_TREE = "011202133303032404124114441201150505210501022525540551434312353"
-DK_TREE = "011202230302020401042203040443255115012501525315014524043545435"
-DV_TREE = "011221233332313444144214343331155555212333535104510402554435224"
-BWD_ORDER = "vtfrsnmud7qjklp3cobe9ai6h45g128"
+DK_TREE = "011202030312311404440413410322055502551351320125544451033135454"
+DV_TREE = "011222133313020444022124310233455512520331055524450502154433451"
+BWD_ORDER = "vtrujnfsd7meockplbq36i95ha8g124"
 
 
 def popcount(value):
@@ -101,7 +101,7 @@
         self.fwd_pairs = order
         self.fwd_mate = max(i for i, pair in enumerate(order) if pair == 0)
 
-    def backward(self, unit_us=2.9, hop_us=2.1, turn_us=1.6, add_us=0.025):
+    def backward(self, unit_us=2.84, hop_us=2.75, turn_us=1.62, add_us=0.025):
         if self.dims == 6:
             order = [int(c, 32) for c in BWD_ORDER]
         else:

time: 121 us -> 121 us (level)
  no operation moved by 1% of the time
where the time goes in v11:
time: 121 us
  Pallas kernels  120 us (99%)
    pallas_call x1, Pallas kernels, local(): pl.pallas_call(functools.partial(kernel, plan), out_shape=(big, big, smal...  118 us

profile of v11, /device:TPU:0, one launch (start us, length us, event | category | flops | bytes accessed | tf_op | source)
XLA Modules:
  0.0 121.1 jit_solution(3777004391156369922)
XLA Ops:
  0.6 118.3 %shard_map.75 = (bf16[5,256,128]{2,1,0:T(8,128)(2,1)}, bf16[5,256,128]{2,1,0:T(8,128)(2,1)}, bf16[256,128]{1,0:T(8,128)(2,1)}, bf16[256,128]{1,0:T(8,128)(2,1)}) custom-call(bf16[5,256,128]{2,1,0:T(8,128)(2,1)} %bitcast.16, bf16[256,128]{1,0:T(8,128)(2,1)} %bitcast.20, bf16[256,128]{1,0:T(8,128)(2,1)} %bitcast.21, bf16[5,256,128]{2,1,0:T(8,128)(2,1)} %bitcast.17), custom_call_target="tpu_custom_call" | custom-call | flops 18790481920 | bytes 4194304 | tf_op jit(solution)/shard_map/pallas_call | solution.py:651
  119.0 1.9 %shard_map.76 = (bf16[5,256,128]{2,1,0:T(8,128)(2,1)}, bf16[5,256,128]{2,1,0:T(8,128)(2,1)}, bf16[256,128]{1,0:T(8,128)(2,1)}, bf16[256,128]{1,0:T(8,128)(2,1)}) custom-call(bf16[5,256,128]{2,1,0:T(8,128)(2,1)} %get-tuple-element.12.refs_0_, bf16[5,256,128]{2,1,0:T(8,128)(2,1)} %get-tuple-element.13.refs_1_, bf16[256,128]{1,0:T(8,128)(2,1)} %get-tuple-element.14.refs_2_, ...), custom_call_target="tpu_custom_call" | custom-call | flops 1048576 | bytes 2097152 | tf_op jit(solution)/shard_map/pallas_call | solution.py:669

commit v12 on v11

--- a/solution.py
+++ b/solution.py
@@ -20,9 +20,9 @@
 
 KEY_TREE = "011222133332330444044204331303450512252553132154554251534405024"
 VALUE_TREE = "011202133303032404124114441201150505210501022525540551434312353"
-DK_TREE = "011202030312311404440413410322055502551351320125544451033135454"
-DV_TREE = "011222133313020444022124310233455512520331055524450502154433451"
-BWD_ORDER = "vtrujnfsd7meockplbq36i95ha8g124"
+DK_TREE = "010221133103211404040144031203455152212301535105514225055432452"
+DV_TREE = "011221033332230444442413330244055105022533550214551404233315450"
+BWD_ORDER = "vtnudrlfjemp5kbq9s7ioah63c482g1"
 
 
 def popcount(value):
@@ -101,7 +101,7 @@
         self.fwd_pairs = order
         self.fwd_mate = max(i for i, pair in enumerate(order) if pair == 0)
 
-    def backward(self, unit_us=2.84, hop_us=2.75, turn_us=1.62, add_us=0.025):
+    def backward(self, unit_us=2.95, hop_us=2.5, turn_us=1.58, add_us=0.025):
         if self.dims == 6:
             order = [int(c, 32) for c in BWD_ORDER]
         else:

time: 121 us -> 121 us (level)
  no operation moved by 1% of the time
where the time goes in v12:
time: 121 us
  Pallas kernels  120 us (99%)
    pallas_call x1, Pallas kernels, local(): pl.pallas_call(functools.partial(kernel, plan), out_shape=(big, big, smal...  118 us

profile of v12, /device:TPU:0, one launch (start us, length us, event | category | flops | bytes accessed | tf_op | source)
XLA Modules:
  0.0 120.7 jit_solution(14828470601627899546)
XLA Ops:
  0.6 118.0 %shard_map.75 = (bf16[5,256,128]{2,1,0:T(8,128)(2,1)}, bf16[5,256,128]{2,1,0:T(8,128)(2,1)}, bf16[256,128]{1,0:T(8,128)(2,1)}, bf16[256,128]{1,0:T(8,128)(2,1)}) custom-call(bf16[5,256,128]{2,1,0:T(8,128)(2,1)} %bitcast.16, bf16[256,128]{1,0:T(8,128)(2,1)} %bitcast.20, bf16[256,128]{1,0:T(8,128)(2,1)} %bitcast.21, bf16[5,256,128]{2,1,0:T(8,128)(2,1)} %bitcast.17), custom_call_target="tpu_custom_call" | custom-call | flops 18790481920 | bytes 4194304 | tf_op jit(solution)/shard_map/pallas_call | solution.py:651
  118.6 1.9 %shard_map.76 = (bf16[5,256,128]{2,1,0:T(8,128)(2,1)}, bf16[5,256,128]{2,1,0:T(8,128)(2,1)}, bf16[256,128]{1,0:T(8,128)(2,1)}, bf16[256,128]{1,0:T(8,128)(2,1)}) custom-call(bf16[5,256,128]{2,1,0:T(8,128)(2,1)} %get-tuple-element.12.refs_0_, bf16[5,256,128]{2,1,0:T(8,128)(2,1)} %get-tuple-element.13.refs_1_, bf16[256,128]{1,0:T(8,128)(2,1)} %get-tuple-element.14.refs_2_, ...), custom_call_target="tpu_custom_call" | custom-call | flops 1048576 | bytes 2097152 | tf_op jit(solution)/shard_map/pallas_call | solution.py:669

commit v13 on v9

--- a/solution.py
+++ b/solution.py
@@ -617,16 +617,14 @@
 
 
 def relay(*refs):
-    count = (len(refs) - 1) // 3
-    src, dst, buf, sem = refs[:count], refs[count:2 * count], refs[2 * count:3 * count], refs[3 * count]
-    into = [pltpu.make_async_copy(a, b, sem.at[i]) for i, (a, b) in enumerate(zip(src, buf))]
-    out = [pltpu.make_async_copy(b, c, sem.at[count + i]) for i, (b, c) in enumerate(zip(buf, dst))]
-    for copy in into:
+    count = (len(refs) - 1) // 2
+    pairs = []
+    for src, dst in zip(refs[:count], refs[count:2 * count]):
+        pairs += [(src.at[h], dst.at[h]) for h in range(HEADS)] if len(src.shape) > 2 else [(src, dst)]
+    copies = [pltpu.make_async_copy(src, dst, refs[-1].at[i]) for i, (src, dst) in enumerate(pairs)]
+    for copy in copies:
         copy.start()
-    for i in range(count):
-        into[i].wait()
-        out[i].start()
-    for copy in out:
+    for copy in copies:
         copy.wait()
 
 
@@ -671,7 +669,7 @@
             out_shape=(big, big, small, small),
             in_specs=[anywhere] * 4,
             out_specs=(anywhere,) * 4,
-            scratch_shapes=[vm(x.shape, bf16) for x in (big, big, small, small)] + [sem((8,))],
+            scratch_shapes=[sem((2 * HEADS + 2,))],
             cost_estimate=pl.CostEstimate(flops=1 << 20, bytes_accessed=2 << 20, transcendentals=0),
         )(*results)
         return (o.transpose(1, 0, 2)[None], dq.transpose(1, 0, 2)[None], dk[None, :, None], dv[None, :, None])

time: 121 us -> 144 us (1.19)
  Pallas kernels: 120 us -> 143 us
    pallas_call x1, Pallas kernels: 1.91 us -> 25 us  [local(): pl.pallas_call(relay, out_shape=(big, big, small, small), in_specs=[anywh...]
where the time goes in v13:
time: 144 us
  Pallas kernels  143 us (99%)
    pallas_call x1, Pallas kernels, local(): pl.pallas_call(functools.partial(kernel, plan), out_shape=(big, big, smal...  118 us
    pallas_call x1, Pallas kernels, local(): pl.pallas_call(relay, out_shape=(big, big, small, small), in_specs=[anywh...  25 us

profile of v13, /device:TPU:0, one launch (start us, length us, event | category | flops | bytes accessed | tf_op | source)
XLA Modules:
  0.0 143.8 jit_solution(10929701142616601934)
XLA Ops:
  0.6 118.0 %shard_map.75 = (bf16[5,256,128]{2,1,0:T(8,128)(2,1)}, bf16[5,256,128]{2,1,0:T(8,128)(2,1)}, bf16[256,128]{1,0:T(8,128)(2,1)}, bf16[256,128]{1,0:T(8,128)(2,1)}) custom-call(bf16[5,256,128]{2,1,0:T(8,128)(2,1)} %bitcast.16, bf16[256,128]{1,0:T(8,128)(2,1)} %bitcast.20, bf16[256,128]{1,0:T(8,128)(2,1)} %bitcast.21, bf16[5,256,128]{2,1,0:T(8,128)(2,1)} %bitcast.17), custom_call_target="tpu_custom_call" | custom-call | flops 18790481920 | bytes 4194304 | tf_op jit(solution)/shard_map/pallas_call | solution.py:649
  118.6 25.0 %shard_map.76 = (bf16[5,256,128]{2,1,0:T(8,128)(2,1)}, bf16[5,256,128]{2,1,0:T(8,128)(2,1)}, bf16[256,128]{1,0:T(8,128)(2,1)}, bf16[256,128]{1,0:T(8,128)(2,1)}) custom-call(bf16[5,256,128]{2,1,0:T(8,128)(2,1)} %get-tuple-element.12.refs_0_, bf16[5,256,128]{2,1,0:T(8,128)(2,1)} %get-tuple-element.13.refs_1_, bf16[256,128]{1,0:T(8,128)(2,1)} %get-tuple-element.14.refs_2_, ...), custom_call_target="tpu_custom_call" | custom-call | flops 1048576 | bytes 2097152 | tf_op jit(solution)/shard_map/pallas_call | solution.py:667
